TPU v7x, 512 devices: a whole 4x4x16 slice. The times are simulated.
512 devices in a mesh: gx: 8 (over y_hi, x), gy: 4 (over y_lo, core), gz: 16 (over z).
Axes of the slice: x: 4, y: 4 (y_hi: 2, y_lo: 2; y = y_hi * 2 + y_lo), z: 16, core: 2. Of those that a mesh axis runs over, the one named last changes fastest.
Arguments:
- fields: float32 [6, 128, 64, 2048], P(None, 'gx', 'gy', 'gz'), may hold values from -6 to 6
- permittivity: float32 [128, 64, 2048], P('gx', 'gy', 'gz'), may hold values from 1 to 4
- donor_owner: int32 [65536, 1], P(('gx', 'gy', 'gz')), may hold values from 0 to 63; in each aligned block of 128 rows (0 to 127, 128 to 255, ...) at most 4 rows name the same one
- donor_base: int32 [65536, 3], P(('gx', 'gy', 'gz')), may hold values from 0 to 127, as said below
- donor_weights: float32 [65536, 15], P(('gx', 'gy', 'gz')), may hold values from -3 to 3
Outputs:
- new_fields: float32 [6, 128, 64, 2048], P(None, 'gx', 'gy', 'gz')
- receptor_values: float32 [6, 65536], P(None, ('gx', 'gy', 'gz'))
Inputs may be any that keep to these rules, and one draw needn't show every extreme that they name: `donor_owner`: within the 128 rows of one device no owner index is named by more than 4 rows, and one is named by exactly 4. `donor_base`: column 0 lies in 0 to 15, column 1 in 0 to 15, column 2 in 0 to 127.
All inputs are finite; a program needn't handle non-finite values.
Results may differ from a plain program's by a relative error of at most 0.00002.
Values sent between devices are 32-bit elements; how exact they have to be, the bound alone decides.
No kernel may reach another device: no remote copies, remote signals or barrier semaphores. Data moves between devices by JAX's collectives and lax.ppermute only.
A program may use at most 192 MiB of HBM per device.

v0:
```python
import jax
import jax.numpy as jnp
from jax import lax
from jax.sharding import PartitionSpec as P

step_size = 0.25


def extended(array, sides, width):
    edges = {}
    for axis, dim in sides:
        size, length = (lax.axis_size(axis), array.shape[dim])
        up = [(i, (i + 1) % size) for i in range(size - 1)]
        last = lax.slice_in_dim(array, length - width, length, axis=dim)
        initial = lax.slice_in_dim(array, 0, width, axis=dim)
        edges[dim] = (
            lax.ppermute(last, axis, up),
            lax.ppermute(initial, axis, [(b, a) for a, b in up]),
        )
    done = []
    for _, dim in sides:
        low, high = edges[dim]
        around = [(width, width) if d in done else (0, 0) for d in range(array.ndim)]
        array = jnp.concatenate([jnp.pad(low, around), array, jnp.pad(high, around)], axis=dim)
        done.append(dim)
    return array


def padded_2(cells, sides, width):
    for axis, dim in sides:
        count = lax.axis_size(axis)
        ends = count - 1
        head = lax.slice_in_dim(cells, 0, width, axis=dim)
        tail = lax.slice_in_dim(cells, cells.shape[dim] - width, cells.shape[dim], axis=dim)
        cells = jnp.concatenate(
            [
                lax.ppermute(tail, axis, [(i, (i + 1) % count) for i in range(ends)]),
                cells,
                lax.ppermute(head, axis, [((i + 1) % count, i) for i in range(ends)]),
            ],
            axis=dim,
        )
    return cells


def shifted(field, axis_index, offset):
    window = [slice(2, -2), slice(2, -2), slice(2, -2)]
    length = field.shape[axis_index] - 4
    window[axis_index] = slice(2 + offset, 2 + offset + length)
    return field[tuple(window)]


def derivative(field, axis_index):
    outer = shifted(field, axis_index, -2) - shifted(field, axis_index, 2)
    inner = shifted(field, axis_index, 1) - shifted(field, axis_index, -1)
    return (outer + 8.0 * inner) / 12.0


def curl_rate(padded, coefficient):
    rate_ex = (derivative(padded[5], 1) - derivative(padded[4], 2)) / coefficient
    rate_ey = (derivative(padded[3], 2) - derivative(padded[5], 0)) / coefficient
    rate_ez = (derivative(padded[4], 0) - derivative(padded[3], 1)) / coefficient
    rate_hx = derivative(padded[1], 2) - derivative(padded[2], 1)
    rate_hy = derivative(padded[2], 0) - derivative(padded[0], 2)
    rate_hz = derivative(padded[0], 1) - derivative(padded[1], 0)
    return jnp.stack([rate_ex, rate_ey, rate_ez, rate_hx, rate_hy, rate_hz])


def contract(donor_tiles, weights):
    weight_x = weights[0:5]
    weight_y = weights[5:10]
    weight_z = weights[10:15]
    along_z = jnp.sum(donor_tiles * weight_z[None, None, None, :, :], axis=3)
    along_y = jnp.sum(along_z * weight_y[None, None, :, :], axis=2)
    return jnp.sum(along_y * weight_x[None, :, :], axis=1)


def gather_tiles(donor_grid, corner_rows):
    components, extent_x, extent_y, extent_z = donor_grid.shape
    flat_grid = donor_grid.reshape(components, extent_x * extent_y * extent_z)
    stencil = jnp.arange(5, dtype=jnp.int32)
    offsets = (
        stencil[:, None, None] * (extent_y * extent_z)
        + stencil[None, :, None] * extent_z
        + stencil[None, None, :]
    ).reshape(125)
    starts = corner_rows[0] * (extent_y * extent_z) + corner_rows[1] * extent_z + corner_rows[2]
    picked = jnp.take(flat_grid, offsets[:, None] + starts[None, :], axis=1)
    return picked.reshape(components, 5, 5, 5, corner_rows.shape[1])


def local(fields, permittivity, donor_owner, donor_base, donor_weights):
    accumulated = fields
    taylor_term = fields
    for power in range(1, 5):
        padded = extended(taylor_term, (("gx", 1), ("gy", 2), ("gz", 3)), 2)
        taylor_term = step_size / power * curl_rate(padded, permittivity)
        accumulated = accumulated + taylor_term
    donor_grid = padded_2(accumulated, (("gx", 1), ("gy", 2), ("gz", 3)), 2)
    group_size = lax.axis_size("gy") * lax.axis_size("gz")
    row_count = donor_owner.shape[0]
    capacity = 2 * row_count // group_size
    owner_id = donor_owner[:, 0]
    owner_hits = (owner_id[:, None] == jnp.arange(group_size, dtype=jnp.int32)[None, :]).astype(
        jnp.int32
    )
    earlier = jnp.cumsum(owner_hits, axis=0) - owner_hits
    slot_index = jnp.sum(earlier * owner_hits, axis=1)
    flat_index = owner_id * capacity + slot_index
    corner_send = (
        jnp.zeros((3, group_size * capacity), jnp.int32).at[:, flat_index].set(donor_base.T)
    )
    corner_send = corner_send.reshape(3, group_size, capacity)
    weight_send = (
        jnp.zeros((15, group_size * capacity), jnp.float32).at[:, flat_index].set(donor_weights.T)
    )
    weight_send = weight_send.reshape(15, group_size, capacity)
    donor_corners = lax.all_to_all(
        corner_send, ("gy", "gz"), split_axis=1, concat_axis=1, tiled=True
    )
    piece_weights = lax.all_to_all(
        weight_send, ("gy", "gz"), split_axis=1, concat_axis=1, tiled=True
    )
    slot_count = donor_corners.shape[2]
    donor_tiles = gather_tiles(donor_grid, donor_corners.reshape(3, -1))
    values = contract(donor_tiles, piece_weights.reshape(15, -1)).reshape(6, group_size, slot_count)
    answers = lax.all_to_all(values, ("gy", "gz"), split_axis=1, concat_axis=1, tiled=True)
    receptor_values = answers.reshape(6, -1)[:, flat_index]
    return (accumulated, receptor_values)


def solution(mesh):
    placed = (
        P(None, "gx", "gy", "gz"),
        P("gx", "gy", "gz"),
        P(("gx", "gy", "gz"), None),
        P(("gx", "gy", "gz"), None),
        P(("gx", "gy", "gz"), None),
    )
    return jax.shard_map(
        local,
        mesh=mesh,
        in_specs=placed,
        out_specs=(P(None, "gx", "gy", "gz"), P(None, ("gx", "gy", "gz"))),
        check_vma=False,
    )
```

profile of v0, /device:TPU:7, one launch (start us, length us, event | category | flops | bytes accessed | tf_op | source)
XLA Modules:
  0.0 377.1 jit_solution(17785123580572100083)
XLA Ops:
  0.7 1.7 fusion.259
  3.0 3.6 collective-permute-start
  8.6 4.0 %collective-permute-start.1 = (f32[6,16,2,128]{3,1,2,0:T(8,128)S(1)}, f32[6,16,2,128]{3,1,2,0:T(8,128)S(1)}, u32[]{:S(2)}, u32[]{:S(2)}) collective-permute-start(f32[6,16,2,128]{3,1,2,0:T(8,128)S(1)} %copy.154), channel_id=1, source_target_pairs={{0,16},{16,32},{32,48},{1,17},{17,33},{33,49},{2,18},{18,34},{34,5... | collective-permute-start | bytes 294920 | tf_op jit(solution)/shard_map/ppermute | solution.py:17
  12.7 1.9 collective-permute-start.4
  14.6 4.4 %collective-permute-start.2 = (f32[6,2,16,128]{3,2,1,0:T(8,128)S(1)}, f32[6,2,16,128]{3,2,1,0:T(8,128)S(1)}, u32[]{:S(2)}, u32[]{:S(2)}) collective-permute-start(f32[6,2,16,128]{3,2,1,0:T(8,128)S(1)} %get-tuple-element.60), channel_id=1, source_target_pairs={{0,64},{64,128},{128,192},{192,256},{256,320},{320,384},{384,448},... | collective-permute-start | bytes 294920 | tf_op jit(solution)/shard_map/ppermute | solution.py:17
  21.7 18.8 %all-to-all-start = ((s32[3,64,4]{2,0,1:T(4,128)}), s32[3,64,4]{2,0,1:T(4,128)S(1)}, u32[]{:S(2)}, u32[]{:S(2)}) async-start(s32[3,64,4]{2,0,1:T(4,128)} %copy.142), calls=%async_computation | async-start | bytes 262144 | tf_op jit(solution)/shard_map/all_to_all | solution.py:118
  40.6 1.9 collective-permute-start.3
  44.0 6.0 %collective-permute-done.3 = f32[6,2,16,128]{3,2,1,0:T(8,128)S(1)} collective-permute-done((f32[6,2,16,128]{3,2,1,0:T(8,128)S(1)}, f32[6,2,16,128]{3,2,1,0:T(8,128)S(1)}, u32[]{:S(2)}, u32[]{:S(2)}) %collective-permute-start.3) | collective-permute-done | bytes 98336 | tf_op jit(solution)/shard_map/ppermute | solution.py:18
  50.0 2.1 select_maximum_fusion.9
  56.9 2.4 copy.117
  59.3 3.9 %collective-permute-start.6 = (f32[6,16,16,2]{2,1,3,0:T(8,128)}, f32[6,16,16,2]{2,1,3,0:T(8,128)}, u32[]{:S(2)}, u32[]{:S(2)}) collective-permute-start(f32[6,16,16,2]{2,1,3,0:T(8,128)} %copy.117), channel_id=1, source_target_pairs={{0,1},{1,2},{2,3},{3,4},{4,5},{5,6},{6,7},{7,8},{8,9},{9,10},{10,1... | collective-permute-start | bytes 36872 | tf_op jit(solution)/shard_map/ppermute | solution.py:17
  66.5 1.5 copy.118
  68.0 4.9 %collective-permute-start.7 = (f32[6,16,2,128]{3,1,2,0:T(8,128)}, f32[6,16,2,128]{3,1,2,0:T(8,128)}, u32[]{:S(2)}, u32[]{:S(2)}) collective-permute-start(f32[6,16,2,128]{3,1,2,0:T(8,128)} %copy.118), channel_id=1, source_target_pairs={{0,16},{16,32},{32,48},{1,17},{17,33},{33,49},{2,18},{18,34},{34,5... | collective-permute-start | bytes 294920 | tf_op jit(solution)/shard_map/ppermute | solution.py:17
  73.5 1.9 collective-permute-start.10
  75.4 1.9 collective-permute-start.8
  77.4 3.4 collective-permute-start.9
  81.4 1.5 scatter_custom_fusion.1
  82.9 1.5 copy.163
  84.4 2.4 copy.166
  88.8 3.1 select_maximum_fusion.6
  96.4 2.4 copy.125
  98.8 4.9 %collective-permute-start.12 = (f32[6,16,16,2]{2,1,3,0:T(8,128)}, f32[6,16,16,2]{2,1,3,0:T(8,128)}, u32[]{:S(2)}, u32[]{:S(2)}) collective-permute-start(f32[6,16,16,2]{2,1,3,0:T(8,128)} %copy.125), channel_id=1, source_target_pairs={{0,1},{1,2},{2,3},{3,4},{4,5},{5,6},{6,7},{7,8},{8,9},{9,10},{10,1... | collective-permute-start | bytes 36872 | tf_op jit(solution)/shard_map/ppermute | solution.py:17
  104.3 2.4 copy.130
  108.0 1.5 copy.126
  109.6 4.5 %collective-permute-start.13 = (f32[6,16,2,128]{3,1,2,0:T(8,128)}, f32[6,16,2,128]{3,1,2,0:T(8,128)}, u32[]{:S(2)}, u32[]{:S(2)}) collective-permute-start(f32[6,16,2,128]{3,1,2,0:T(8,128)} %copy.126), channel_id=1, source_target_pairs={{0,16},{16,32},{32,48},{1,17},{17,33},{33,49},{2,18},{18,34},{34,5... | collective-permute-start | bytes 294920 | tf_op jit(solution)/shard_map/ppermute | solution.py:17
  114.7 1.9 collective-permute-start.16
  116.6 5.9 %collective-permute-start.14 = (f32[6,2,16,128]{3,2,1,0:T(8,128)}, f32[6,2,16,128]{3,2,1,0:T(8,128)}, u32[]{:S(2)}, u32[]{:S(2)}) collective-permute-start(f32[6,2,16,128]{3,2,1,0:T(8,128)} %get-tuple-element.48), channel_id=1, source_target_pairs={{0,64},{64,128},{128,192},{192,256},{256,320},{320,384},{384,448},... | collective-permute-start | bytes 294920 | tf_op jit(solution)/shard_map/ppermute | solution.py:17
  122.5 15.5 %all-to-all-start.1 = ((f32[15,64,4]{0,2,1:T(4,128)}), f32[15,64,4]{0,2,1:T(4,128)S(1)}, u32[]{:S(2)}, u32[]{:S(2)}) async-start(f32[15,64,4]{0,2,1:T(4,128)} %bitcast.55), calls=%async_computation.1 | async-start | bytes 262144 | tf_op jit(solution)/shard_map/all_to_all | solution.py:121
  138.0 1.9 collective-permute-start.15
  141.5 2.4 copy.167
  144.0 2.4 copy.170
  148.3 3.2 select_maximum_fusion.3
  156.9 2.4 copy.133
  159.3 3.9 %collective-permute-start.18 = (f32[6,16,16,2]{2,1,3,0:T(8,128)}, f32[6,16,16,2]{2,1,3,0:T(8,128)}, u32[]{:S(2)}, u32[]{:S(2)}) collective-permute-start(f32[6,16,16,2]{2,1,3,0:T(8,128)} %copy.133), channel_id=1, source_target_pairs={{0,1},{1,2},{2,3},{3,4},{4,5},{5,6},{6,7},{7,8},{8,9},{9,10},{10,1... | collective-permute-start | bytes 36872 | tf_op jit(solution)/shard_map/ppermute | solution.py:17
  163.9 2.4 copy.138
  167.5 1.5 copy.134
  169.1 4.2 %collective-permute-start.19 = (f32[6,16,2,128]{3,1,2,0:T(8,128)}, f32[6,16,2,128]{3,1,2,0:T(8,128)}, u32[]{:S(2)}, u32[]{:S(2)}) collective-permute-start(f32[6,16,2,128]{3,1,2,0:T(8,128)} %copy.134), channel_id=1, source_target_pairs={{0,16},{16,32},{32,48},{1,17},{17,33},{33,49},{2,18},{18,34},{34,5... | collective-permute-start | bytes 294920 | tf_op jit(solution)/shard_map/ppermute | solution.py:17
  173.9 1.9 collective-permute-start.22
  175.8 7.4 %collective-permute-start.20 = (f32[6,2,16,128]{3,2,1,0:T(8,128)}, f32[6,2,16,128]{3,2,1,0:T(8,128)}, u32[]{:S(2)}, u32[]{:S(2)}) collective-permute-start(f32[6,2,16,128]{3,2,1,0:T(8,128)} %get-tuple-element.42), channel_id=1, source_target_pairs={{0,64},{64,128},{128,192},{192,256},{256,320},{320,384},{384,448},... | collective-permute-start | bytes 294920 | tf_op jit(solution)/shard_map/ppermute | solution.py:17
  183.3 2.1 collective-permute-start.21
  187.1 2.4 copy.171
  189.5 2.4 copy.174
  193.8 3.2 select_maximum_fusion
  199.7 7.0 %collective-permute-start.24 = (f32[6,2,16,128]{3,2,1,0:T(8,128)S(1)}, f32[6,2,16,128]{3,2,1,0:T(8,128)S(1)}, u32[]{:S(2)}, u32[]{:S(2)}) collective-permute-start(f32[6,2,16,128]{3,2,1,0:T(8,128)S(1)} %get-tuple-element.40), channel_id=1, source_target_pairs={{0,64},{64,128},{128,192},{192,256},{256,320},{320,384},{384,448},... | collective-permute-start | bytes 294920 | tf_op jit(solution)/shard_map/ppermute | solution.py:37
  206.6 1.9 collective-permute-start.25
  208.6 7.1 %collective-permute-done.25 = f32[6,2,16,128]{3,2,1,0:T(8,128)S(1)} collective-permute-done((f32[6,2,16,128]{3,2,1,0:T(8,128)S(1)}, f32[6,2,16,128]{3,2,1,0:T(8,128)S(1)}, u32[]{:S(2)}, u32[]{:S(2)}) %collective-permute-start.25) | collective-permute-done | bytes 98336 | tf_op jit(solution)/shard_map/ppermute | solution.py:39
  215.8 4.9 %collective-permute-start.26 = (f32[6,20,2,128]{3,2,1,0:T(2,128)S(1)}, f32[6,20,2,128]{3,2,1,0:T(2,128)S(1)}, u32[]{:S(2)}, u32[]{:S(2)}) collective-permute-start(f32[6,20,2,128]{3,2,1,0:T(2,128)S(1)} %get-tuple-element.38), channel_id=1, source_target_pairs={{0,16},{16,32},{32,48},{1,17},{17,33},{33,49},{2,18},{18,34},{34,5... | collective-permute-start | bytes 368648 | tf_op jit(solution)/shard_map/ppermute | solution.py:37
  220.7 1.9 collective-permute-start.27
  222.8 4.1 %collective-permute-done.27 = f32[6,20,2,128]{3,2,1,0:T(2,128)S(1)} collective-permute-done((f32[6,20,2,128]{3,2,1,0:T(2,128)S(1)}, f32[6,20,2,128]{3,2,1,0:T(2,128)S(1)}, u32[]{:S(2)}, u32[]{:S(2)}) %collective-permute-start.27) | collective-permute-done | bytes 122912 | tf_op jit(solution)/shard_map/ppermute | solution.py:39
  227.2 1.6 fusion.247
  228.8 3.0 copy.157
  231.8 4.9 %collective-permute-start.28 = (f32[6,20,20,2]{2,1,3,0:T(8,128)}, f32[6,20,20,2]{2,1,3,0:T(8,128)}, u32[]{:S(2)}, u32[]{:S(2)}) collective-permute-start(f32[6,20,20,2]{2,1,3,0:T(8,128)} %copy.157), channel_id=1, source_target_pairs={{0,1},{1,2},{2,3},{3,4},{4,5},{5,6},{6,7},{7,8},{8,9},{9,10},{10,1... | collective-permute-start | bytes 57608 | tf_op jit(solution)/shard_map/ppermute | solution.py:37
  236.7 1.6 copy.158
  238.3 1.5 collective-permute-start.29
  240.3 1.8 copy.145
  242.1 2.4 collective-permute-done.29
  244.5 2.9 copy.146
  247.4 4.7 %pad_maximum_fusion = f32[6,20,20,132]{3,2,1,0:T(8,128)} fusion(f32[6,20,20,2]{3,2,1,0:T(8,128)} %copy.146, f32[6,20,2,128]{3,2,1,0:T(2,128)S(1)} %collective-permute-done.27, f32[6,2,16,128]{3,2,1,0:T(8,128)S(1)} %collective-permute-done.25, f32[6,16,16,128]{3,2,1,0:T(8,128)S(1)} %multiply_add_fusion, f32[6,2,16,128]{3,2,1,0:T(8,128)S(1)} %collective-permute-done.24, ...), kind=kLoop, calls=%fused_computation.32 | loop fusion | flops 1900800 | bytes 2534400 | tf_op jit(solution)/shard_map/concatenate | solution.py:35
  252.1 3.3 reshape.199
  255.4 14.0 %copy.147 = f32[6,52800]{0,1:T(8,128)} copy(f32[6,52800]{1,0:T(8,128)S(1)} %reshape.199) | data formatting | bytes 2534400 | tf_op jit(solution)/shard_map/reshape | solution.py:80
  269.4 67.8 %gather_fusion = f32[32000,6]{1,0:T(8,128)} fusion(f32[6,52800]{0,1:T(8,128)} %copy.147, s32[32768]{0:T(1024)S(1)} %pad_clamp_fusion), kind=kCustom, calls=%fused_computation | custom fusion | bytes 1664000 | tf_op jit(solution)/shard_map/jit(_take)/gather | solution.py:88
  337.2 7.9 %multiply_reduce_fusion = f32[6,5,5,256]{0,3,2,1:T(8,128)S(1)} fusion(f32[6,5,5,5,256]{0,4,3,2,1:T(8,128)} %bitcast.166, f32[5,256]{1,0:T(8,128)S(1)} %copy.149, pred[5,5,5,256]{3,2,1,0:T(8,128)(4,1)S(1)} %fusion.10), kind=kLoop, calls=%fused_computation.4 | loop fusion | flops 537600 | bytes 958720 | tf_op jit(solution)/shard_map/reduce_sum | solution.py:73
  346.4 13.4 %all-to-all-start.2 = ((f32[6,64,4]{0,2,1:T(4,128)}), f32[6,64,4]{0,2,1:T(4,128)S(1)}, u32[]{:S(2)}, u32[]{:S(2)}) async-start(f32[6,64,4]{0,2,1:T(4,128)} %bitcast.59), calls=%async_computation.2 | async-start | bytes 262144 | tf_op jit(solution)/shard_map/all_to_all | solution.py:127
  359.9 15.9 %all-to-all-done.2 = f32[6,64,4]{0,2,1:T(4,128)S(1)} async-done(((f32[6,64,4]{0,2,1:T(4,128)}), f32[6,64,4]{0,2,1:T(4,128)S(1)}, u32[]{:S(2)}, u32[]{:S(2)}) %all-to-all-start.2) | async-done | bytes 6176 | tf_op jit(solution)/shard_map/all_to_all | solution.py:127
  (143 shorter events, 46.0 us)
Async XLA Ops:
  0.6 7.9 %copy-start.1 = (f32[6,16,16,128]{3,2,1,0:T(8,128)S(1)}, f32[6,16,16,128]{3,2,1,0:T(8,128)}, u32[]{:S(2)}) copy-start(f32[6,16,16,128]{3,2,1,0:T(8,128)} %param.5) | copy-start | bytes 2359300
  0.6 18.4 %copy-start.8 = (s32[128,1]{0,1:T(1,128)S(1)}, s32[128,1]{0,1:T(1,128)}, u32[]{:S(2)}) copy-start(s32[128,1]{0,1:T(1,128)} %param.7) | copy-start | bytes 1540
  0.6 18.9 %copy-start.9 = (s32[128,3]{0,1:T(4,128)S(1)}, s32[128,3]{0,1:T(4,128)}, u32[]{:S(2)}) copy-start(s32[128,3]{0,1:T(4,128)} %param.8) | copy-start | bytes 4612
  3.0 37.5 %collective-permute-start = (f32[6,16,16,2]{2,1,3,0:T(8,128)S(1)}, f32[6,16,16,2]{2,1,3,0:T(8,128)S(1)}, u32[]{:S(2)}, u32[]{:S(2)}) collective-permute-start(f32[6,16,16,2]{2,1,3,0:T(8,128)S(1)} %copy.153), channel_id=1, source_target_pairs={{0,1},{1,2},{2,3},{3,4},{4,5},{5,6},{6,7},{7,8},{8,9},{9,10},{10,1... | collective-permute-start | bytes 36872 | tf_op jit(solution)/shard_map/ppermute | solution.py:17
  7.2 36.0 %collective-permute-start.5 = (f32[6,16,16,2]{2,1,3,0:T(8,128)S(1)}, f32[6,16,16,2]{2,1,3,0:T(8,128)S(1)}, u32[]{:S(2)}, u32[]{:S(2)}) collective-permute-start(f32[6,16,16,2]{2,1,3,0:T(8,128)S(1)} %copy.156), channel_id=1, source_target_pairs={{1,0},{2,1},{3,2},{4,3},{5,4},{6,5},{7,6},{8,7},{9,8},{10,9},{11,1... | collective-permute-start | bytes 36872 | tf_op jit(solution)/shard_map/ppermute | solution.py:18
  8.6 35.2 %collective-permute-start.1 = (f32[6,16,2,128]{3,1,2,0:T(8,128)S(1)}, f32[6,16,2,128]{3,1,2,0:T(8,128)S(1)}, u32[]{:S(2)}, u32[]{:S(2)}) collective-permute-start(f32[6,16,2,128]{3,1,2,0:T(8,128)S(1)} %copy.154), channel_id=1, source_target_pairs={{0,16},{16,32},{32,48},{1,17},{17,33},{33,49},{2,18},{18,34},{34,5... | collective-permute-start | bytes 294920 | tf_op jit(solution)/shard_map/ppermute | solution.py:17
  12.7 31.2 %collective-permute-start.4 = (f32[6,16,2,128]{3,1,2,0:T(8,128)S(1)}, f32[6,16,2,128]{3,1,2,0:T(8,128)S(1)}, u32[]{:S(2)}, u32[]{:S(2)}) collective-permute-start(f32[6,16,2,128]{3,1,2,0:T(8,128)S(1)} %copy.155), channel_id=1, source_target_pairs={{16,0},{32,16},{48,32},{17,1},{33,17},{49,33},{18,2},{34,18},{50,3... | collective-permute-start | bytes 294920 | tf_op jit(solution)/shard_map/ppermute | solution.py:18
  14.6 29.3 %collective-permute-start.2 = (f32[6,2,16,128]{3,2,1,0:T(8,128)S(1)}, f32[6,2,16,128]{3,2,1,0:T(8,128)S(1)}, u32[]{:S(2)}, u32[]{:S(2)}) collective-permute-start(f32[6,2,16,128]{3,2,1,0:T(8,128)S(1)} %get-tuple-element.60), channel_id=1, source_target_pairs={{0,64},{64,128},{128,192},{192,256},{256,320},{320,384},{384,448},... | collective-permute-start | bytes 294920 | tf_op jit(solution)/shard_map/ppermute | solution.py:17
  21.7 100.8 %all-to-all-start = ((s32[3,64,4]{2,0,1:T(4,128)}), s32[3,64,4]{2,0,1:T(4,128)S(1)}, u32[]{:S(2)}, u32[]{:S(2)}) async-start(s32[3,64,4]{2,0,1:T(4,128)} %copy.142), calls=%async_computation | async-start | bytes 262144 | tf_op jit(solution)/shard_map/all_to_all | solution.py:118
  40.6 9.4 %collective-permute-start.3 = (f32[6,2,16,128]{3,2,1,0:T(8,128)S(1)}, f32[6,2,16,128]{3,2,1,0:T(8,128)S(1)}, u32[]{:S(2)}, u32[]{:S(2)}) collective-permute-start(f32[6,2,16,128]{3,2,1,0:T(8,128)S(1)} %get-tuple-element.61), channel_id=1, source_target_pairs={{64,0},{128,64},{192,128},{256,192},{320,256},{384,320},{448,384},... | collective-permute-start | bytes 294920 | tf_op jit(solution)/shard_map/ppermute | solution.py:18
  52.0 0.9 copy-start
  55.0 25.9 %copy-start.7 = (f32[128,15]{0,1:T(8,128)S(1)}, f32[128,15]{0,1:T(8,128)}, u32[]{:S(2)}) copy-start(f32[128,15]{0,1:T(8,128)} %param.9) | copy-start | bytes 23044
  59.3 18.1 %collective-permute-start.6 = (f32[6,16,16,2]{2,1,3,0:T(8,128)}, f32[6,16,16,2]{2,1,3,0:T(8,128)}, u32[]{:S(2)}, u32[]{:S(2)}) collective-permute-start(f32[6,16,16,2]{2,1,3,0:T(8,128)} %copy.117), channel_id=1, source_target_pairs={{0,1},{1,2},{2,3},{3,4},{4,5},{5,6},{6,7},{7,8},{8,9},{9,10},{10,1... | collective-permute-start | bytes 36872 | tf_op jit(solution)/shard_map/ppermute | solution.py:17
  65.2 19.3 %collective-permute-start.11 = (f32[6,16,16,2]{2,1,3,0:T(8,128)}, f32[6,16,16,2]{2,1,3,0:T(8,128)}, u32[]{:S(2)}, u32[]{:S(2)}) collective-permute-start(f32[6,16,16,2]{2,1,3,0:T(8,128)} %copy.122), channel_id=1, source_target_pairs={{1,0},{2,1},{3,2},{4,3},{5,4},{6,5},{7,6},{8,7},{9,8},{10,9},{11,1... | collective-permute-start | bytes 36872 | tf_op jit(solution)/shard_map/ppermute | solution.py:18
  68.0 18.8 %collective-permute-start.7 = (f32[6,16,2,128]{3,1,2,0:T(8,128)}, f32[6,16,2,128]{3,1,2,0:T(8,128)}, u32[]{:S(2)}, u32[]{:S(2)}) collective-permute-start(f32[6,16,2,128]{3,1,2,0:T(8,128)} %copy.118), channel_id=1, source_target_pairs={{0,16},{16,32},{32,48},{1,17},{17,33},{33,49},{2,18},{18,34},{34,5... | collective-permute-start | bytes 294920 | tf_op jit(solution)/shard_map/ppermute | solution.py:17
  73.5 14.3 %collective-permute-start.10 = (f32[6,16,2,128]{3,1,2,0:T(8,128)}, f32[6,16,2,128]{3,1,2,0:T(8,128)}, u32[]{:S(2)}, u32[]{:S(2)}) collective-permute-start(f32[6,16,2,128]{3,1,2,0:T(8,128)} %copy.119), channel_id=1, source_target_pairs={{16,0},{32,16},{48,32},{17,1},{33,17},{49,33},{18,2},{34,18},{50,3... | collective-permute-start | bytes 294920 | tf_op jit(solution)/shard_map/ppermute | solution.py:18
  75.4 13.3 %collective-permute-start.8 = (f32[6,2,16,128]{3,2,1,0:T(8,128)}, f32[6,2,16,128]{3,2,1,0:T(8,128)}, u32[]{:S(2)}, u32[]{:S(2)}) collective-permute-start(f32[6,2,16,128]{3,2,1,0:T(8,128)} %get-tuple-element.54), channel_id=1, source_target_pairs={{0,64},{64,128},{128,192},{192,256},{256,320},{320,384},{384,448},... | collective-permute-start | bytes 294920 | tf_op jit(solution)/shard_map/ppermute | solution.py:17
  77.4 11.4 %collective-permute-start.9 = (f32[6,2,16,128]{3,2,1,0:T(8,128)}, f32[6,2,16,128]{3,2,1,0:T(8,128)}, u32[]{:S(2)}, u32[]{:S(2)}) collective-permute-start(f32[6,2,16,128]{3,2,1,0:T(8,128)} %get-tuple-element.55), channel_id=1, source_target_pairs={{64,0},{128,64},{192,128},{256,192},{320,256},{384,320},{448,384},... | collective-permute-start | bytes 294920 | tf_op jit(solution)/shard_map/ppermute | solution.py:18
  80.8 0.6 copy-start.5
  98.8 39.2 %collective-permute-start.12 = (f32[6,16,16,2]{2,1,3,0:T(8,128)}, f32[6,16,16,2]{2,1,3,0:T(8,128)}, u32[]{:S(2)}, u32[]{:S(2)}) collective-permute-start(f32[6,16,16,2]{2,1,3,0:T(8,128)} %copy.125), channel_id=1, source_target_pairs={{0,1},{1,2},{2,3},{3,4},{4,5},{5,6},{6,7},{7,8},{8,9},{9,10},{10,1... | collective-permute-start | bytes 36872 | tf_op jit(solution)/shard_map/ppermute | solution.py:17
  106.7 37.2 %collective-permute-start.17 = (f32[6,16,16,2]{2,1,3,0:T(8,128)}, f32[6,16,16,2]{2,1,3,0:T(8,128)}, u32[]{:S(2)}, u32[]{:S(2)}) collective-permute-start(f32[6,16,16,2]{2,1,3,0:T(8,128)} %copy.130), channel_id=1, source_target_pairs={{1,0},{2,1},{3,2},{4,3},{5,4},{6,5},{7,6},{8,7},{9,8},{10,9},{11,1... | collective-permute-start | bytes 36872 | tf_op jit(solution)/shard_map/ppermute | solution.py:18
  109.6 36.8 %collective-permute-start.13 = (f32[6,16,2,128]{3,1,2,0:T(8,128)}, f32[6,16,2,128]{3,1,2,0:T(8,128)}, u32[]{:S(2)}, u32[]{:S(2)}) collective-permute-start(f32[6,16,2,128]{3,1,2,0:T(8,128)} %copy.126), channel_id=1, source_target_pairs={{0,16},{16,32},{32,48},{1,17},{17,33},{33,49},{2,18},{18,34},{34,5... | collective-permute-start | bytes 294920 | tf_op jit(solution)/shard_map/ppermute | solution.py:17
  114.7 32.6 %collective-permute-start.16 = (f32[6,16,2,128]{3,1,2,0:T(8,128)}, f32[6,16,2,128]{3,1,2,0:T(8,128)}, u32[]{:S(2)}, u32[]{:S(2)}) collective-permute-start(f32[6,16,2,128]{3,1,2,0:T(8,128)} %copy.127), channel_id=1, source_target_pairs={{16,0},{32,16},{48,32},{17,1},{33,17},{49,33},{18,2},{34,18},{50,3... | collective-permute-start | bytes 294920 | tf_op jit(solution)/shard_map/ppermute | solution.py:18
  116.6 31.7 %collective-permute-start.14 = (f32[6,2,16,128]{3,2,1,0:T(8,128)}, f32[6,2,16,128]{3,2,1,0:T(8,128)}, u32[]{:S(2)}, u32[]{:S(2)}) collective-permute-start(f32[6,2,16,128]{3,2,1,0:T(8,128)} %get-tuple-element.48), channel_id=1, source_target_pairs={{0,64},{64,128},{128,192},{192,256},{256,320},{320,384},{384,448},... | collective-permute-start | bytes 294920 | tf_op jit(solution)/shard_map/ppermute | solution.py:17
  122.5 117.4 %all-to-all-start.1 = ((f32[15,64,4]{0,2,1:T(4,128)}), f32[15,64,4]{0,2,1:T(4,128)S(1)}, u32[]{:S(2)}, u32[]{:S(2)}) async-start(f32[15,64,4]{0,2,1:T(4,128)} %bitcast.55), calls=%async_computation.1 | async-start | bytes 262144 | tf_op jit(solution)/shard_map/all_to_all | solution.py:121
  138.0 10.3 %collective-permute-start.15 = (f32[6,2,16,128]{3,2,1,0:T(8,128)}, f32[6,2,16,128]{3,2,1,0:T(8,128)}, u32[]{:S(2)}, u32[]{:S(2)}) collective-permute-start(f32[6,2,16,128]{3,2,1,0:T(8,128)} %get-tuple-element.49), channel_id=1, source_target_pairs={{64,0},{128,64},{192,128},{256,192},{320,256},{384,320},{448,384},... | collective-permute-start | bytes 294920 | tf_op jit(solution)/shard_map/ppermute | solution.py:18
  153.8 0.9 copy-start.3
  159.3 24.0 %collective-permute-start.18 = (f32[6,16,16,2]{2,1,3,0:T(8,128)}, f32[6,16,16,2]{2,1,3,0:T(8,128)}, u32[]{:S(2)}, u32[]{:S(2)}) collective-permute-start(f32[6,16,16,2]{2,1,3,0:T(8,128)} %copy.133), channel_id=1, source_target_pairs={{0,1},{1,2},{2,3},{3,4},{4,5},{5,6},{6,7},{7,8},{8,9},{9,10},{10,1... | collective-permute-start | bytes 36872 | tf_op jit(solution)/shard_map/ppermute | solution.py:17
  166.3 23.2 %collective-permute-start.23 = (f32[6,16,16,2]{2,1,3,0:T(8,128)}, f32[6,16,16,2]{2,1,3,0:T(8,128)}, u32[]{:S(2)}, u32[]{:S(2)}) collective-permute-start(f32[6,16,16,2]{2,1,3,0:T(8,128)} %copy.138), channel_id=1, source_target_pairs={{1,0},{2,1},{3,2},{4,3},{5,4},{6,5},{7,6},{8,7},{9,8},{10,9},{11,1... | collective-permute-start | bytes 36872 | tf_op jit(solution)/shard_map/ppermute | solution.py:18
  169.1 22.8 %collective-permute-start.19 = (f32[6,16,2,128]{3,1,2,0:T(8,128)}, f32[6,16,2,128]{3,1,2,0:T(8,128)}, u32[]{:S(2)}, u32[]{:S(2)}) collective-permute-start(f32[6,16,2,128]{3,1,2,0:T(8,128)} %copy.134), channel_id=1, source_target_pairs={{0,16},{16,32},{32,48},{1,17},{17,33},{33,49},{2,18},{18,34},{34,5... | collective-permute-start | bytes 294920 | tf_op jit(solution)/shard_map/ppermute | solution.py:17
  173.9 18.9 %collective-permute-start.22 = (f32[6,16,2,128]{3,1,2,0:T(8,128)}, f32[6,16,2,128]{3,1,2,0:T(8,128)}, u32[]{:S(2)}, u32[]{:S(2)}) collective-permute-start(f32[6,16,2,128]{3,1,2,0:T(8,128)} %copy.135), channel_id=1, source_target_pairs={{16,0},{32,16},{48,32},{17,1},{33,17},{49,33},{18,2},{34,18},{50,3... | collective-permute-start | bytes 294920 | tf_op jit(solution)/shard_map/ppermute | solution.py:18
  175.8 18.0 %collective-permute-start.20 = (f32[6,2,16,128]{3,2,1,0:T(8,128)}, f32[6,2,16,128]{3,2,1,0:T(8,128)}, u32[]{:S(2)}, u32[]{:S(2)}) collective-permute-start(f32[6,2,16,128]{3,2,1,0:T(8,128)} %get-tuple-element.42), channel_id=1, source_target_pairs={{0,64},{64,128},{128,192},{192,256},{256,320},{320,384},{384,448},... | collective-permute-start | bytes 294920 | tf_op jit(solution)/shard_map/ppermute | solution.py:17
  183.3 10.5 %collective-permute-start.21 = (f32[6,2,16,128]{3,2,1,0:T(8,128)}, f32[6,2,16,128]{3,2,1,0:T(8,128)}, u32[]{:S(2)}, u32[]{:S(2)}) collective-permute-start(f32[6,2,16,128]{3,2,1,0:T(8,128)} %get-tuple-element.43), channel_id=1, source_target_pairs={{64,0},{128,64},{192,128},{256,192},{320,256},{384,320},{448,384},... | collective-permute-start | bytes 294920 | tf_op jit(solution)/shard_map/ppermute | solution.py:18
  197.7 1.6 copy-start.4
  199.3 23.3 %copy-start.6 = (s32[5,5,5]{2,1,0:T(8,128)S(1)}, s32[5,5,5]{2,1,0:T(8,128)}, u32[]{:S(2)}) copy-start(s32[5,5,5]{2,1,0:T(8,128)} %copy-done.5) | copy-start | bytes 1504
  199.6 47.8 %copy-start.2 = (f32[6,16,16,128]{3,2,1,0:T(8,128)}, f32[6,16,16,128]{3,2,1,0:T(8,128)S(1)}, u32[]{:S(2)}) copy-start(f32[6,16,16,128]{3,2,1,0:T(8,128)S(1)} %multiply_add_fusion) | copy-start | bytes 2359300
  199.7 8.9 %collective-permute-start.24 = (f32[6,2,16,128]{3,2,1,0:T(8,128)S(1)}, f32[6,2,16,128]{3,2,1,0:T(8,128)S(1)}, u32[]{:S(2)}, u32[]{:S(2)}) collective-permute-start(f32[6,2,16,128]{3,2,1,0:T(8,128)S(1)} %get-tuple-element.40), channel_id=1, source_target_pairs={{0,64},{64,128},{128,192},{192,256},{256,320},{320,384},{384,448},... | collective-permute-start | bytes 294920 | tf_op jit(solution)/shard_map/ppermute | solution.py:37
  206.6 9.1 %collective-permute-start.25 = (f32[6,2,16,128]{3,2,1,0:T(8,128)S(1)}, f32[6,2,16,128]{3,2,1,0:T(8,128)S(1)}, u32[]{:S(2)}, u32[]{:S(2)}) collective-permute-start(f32[6,2,16,128]{3,2,1,0:T(8,128)S(1)} %get-tuple-element.41), channel_id=1, source_target_pairs={{64,0},{128,64},{192,128},{256,192},{320,256},{384,320},{448,384},... | collective-permute-start | bytes 294920 | tf_op jit(solution)/shard_map/ppermute | solution.py:39
  215.8 7.0 %collective-permute-start.26 = (f32[6,20,2,128]{3,2,1,0:T(2,128)S(1)}, f32[6,20,2,128]{3,2,1,0:T(2,128)S(1)}, u32[]{:S(2)}, u32[]{:S(2)}) collective-permute-start(f32[6,20,2,128]{3,2,1,0:T(2,128)S(1)} %get-tuple-element.38), channel_id=1, source_target_pairs={{0,16},{16,32},{32,48},{1,17},{17,33},{33,49},{2,18},{18,34},{34,5... | collective-permute-start | bytes 368648 | tf_op jit(solution)/shard_map/ppermute | solution.py:37
  220.7 6.2 %collective-permute-start.27 = (f32[6,20,2,128]{3,2,1,0:T(2,128)S(1)}, f32[6,20,2,128]{3,2,1,0:T(2,128)S(1)}, u32[]{:S(2)}, u32[]{:S(2)}) collective-permute-start(f32[6,20,2,128]{3,2,1,0:T(2,128)S(1)} %get-tuple-element.39), channel_id=1, source_target_pairs={{16,0},{32,16},{48,32},{17,1},{33,17},{49,33},{18,2},{34,18},{50,3... | collective-permute-start | bytes 368648 | tf_op jit(solution)/shard_map/ppermute | solution.py:39
  231.8 8.6 %collective-permute-start.28 = (f32[6,20,20,2]{2,1,3,0:T(8,128)}, f32[6,20,20,2]{2,1,3,0:T(8,128)}, u32[]{:S(2)}, u32[]{:S(2)}) collective-permute-start(f32[6,20,20,2]{2,1,3,0:T(8,128)} %copy.157), channel_id=1, source_target_pairs={{0,1},{1,2},{2,3},{3,4},{4,5},{5,6},{6,7},{7,8},{8,9},{9,10},{10,1... | collective-permute-start | bytes 57608 | tf_op jit(solution)/shard_map/ppermute | solution.py:37
  238.3 6.2 %collective-permute-start.29 = (f32[6,20,20,2]{2,1,3,0:T(8,128)}, f32[6,20,20,2]{2,1,3,0:T(8,128)}, u32[]{:S(2)}, u32[]{:S(2)}) collective-permute-start(f32[6,20,20,2]{2,1,3,0:T(8,128)} %copy.158), channel_id=1, source_target_pairs={{1,0},{2,1},{3,2},{4,3},{5,4},{6,5},{7,6},{8,7},{9,8},{10,9},{11,1... | collective-permute-start | bytes 57608 | tf_op jit(solution)/shard_map/ppermute | solution.py:39
  346.4 29.4 %all-to-all-start.2 = ((f32[6,64,4]{0,2,1:T(4,128)}), f32[6,64,4]{0,2,1:T(4,128)S(1)}, u32[]{:S(2)}, u32[]{:S(2)}) async-start(f32[6,64,4]{0,2,1:T(4,128)} %bitcast.59), calls=%async_computation.2 | async-start | bytes 262144 | tf_op jit(solution)/shard_map/all_to_all | solution.py:127
where the time goes:
time: 380 us; the launch traced here: 377 us
  local copies, waits for them, and re-layouts  158 us (42%)
  starting transfers between devices  146 us (38%)
  other arithmetic  36.2 us (10%)
  waiting for transfers between devices  35.7 us (9%)
    gather x1, local copies, waits for them, and re-layouts, gather_tiles(): picked = jnp.take(flat_grid, offsets[:, None] + starts[None, :], axis=1)  67.8 us
    ppermute x12, starting transfers between devices, extended(): lax.ppermute(last, axis, up)  53.5 us
    unnamed x45, local copies, waits for them, and re-layouts  29.2 us
    ppermute x12, starting transfers between devices, extended(): lax.ppermute(initial, axis, [(b, a) for a, b in up])  22.1 us
    slice x18, local copies, waits for them, and re-layouts, extended(): last = lax.slice_in_dim(array, length - width, length, axis=dim)  21.8 us
    all_to_all x1, starting transfers between devices, local(): lax.all_to_all(corner_send, ('gy', 'gz'), split_axis=1, concat_axis=1, ti...  18.8 us
    reshape x2, local copies, waits for them, and re-layouts, gather_tiles(): flat_grid = donor_grid.reshape(components, extent_x * extent_y * extent_z)  17.3 us
    ppermute x3, starting transfers between devices, padded_2(): lax.ppermute(tail, axis, [(i, (i + 1) % count) for i in range(ends)])  16.8 us
  transfers between devices with their start and end apart: 33, of which 5 were waited for; matrix products, arithmetic and copies ran while one was open for 23% of the time, Pallas kernels for 0%

commit v1 on v0

v1 whole, which is shorter than its diff:
```python
import jax
import jax.numpy as jnp
from jax import lax
from jax.experimental import pallas as pl
from jax.experimental.pallas import tpu as pltpu
from jax.sharding import PartitionSpec as P

STEP = 0.25
CX, CY, CZ = 16, 16, 128
GX, GZ = 10, 10
NF = 7
PAIRS = NF * CX
ZPER, YPER = 12, 6
ZGROUPS = -(-PAIRS // ZPER)
YGROUPS = -(-PAIRS // YPER)
XW = CX + 2 * GX
STRIDE = 20
EXACT = lax.Precision.HIGHEST
F32 = jnp.float32


def x_list():
    entries = []
    for k in range(1, 5):
        entries += [(k, c, t) for c in range(NF) for t in (0, 1, 2, 3)]
    for k in range(5, 9):
        entries += [(k, c, t) for c in range(NF) for t in (1, 2, 4)]
    for k in range(9, 11):
        entries += [(k, c, t) for c in (1, 2, 4, 5) for t in (1, 2)]
    return entries


XLIST = x_list()
XROWS = len(XLIST)
XGROUPS = -(-XROWS // YPER)


def roll(value, shift, axis):
    size = value.shape[axis]
    shift = shift % size
    return value if shift == 0 else pltpu.roll(value, shift, axis)


def lanes(shape):
    return lax.broadcasted_iota(jnp.int32, shape, len(shape) - 1)


def rows_of(shape):
    return lax.broadcasted_iota(jnp.int32, shape, len(shape) - 2)


def vmem(count):
    return [pl.BlockSpec(memory_space=pltpu.VMEM)] * count


def call(body, outs, ins, limit, scratch=(), flops=1000000):
    many = isinstance(outs, list)
    return pl.pallas_call(
        body,
        out_shape=[jax.ShapeDtypeStruct(s, F32) for s in outs] if many else jax.ShapeDtypeStruct(outs, F32),
        in_specs=vmem(len(ins)),
        out_specs=vmem(len(outs)) if many else vmem(1)[0],
        scratch_shapes=list(scratch),
        compiler_params=pltpu.CompilerParams(vmem_limit_bytes=limit * 1048576),
        cost_estimate=pl.CostEstimate(flops=flops, bytes_accessed=1000000, transcendentals=0),
    )(*ins)


def pack_z(f_ref, e_ref, lo_ref, hi_ref, inv_ref):
    inv_ref[...] = 1.0 / e_ref[...]
    lane = lanes((CY, CZ))
    for g in range(ZGROUPS):
        lo = jnp.zeros((CY, CZ), F32)
        hi = jnp.zeros((CY, CZ), F32)
        for j in range(min(ZPER, PAIRS - g * ZPER)):
            c, x = divmod(g * ZPER + j, CX)
            tile = f_ref[c, x] if c < 6 else inv_ref[x]
            lo = lo + roll(jnp.where(lane < GZ, tile, 0.0), GZ * j, 1)
            hi = hi + roll(jnp.where(lane >= CZ - GZ, tile, 0.0), GZ * (j + 1), 1)
        lo_ref[g] = lo
        hi_ref[g] = hi


def pack_y(f_ref, inv_ref, zlo_ref, zhi_ref, h_ref, lo_ref, hi_ref):
    lane = lanes((CY, CZ))
    for g in range(YGROUPS):
        lo = jnp.zeros((8, CZ), F32)
        hi = jnp.zeros((8, CZ), F32)
        for j in range(min(YPER, PAIRS - g * YPER)):
            p = g * YPER + j
            c, x = divmod(p, CX)
            zg, zj = divmod(p, ZPER)
            below = roll(zlo_ref[zg], CZ - GZ - GZ * zj, 1)
            above = roll(zhi_ref[zg], -GZ * zj, 1)
            ghost = jnp.where(lane >= CZ - GZ, below, jnp.where(lane < GZ, above, 0.0))
            h_ref[c, x] = ghost
            tile = f_ref[c, x] if c < 6 else inv_ref[x]
            lo_ref[p] = tile[0:8]
            hi_ref[p] = tile[8:16]
            packed = roll(ghost, GZ + 2 * GZ * j, 1)
            lo = lo + packed[0:8]
            hi = hi + packed[8:16]
        lo_ref[PAIRS + g] = lo
        hi_ref[PAIRS + g] = hi


def ring_lanes(packed, j, lane):
    moved = roll(packed, -(GZ + 2 * GZ * j), 1)
    return jnp.where((lane < GZ) | (lane >= CZ - GZ), moved, 0.0)


def pack_x(f_ref, inv_ref, h_ref, ylo_ref, yhi_ref, lo_ref, hi_ref):
    lane = lanes((8, CZ))
    row = rows_of((8, CZ))

    def tile_of(c, x, t):
        p = c * CX + x
        if t in (1, 2):
            own = pl.ds(8 * (t - 1), 8)
            main = f_ref[c, x, own] if c < 6 else inv_ref[x, own]
            return main, h_ref[c, x, own]
        if t == 4:
            a, b = tile_of(c, x, 0), tile_of(c, x, 3)
            return jnp.where(row >= 4, a[0], b[0]), jnp.where(row >= 4, a[1], b[1])
        ref = ylo_ref if t == 0 else yhi_ref
        return ref[p], ring_lanes(ref[PAIRS + p // YPER], p % YPER, lane)

    for ref, side in ((lo_ref, 0), (hi_ref, 1)):
        for g in range(XGROUPS):
            total = jnp.zeros((8, CZ), F32)
            for j in range(min(YPER, XROWS - g * YPER)):
                n = g * YPER + j
                k, c, t = XLIST[n]
                main, ghost = tile_of(c, k - 1 if side == 0 else CX - k, t)
                ref[n] = main
                total = total + roll(ghost, GZ + 2 * GZ * j, 1)
            ref[XROWS + g] = total


def along_y(tiles, t, row):
    before, here, after = tiles[(t - 1) % 4], tiles[t], tiles[(t + 1) % 4]
    down = lambda d: roll(jnp.where(row >= 8 - d, before, here), d, 0)
    up = lambda d: roll(jnp.where(row < d, after, here), -d, 0)
    return up(1) - down(1), down(2) - up(2)


def along_z(here, other, lane):
    down = lambda d: roll(jnp.where(lane >= CZ - d, other, here), d, 1)
    up = lambda d: roll(jnp.where(lane < d, other, here), -d, 1)
    return up(1) - down(1), down(2) - up(2)


def taylor(source, inv_ref, x, tiles, scale, put):
    row = rows_of((8, CZ))
    lane = lanes((8, CZ))
    for t in tiles:
        for half in (0, 1):
            def dx(c):
                at = lambda d: source[half, c, x + d, t]
                return at(1) - at(-1), at(-2) - at(2)

            def dy(c):
                near = {u % 4: source[half, c, x, u % 4] for u in (t - 1, t, t + 1)}
                return along_y(near, t, row)

            def dz(c):
                return along_z(source[half, c, x, t], source[1 - half, c, x, t], lane)

            def rate(plus, minus):
                return (plus[1] - minus[1]) + 8.0 * (plus[0] - minus[0])

            inv = inv_ref[half, 6, x, t]
            electric = inv * scale
            magnetic = jnp.where(inv > 0.0, scale, 0.0)
            put(half, 0, t, electric * rate(dy(5), dz(4)))
            put(half, 1, t, electric * rate(dz(3), dx(5)))
            put(half, 2, t, electric * rate(dx(4), dy(3)))
            put(half, 3, t, magnetic * rate(dz(1), dy(2)))
            put(half, 4, t, magnetic * rate(dx(2), dz(0)))
            put(half, 5, t, magnetic * rate(dy(0), dx(1)))


def dot(a, b, da=1, db=0):
    return lax.dot_general(a, b, (((da,), (db,)), ((), ())), precision=EXACT, preferred_element_type=F32)


def spread(count, parity):
    shape = (count, 128)
    return (lanes(shape) == rows_of(shape) + parity * 64).astype(F32)


def compute(
    f_ref, own_inv_ref, h_ref, ylo_ref, yhi_ref, xlo_ref, xhi_ref, req_ref,
    new_ref, ans_ref,
    full, t1, t2, t3, acc, words, wz, wxy, spill, parts,
):
    lane = lanes((8, CZ))
    row = rows_of((8, CZ))
    zero = jnp.zeros((8, CZ), F32)
    for p in range(PAIRS):
        c, x = divmod(p, CX)
        for t in (1, 2):
            own = pl.ds(8 * (t - 1), 8)
            full[0, c, GX + x, t] = f_ref[c, x, own] if c < 6 else own_inv_ref[x, own]
            full[1, c, GX + x, t] = h_ref[c, x, own]
        for ref, t in ((ylo_ref, 0), (yhi_ref, 3)):
            full[0, c, GX + x, t] = ref[p]
            full[1, c, GX + x, t] = ring_lanes(ref[PAIRS + p // YPER], p % YPER, lane)
    for side in (0, 1):
        ref = xlo_ref if side == 0 else xhi_ref
        for n, (k, c, t) in enumerate(XLIST):
            x = GX - k if side == 0 else GX + CX + k - 1
            pair = (ref[n], ring_lanes(ref[XROWS + n // YPER], n % YPER, lane))
            for half in (0, 1):
                if t == 4:
                    full[half, c, x, 0] = jnp.where(row >= 4, pair[half], 0.0)
                    full[half, c, x, 3] = jnp.where(row >= 4, 0.0, pair[half])
                else:
                    full[half, c, x, t] = pair[half]
        for k in (9, 10):
            x = GX - k if side == 0 else GX + CX + k - 1
            for c in (1, 2, 4, 5):
                for half in (0, 1):
                    full[half, c, x, 0] = zero
                    full[half, c, x, 3] = zero

    for power, source, target in ((1, full, t1), (2, t1, t2), (3, t2, t3)):
        def body(x, carry, source=source, target=target, power=power):
            def put(half, c, t, value):
                target[half, c, x, t] = value

            taylor(source, full, x, (0, 1, 2, 3), STEP / power / 12.0, put)
            return carry

        lax.fori_loop(2 * power, XW - 2 * power, body, 0)

    def last(x, carry):
        def put(half, c, t, value):
            total = full[half, c, x, t] + t1[half, c, x, t]
            total = total + t2[half, c, x, t]
            total = total + t3[half, c, x, t]
            acc[half, c, x - 8, t - 1] = total + value

        taylor(t3, full, x, (1, 2), STEP / 4 / 12.0, put)
        return carry

    lax.fori_loop(8, XW - 8, last, 0)
    for c in range(6):
        for t in (0, 1):
            new_ref[c, :, pl.ds(8 * t, 8), :] = acc[0, c, 2:18, t]

    req = req_ref[...]
    words[0] = dot(req, spread(64, 0), 0, 0)
    words[1] = dot(req, spread(64, 1), 0, 0)

    def word(pair, w):
        even = words[0, pl.ds(2 * pair * STRIDE + w, 1), :]
        return even + words[1, pl.ds((2 * pair + 1) * STRIDE + w, 1), :]

    cell = rows_of((CZ, 128)).astype(F32)
    low = rows_of((8, 128)).astype(F32)
    for pair in range(6):
        kind, at = divmod(pair, 2)
        columns = pl.ds(128 * at, 128)
        bx, by, bz = word(pair, 0), word(pair, 1), word(pair, 2)
        wx = [word(pair, 3 + i) for i in range(5)]
        wy = [word(pair, 8 + i) for i in range(5)]
        wz_rows = [word(pair, 13 + i) for i in range(5)]

        def weights(position, base, values):
            away = position - base
            total = jnp.zeros(away.shape, F32)
            for i in range(5):
                total = jnp.where(away == float(i), values[i], total)
            return total

        wz[kind, pl.ds(0, CZ), columns] = weights(cell + 2.0, bz, wz_rows)
        wz[kind, pl.ds(CZ, CZ), columns] = jnp.zeros((CZ, 128), F32)
        wz[kind, pl.ds(CZ, 8), columns] = weights(low + (CZ + 2.0), bz, wz_rows)
        wz[kind, pl.ds(2 * CZ - 8, 8), columns] = weights(low - 6.0, bz, wz_rows)
        in_x = [weights(jnp.full((1, 128), float(x), F32), bx, wx) for x in range(CX + 4)]
        for t in (0, 1):
            in_y = weights(low + (8.0 * t + 2.0), by, wy)
            for x in range(CX + 4):
                if kind == 0:
                    wxy[x, t, :, columns] = in_x[x] * in_y
                elif kind == 2 - t:
                    spill[kind - 1, x, :, columns] = in_x[x] * in_y

    parts[...] = jnp.zeros((48, 128), F32)
    for c in range(6):
        def both(t):
            grid = [acc[half, c] if t is None else acc[half, c, :, t] for half in (0, 1)]
            return jnp.concatenate([g.reshape(-1, CZ) for g in grid], axis=1)

        for kind, t, weight in ((0, None, wxy), (1, 1, spill.at[0]), (2, 0, spill.at[1])):
            along = dot(both(t), wz[kind])
            product = along * weight[...].reshape(along.shape)
            total = jnp.sum(product, axis=0, keepdims=True)
            for at in (0, 1):
                parts[pl.ds((2 * kind + at) * 8 + c, 1), :] = total[:, 128 * at:128 * at + 128]
    values = parts[...]
    blank = jnp.zeros((16, 128), F32)
    filled = jnp.concatenate([values, blank], axis=0)
    empty = jnp.zeros((64, 128), F32)
    ans_ref[...] = dot(spread(64, 0), jnp.concatenate([filled, empty], axis=0), 1, 1) + dot(
        spread(64, 1), jnp.concatenate([empty, filled], axis=0), 1, 1
    )


def requests(data_ref, send_ref, pick_ref, rank_ref):
    data = data_ref[...]
    wide = (128, 128)
    owner = jnp.broadcast_to(data[:, 18:19], wide)
    base_y = jnp.broadcast_to(data[:, 1:2], wide)
    r, q = rows_of(wide), lanes(wide)
    owner_row = jnp.sum(jnp.where(r == q, owner, 0.0), axis=0, keepdims=True)
    base_row = jnp.sum(jnp.where(r == q, base_y, 0.0), axis=0, keepdims=True)
    same = owner == owner_row
    rank_col = jnp.sum(jnp.where(same & (q < r), 1.0, 0.0), axis=1, keepdims=True)
    rank_row = jnp.sum(jnp.where(same & (r < q), 1.0, 0.0), axis=0, keepdims=True)
    rank_ref[...] = jnp.broadcast_to(rank_row, (8, 128))

    lane = lanes((128, 256))
    slot, w = lane // STRIDE, lane % STRIDE
    word_row = rows_of((128, 256))
    copies = jnp.where((lanes((128, 256)) % STRIDE == word_row) & (word_row < 18) & (lane < 12 * STRIDE), 1.0, 0.0)
    spread_out = dot(data, copies)
    moved = jnp.where(w == 1, jnp.where(slot // 4 == 1, float(CY), jnp.where(slot // 4 == 2, -float(CY), 0.0)), 0.0)
    chosen = (slot % 4).astype(F32) == rank_col
    spread_out = jnp.where(chosen, spread_out + moved, 0.0)

    place = rows_of((64, 128)).astype(F32)
    total = jnp.zeros((64, 256), F32)
    for kind, move in ((0, 0.0), (1, -16.0), (2, 16.0)):
        hit = place == owner_row + move
        if kind == 1:
            hit = hit & (base_row < 2.0)
        if kind == 2:
            hit = hit & (base_row > 13.0)
        pick = jnp.where(hit, 1.0, 0.0)
        pick_ref[kind] = pick
        total = total + dot(pick, jnp.where(slot // 4 == kind, spread_out, 0.0))
    send_ref[...] = total


def collect(ans_ref, pick_ref, rank_ref, out_ref):
    ans = ans_ref[...]
    rank = rank_ref[...]
    total = jnp.zeros((8, 128), F32)
    for kind in range(3):
        got = dot(ans, pick_ref[kind], 0, 0)
        for j in range(4):
            start = (j % 2) * 64 + (2 * kind + j // 2) * 8
            total = total + jnp.where(rank == float(j), got[start:start + 8], 0.0)
    out_ref[...] = total[0:6]


def shift_both(low_edge, high_edge, axis):
    size = lax.axis_size(axis)
    up = [(i, i + 1) for i in range(size - 1)]
    down = [(i + 1, i) for i in range(size - 1)]
    return lax.ppermute(high_edge, axis, up), lax.ppermute(low_edge, axis, down)


def local(fields, permittivity, donor_owner, donor_base, donor_weights):
    data = jnp.concatenate(
        [
            donor_base.astype(F32),
            donor_weights,
            donor_owner.astype(F32),
            jnp.zeros((donor_owner.shape[0], 128 - 19), F32),
        ],
        axis=1,
    )
    zshape = (ZGROUPS, CY, CZ)
    zlo, zhi, inv = call(pack_z, [zshape, zshape, (CX, CY, CZ)], (fields, permittivity), 16)
    zlo, zhi = shift_both(zlo, zhi, "gz")
    yshape = (PAIRS + YGROUPS, 8, CZ)
    ghosts, ylo, yhi = call(pack_y, [(NF, CX, CY, CZ), yshape, yshape], (fields, inv, zlo, zhi), 16)
    ylo, yhi = shift_both(ylo, yhi, "gy")
    xshape = (XROWS + XGROUPS, 8, CZ)
    xlo, xhi = call(pack_x, [xshape, xshape], (fields, inv, ghosts, ylo, yhi), 20)
    send, pick, rank = call(requests, [(64, 256), (3, 64, 128), (8, 128)], (data,), 8)
    send, xlo, xhi = lax.optimization_barrier((send, xlo, xhi))
    xlo, xhi = shift_both(xlo, xhi, "gx")
    req = lax.all_to_all(send, ("gy", "gz"), 0, 0, tiled=True)
    big = pltpu.VMEM((2, 6, XW, 4, 8, CZ), F32)
    new_fields, answers = call(
        compute,
        [(6, CX, CY, CZ), (64, 128)],
        (fields, inv, ghosts, ylo, yhi, xlo, xhi, req),
        48,
        scratch=[
            pltpu.VMEM((2, NF, XW, 4, 8, CZ), F32),
            big,
            big,
            big,
            pltpu.VMEM((2, 6, CX + 4, 2, 8, CZ), F32),
            pltpu.VMEM((2, 256, 128), F32),
            pltpu.VMEM((3, 256, 256), F32),
            pltpu.VMEM((CX + 4, 2, 8, 256), F32),
            pltpu.VMEM((2, CX + 4, 8, 256), F32),
            pltpu.VMEM((48, 128), F32),
        ],
        flops=100000000,
    )
    answers = lax.all_to_all(answers, ("gy", "gz"), 0, 0, tiled=True)
    receptor_values = call(collect, (6, 128), (answers, pick, rank), 8)
    return new_fields, receptor_values


def solution(mesh):
    placed = (
        P(None, "gx", "gy", "gz"),
        P("gx", "gy", "gz"),
        P(("gx", "gy", "gz"), None),
        P(("gx", "gy", "gz"), None),
        P(("gx", "gy", "gz"), None),
    )
    return jax.shard_map(
        local,
        mesh=mesh,
        in_specs=placed,
        out_specs=(P(None, "gx", "gy", "gz"), P(None, ("gx", "gy", "gz"))),
        check_vma=False,
    )
```

time: 380 us -> 125 us (0.33)
  local copies, waits for them, and re-layouts: 158 us -> 3.77 us
  starting transfers between devices: 146 us -> 18.3 us
  blocking collectives: 0 us -> 51.5 us
  Pallas kernels: 0 us -> 40 us
  other arithmetic: 36.2 us -> 0.98 us
  waiting for transfers between devices: 35.7 us -> 9.33 us
    ppermute x30 -> x6, starting transfers between devices: 97.8 us -> 18.3 us  [the longest x3 13.1 us: shift_both(): lax.ppermute(high_edge, axis, up)]
    gather x2 -> x0, local copies, waits for them, and re-layouts: 68.5 us -> none  [the longest x1 67.8 us: gather_tiles(): picked = jnp.take(flat_grid, offsets[:, None] + starts[None, :], axis=1)]
    all_to_all x0 -> x2, blocking collectives: none -> 51.5 us  [the longest x1 29.6 us: local(): req = lax.all_to_all(send, ('gy', 'gz'), 0, 0, tiled=True)]
    all_to_all x3 -> x0, starting transfers between devices: 47.8 us -> none  [the longest x1 18.8 us: local(): lax.all_to_all(corner_send, ('gy', 'gz'), split_axis=1, concat_axis=1, ti...]
    pallas_call x0 -> x6, Pallas kernels: none -> 40 us  [call(): pl.pallas_call(body, out_shape=[jax.ShapeDtypeStruct(s, F32) for s in out...]
    slice x27 -> x0, local copies, waits for them, and re-layouts: 31.6 us -> none  [the longest x18 21.8 us: extended(): last = lax.slice_in_dim(array, length - width, length, axis=dim)]
    unnamed x45 -> x14, local copies, waits for them, and re-layouts: 29.2 us -> 2.77 us
    reshape x3 -> x0, local copies, waits for them, and re-layouts: 18.4 us -> none  [the longest x2 17.3 us: gather_tiles(): flat_grid = donor_grid.reshape(components, extent_x * extent_y * extent_z)]
  transfers between devices with their start and end apart: 33 -> 6, of which waited for: 5 -> 4; matrix products, arithmetic and copies ran while one was open for 23% -> 2% of each run, Pallas kernels for 0% -> 1%
where the time goes in v1:
time: 125 us
  blocking collectives  51.5 us (41%)
  Pallas kernels  40 us (32%)
  starting transfers between devices  18.3 us (15%)
  waiting for transfers between devices  9.33 us (7%)
  local copies, waits for them, and re-layouts  3.77 us (3%)
    pallas_call x6, Pallas kernels, call(): pl.pallas_call(body, out_shape=[jax.ShapeDtypeStruct(s, F32) for s in out...  40 us
    all_to_all x1, blocking collectives, local(): req = lax.all_to_all(send, ('gy', 'gz'), 0, 0, tiled=True)  29.6 us
    all_to_all x1, blocking collectives, local(): answers = lax.all_to_all(answers, ('gy', 'gz'), 0, 0, tiled=True)  21.9 us
    ppermute x3, starting transfers between devices, shift_both(): lax.ppermute(high_edge, axis, up)  13.1 us
    ppermute x3, waiting for transfers between devices, shift_both(): lax.ppermute(low_edge, axis, down)  7.99 us
    ppermute x3, starting transfers between devices, shift_both(): lax.ppermute(low_edge, axis, down)  5.13 us
    unnamed x14, local copies, waits for them, and re-layouts  2.77 us
  transfers between devices with their start and end apart: 6, of which 4 were waited for; matrix products, arithmetic and copies ran while one was open for 2% of the time, Pallas kernels for 1%

profile of v1, /device:TPU:7, one launch (start us, length us, event | category | flops | bytes accessed | tf_op | source)
XLA Modules:
  0.0 124.6 jit_solution(15700089090321130502)
XLA Ops:
  0.6 0.0 copy-start
  0.6 1.1 copy-done
  1.8 0.0 copy-start.2
  1.8 0.9 copy-done.2
  2.7 0.5 shard_map.68
  3.2 3.5 %collective-permute-start = (f32[10,16,128]{2,1,0:T(8,128)S(1)}, f32[10,16,128]{2,1,0:T(8,128)S(1)}, u32[]{:S(2)}, u32[]{:S(2)}) collective-permute-start(f32[10,16,128]{2,1,0:T(8,128)S(1)} %get-tuple-element.19), channel_id=1, source_target_pairs={{0,1},{1,2},{2,3},{3,4},{4,5},{5,6},{6,7},{7,8},{8,9},{9,10},{10,1... | collective-permute-start | bytes 245768 | tf_op jit(solution)/shard_map/ppermute | solution.py:363
  6.7 1.3 %collective-permute-start.1 = (f32[10,16,128]{2,1,0:T(8,128)S(1)}, f32[10,16,128]{2,1,0:T(8,128)S(1)}, u32[]{:S(2)}, u32[]{:S(2)}) collective-permute-start(f32[10,16,128]{2,1,0:T(8,128)S(1)} %get-tuple-element.20), channel_id=1, source_target_pairs={{1,0},{2,1},{3,2},{4,3},{5,4},{6,5},{7,6},{8,7},{9,8},{10,9},{11,1... | collective-permute-start | bytes 245768 | tf_op jit(solution)/shard_map/ppermute | solution.py:363
  8.0 0.2 collective-permute-done.zlo_ref
  8.2 3.9 %collective-permute-done.1.zhi_ref = f32[10,16,128]{2,1,0:T(8,128)S(1)} collective-permute-done((f32[10,16,128]{2,1,0:T(8,128)S(1)}, f32[10,16,128]{2,1,0:T(8,128)S(1)}, u32[]{:S(2)}, u32[]{:S(2)}) %collective-permute-start.1) | collective-permute-done | bytes 81952 | tf_op jit(solution)/shard_map/ppermute | solution.py:363
  12.1 0.0 copy-start.1
  12.1 7.5 %shard_map.69 = (f32[7,16,16,128]{3,2,1,0:T(8,128)S(1)}, f32[131,8,128]{2,1,0:T(8,128)S(1)}, f32[131,8,128]{2,1,0:T(8,128)}) custom-call(f32[6,16,16,128]{3,2,1,0:T(8,128)S(1)} %copy-done, f32[16,16,128]{2,1,0:T(8,128)S(1)} %get-tuple-element.18.inv_ref.own_inv_ref, f32[10,16,128]{2,1,0:T(8,128)S(1)} %collective-permute-done.zlo_ref, ...), custom_call_target="tpu_custom_call" | custom-call | flops 1000000 | bytes 1000000 | tf_op jit(solution)/shard_map/pallas_call | solution.py:58
  19.6 0.0 copy-start.5
  19.6 0.0 copy-start.4
  19.7 5.1 %collective-permute-start.2 = (f32[131,8,128]{2,1,0:T(8,128)}, f32[131,8,128]{2,1,0:T(8,128)S(1)}, u32[]{:S(2)}, u32[]{:S(2)}) collective-permute-start(f32[131,8,128]{2,1,0:T(8,128)} %get-tuple-element.22), channel_id=1, source_target_pairs={{0,16},{16,32},{32,48},{1,17},{17,33},{33,49},{2,18},{18,34},{34,5... | collective-permute-start | bytes 1609736 | tf_op jit(solution)/shard_map/ppermute | solution.py:363
  24.8 1.9 %collective-permute-start.3 = (f32[131,8,128]{2,1,0:T(8,128)S(1)}, f32[131,8,128]{2,1,0:T(8,128)S(1)}, u32[]{:S(2)}, u32[]{:S(2)}) collective-permute-start(f32[131,8,128]{2,1,0:T(8,128)S(1)} %get-tuple-element.23), channel_id=1, source_target_pairs={{16,0},{32,16},{48,32},{17,1},{33,17},{49,33},{18,2},{34,18},{50,3... | collective-permute-start | bytes 1609736 | tf_op jit(solution)/shard_map/ppermute | solution.py:363
  26.7 0.0 copy-done.5
  26.7 0.0 copy-done.4
  26.8 0.1 copy.10
  26.9 0.0 copy-start.3
  26.9 0.7 copy.12
  27.6 0.0 copy-done.3
  27.6 0.7 copy.11
  28.3 0.1 pad.3.clone
  28.4 1.0 maximum_maximum_fusion.data_ref
  29.4 0.8 shard_map.70
  30.2 1.2 collective-permute-done.2.ylo_ref
  31.3 4.1 %collective-permute-done.3.yhi_ref = f32[131,8,128]{2,1,0:T(8,128)S(1)} collective-permute-done((f32[131,8,128]{2,1,0:T(8,128)S(1)}, f32[131,8,128]{2,1,0:T(8,128)S(1)}, u32[]{:S(2)}, u32[]{:S(2)}) %collective-permute-start.3) | collective-permute-done | bytes 536608 | tf_op jit(solution)/shard_map/ppermute | solution.py:363
  35.4 0.0 copy-done.1
  35.4 3.9 %shard_map.71 = (f32[248,8,128]{2,1,0:T(8,128)S(1)}, f32[248,8,128]{2,1,0:T(8,128)S(1)}) custom-call(f32[6,16,16,128]{3,2,1,0:T(8,128)S(1)} %copy-done.1, f32[16,16,128]{2,1,0:T(8,128)S(1)} %get-tuple-element.18.inv_ref.own_inv_ref, f32[7,16,16,128]{3,2,1,0:T(8,128)S(1)} %get-tuple-element.21.h_ref, f32[131,8,128]{2,1,0:T(8,128)S(1)} %collective-permute-done.2.ylo_ref, ...), custom_call_target="tpu_custom_call" | custom-call | flops 1000000 | bytes 1000000 | tf_op jit(solution)/shard_map/pallas_call | solution.py:58
  39.4 4.4 %collective-permute-start.4 = (f32[248,8,128]{2,1,0:T(8,128)S(1)}, f32[248,8,128]{2,1,0:T(8,128)S(1)}, u32[]{:S(2)}, u32[]{:S(2)}) collective-permute-start(f32[248,8,128]{2,1,0:T(8,128)S(1)} %get-tuple-element.27), channel_id=1, source_target_pairs={{0,64},{64,128},{128,192},{192,256},{256,320},{320,384},{384,448},... | collective-permute-start | bytes 3047432 | tf_op jit(solution)/shard_map/ppermute | solution.py:363
  43.8 1.9 %collective-permute-start.5 = (f32[248,8,128]{2,1,0:T(8,128)S(1)}, f32[248,8,128]{2,1,0:T(8,128)S(1)}, u32[]{:S(2)}, u32[]{:S(2)}) collective-permute-start(f32[248,8,128]{2,1,0:T(8,128)S(1)} %get-tuple-element.28), channel_id=1, source_target_pairs={{64,0},{128,64},{192,128},{256,192},{320,256},{384,320},{448,384},... | collective-permute-start | bytes 3047432 | tf_op jit(solution)/shard_map/ppermute | solution.py:363
  45.7 0.1 copy.13
  45.8 29.6 %all_to_all.22 = f32[64,1,256]{2,1,0:T(1,128)S(1)} all-to-all(f32[64,1,256]{2,1,0:T(1,128)S(1)} %copy.13), channel_id=1, replica_groups=mesh['gx'=8,'gy'=4,'gz'=16] {'gy','gz'}, dimensions={0} | all-to-all | bytes 131072 | tf_op jit(solution)/shard_map/all_to_all | solution.py:387
  75.5 0.0 collective-permute-done.4.xlo_ref
  75.5 0.0 collective-permute-done.5.xhi_ref
  75.5 26.3 %shard_map.72 = (f32[6,16,16,128]{3,2,1,0:T(8,128)}, f32[64,128]{1,0:T(8,128)S(1)}) custom-call(f32[6,16,16,128]{3,2,1,0:T(8,128)S(1)} %copy-done.1, f32[16,16,128]{2,1,0:T(8,128)S(1)} %get-tuple-element.18.inv_ref.own_inv_ref, f32[7,16,16,128]{3,2,1,0:T(8,128)S(1)} %get-tuple-element.21.h_ref, f32[131,8,128]{2,1,0:T(8,128)S(1)} %collective-permute-done.2.ylo_ref, ...), custom_call_target="tpu_custom_call" | custom-call | flops 100000000 | bytes 1000000 | tf_op jit(solution)/shard_map/pallas_call | solution.py:58
  101.8 21.9 %all_to_all.23 = f32[64,1,128]{2,1,0:T(1,128)S(1)} all-to-all(f32[64,1,128]{2,1,0:T(1,128)S(1)} %bitcast.11), channel_id=1, replica_groups=mesh['gx'=8,'gy'=4,'gz'=16] {'gy','gz'}, dimensions={0} | all-to-all | bytes 65536 | tf_op jit(solution)/shard_map/all_to_all | solution.py:408
  123.7 1.0 shard_map.73
  (4 shorter events, 0.0 us)
Async XLA Ops:
  0.6 1.1 copy-start
  1.8 0.9 copy-start.2
  3.2 5.0 %collective-permute-start = (f32[10,16,128]{2,1,0:T(8,128)S(1)}, f32[10,16,128]{2,1,0:T(8,128)S(1)}, u32[]{:S(2)}, u32[]{:S(2)}) collective-permute-start(f32[10,16,128]{2,1,0:T(8,128)S(1)} %get-tuple-element.19), channel_id=1, source_target_pairs={{0,1},{1,2},{2,3},{3,4},{4,5},{5,6},{6,7},{7,8},{8,9},{9,10},{10,1... | collective-permute-start | bytes 245768 | tf_op jit(solution)/shard_map/ppermute | solution.py:363
  6.7 5.4 %collective-permute-start.1 = (f32[10,16,128]{2,1,0:T(8,128)S(1)}, f32[10,16,128]{2,1,0:T(8,128)S(1)}, u32[]{:S(2)}, u32[]{:S(2)}) collective-permute-start(f32[10,16,128]{2,1,0:T(8,128)S(1)} %get-tuple-element.20), channel_id=1, source_target_pairs={{1,0},{2,1},{3,2},{4,3},{5,4},{6,5},{7,6},{8,7},{9,8},{10,9},{11,1... | collective-permute-start | bytes 245768 | tf_op jit(solution)/shard_map/ppermute | solution.py:363
  12.1 23.3 %copy-start.1 = (f32[6,16,16,128]{3,2,1,0:T(8,128)S(1)}, f32[6,16,16,128]{3,2,1,0:T(8,128)}, u32[]{:S(2)}) copy-start(f32[6,16,16,128]{3,2,1,0:T(8,128)} %f_ref.7) | copy-start | bytes 2359300
  19.6 7.1 %copy-start.5 = (s32[128,1]{0,1:T(1,128)S(1)}, s32[128,1]{0,1:T(1,128)}, u32[]{:S(2)}) copy-start(s32[128,1]{0,1:T(1,128)} %param.7) | copy-start | bytes 1540
  19.6 7.1 %copy-start.4 = (s32[128,3]{0,1:T(4,128)S(1)}, s32[128,3]{0,1:T(4,128)}, u32[]{:S(2)}) copy-start(s32[128,3]{0,1:T(4,128)} %param.8) | copy-start | bytes 4612
  19.7 11.7 %collective-permute-start.2 = (f32[131,8,128]{2,1,0:T(8,128)}, f32[131,8,128]{2,1,0:T(8,128)S(1)}, u32[]{:S(2)}, u32[]{:S(2)}) collective-permute-start(f32[131,8,128]{2,1,0:T(8,128)} %get-tuple-element.22), channel_id=1, source_target_pairs={{0,16},{16,32},{32,48},{1,17},{17,33},{33,49},{2,18},{18,34},{34,5... | collective-permute-start | bytes 1609736 | tf_op jit(solution)/shard_map/ppermute | solution.py:363
  24.8 10.6 %collective-permute-start.3 = (f32[131,8,128]{2,1,0:T(8,128)S(1)}, f32[131,8,128]{2,1,0:T(8,128)S(1)}, u32[]{:S(2)}, u32[]{:S(2)}) collective-permute-start(f32[131,8,128]{2,1,0:T(8,128)S(1)} %get-tuple-element.23), channel_id=1, source_target_pairs={{16,0},{32,16},{48,32},{17,1},{33,17},{49,33},{18,2},{34,18},{50,3... | collective-permute-start | bytes 1609736 | tf_op jit(solution)/shard_map/ppermute | solution.py:363
  26.9 0.7 copy-start.3
  39.4 36.1 %collective-permute-start.4 = (f32[248,8,128]{2,1,0:T(8,128)S(1)}, f32[248,8,128]{2,1,0:T(8,128)S(1)}, u32[]{:S(2)}, u32[]{:S(2)}) collective-permute-start(f32[248,8,128]{2,1,0:T(8,128)S(1)} %get-tuple-element.27), channel_id=1, source_target_pairs={{0,64},{64,128},{128,192},{192,256},{256,320},{320,384},{384,448},... | collective-permute-start | bytes 3047432 | tf_op jit(solution)/shard_map/ppermute | solution.py:363
  43.8 31.6 %collective-permute-start.5 = (f32[248,8,128]{2,1,0:T(8,128)S(1)}, f32[248,8,128]{2,1,0:T(8,128)S(1)}, u32[]{:S(2)}, u32[]{:S(2)}) collective-permute-start(f32[248,8,128]{2,1,0:T(8,128)S(1)} %get-tuple-element.28), channel_id=1, source_target_pairs={{64,0},{128,64},{192,128},{256,192},{320,256},{384,320},{448,384},... | collective-permute-start | bytes 3047432 | tf_op jit(solution)/shard_map/ppermute | solution.py:363

commit v2 on v1

--- a/solution.py
+++ b/solution.py
@@ -10,29 +10,40 @@
 GX, GZ = 10, 10
 NF = 7
 PAIRS = NF * CX
-ZPER, YPER = 12, 6
-ZGROUPS = -(-PAIRS // ZPER)
-YGROUPS = -(-PAIRS // YPER)
+ZGROUPS = CX // 2 + 2
 XW = CX + 2 * GX
 STRIDE = 20
 EXACT = lax.Precision.HIGHEST
 F32 = jnp.float32
 
 
-def x_list():
-    entries = []
+def z_slot(c, x):
+    return (x // 2, (x % 2) * 6 + c) if c < 6 else (CX // 2 + x // 8, x % 8)
+
+
+def x_lists():
+    main = []
     for k in range(1, 5):
-        entries += [(k, c, t) for c in range(NF) for t in (0, 1, 2, 3)]
-    for k in range(5, 9):
-        entries += [(k, c, t) for c in range(NF) for t in (1, 2, 4)]
+        main += [(k, c, t) for c in range(NF) for t in (0, 1, 2, 3)]
+    for k in range(5, 7):
+        main += [(k, c, t) for c in range(NF) for t in (1, 2, 4)]
+    for k in range(7, 9):
+        main += [(k, c, t) for c in range(NF) for t in (1, 2)]
+        main += [(k, c, 4) for c in (0, 3)]
     for k in range(9, 11):
-        entries += [(k, c, t) for c in (1, 2, 4, 5) for t in (1, 2)]
-    return entries
-
-
-XLIST = x_list()
-XROWS = len(XLIST)
-XGROUPS = -(-XROWS // YPER)
+        main += [(k, c, t) for c in (1, 2, 4, 5) for t in (1, 2)]
+    ends = []
+    for q in range(5):
+        ends += [(q, t, e) for t in ((0, 1, 2, 3), (0, 1, 2, 3), (1, 2, 4), (1, 2, 4), (1, 2))[q] for e in (0, 1)]
+    ends += [(5, t, e) for t in (0, 1, 2, 3) for e in (0, 1)]
+    return main, ends
+
+
+XMAIN, XENDS = x_lists()
+XROWS = len(XMAIN)
+XEND = {key: XROWS + n for n, key in enumerate(XENDS)}
+XTOTAL = XROWS + len(XENDS)
+YTOTAL = PAIRS + 2 * ZGROUPS
 
 
 def roll(value, shift, axis):
@@ -69,72 +80,60 @@
 def pack_z(f_ref, e_ref, lo_ref, hi_ref, inv_ref):
     inv_ref[...] = 1.0 / e_ref[...]
     lane = lanes((CY, CZ))
+    sums = {}
+    for x in range(CX):
+        for c in range(NF):
+            g, s = z_slot(c, x)
+            tile = f_ref[c, x] if c < 6 else inv_ref[x]
+            for side, keep in ((0, lane < GZ), (1, lane >= CZ - GZ)):
+                part = roll(jnp.where(keep, tile, 0.0), GZ * (s + 1), 1)
+                sums[g, side] = sums[g, side] + part if (g, side) in sums else part
     for g in range(ZGROUPS):
-        lo = jnp.zeros((CY, CZ), F32)
-        hi = jnp.zeros((CY, CZ), F32)
-        for j in range(min(ZPER, PAIRS - g * ZPER)):
-            c, x = divmod(g * ZPER + j, CX)
-            tile = f_ref[c, x] if c < 6 else inv_ref[x]
-            lo = lo + roll(jnp.where(lane < GZ, tile, 0.0), GZ * j, 1)
-            hi = hi + roll(jnp.where(lane >= CZ - GZ, tile, 0.0), GZ * (j + 1), 1)
-        lo_ref[g] = lo
-        hi_ref[g] = hi
-
-
-def pack_y(f_ref, inv_ref, zlo_ref, zhi_ref, h_ref, lo_ref, hi_ref):
-    lane = lanes((CY, CZ))
-    for g in range(YGROUPS):
-        lo = jnp.zeros((8, CZ), F32)
-        hi = jnp.zeros((8, CZ), F32)
-        for j in range(min(YPER, PAIRS - g * YPER)):
-            p = g * YPER + j
+        lo_ref[g] = sums[g, 0]
+        hi_ref[g] = sums[g, 1]
+
+
+def pack_y(f_ref, inv_ref, zlo_ref, zhi_ref, lo_ref, hi_ref):
+    for out, start in ((lo_ref, 0), (hi_ref, 8)):
+        rows = pl.ds(start, 8)
+        for p in range(PAIRS):
             c, x = divmod(p, CX)
-            zg, zj = divmod(p, ZPER)
-            below = roll(zlo_ref[zg], CZ - GZ - GZ * zj, 1)
-            above = roll(zhi_ref[zg], -GZ * zj, 1)
-            ghost = jnp.where(lane >= CZ - GZ, below, jnp.where(lane < GZ, above, 0.0))
-            h_ref[c, x] = ghost
-            tile = f_ref[c, x] if c < 6 else inv_ref[x]
-            lo_ref[p] = tile[0:8]
-            hi_ref[p] = tile[8:16]
-            packed = roll(ghost, GZ + 2 * GZ * j, 1)
-            lo = lo + packed[0:8]
-            hi = hi + packed[8:16]
-        lo_ref[PAIRS + g] = lo
-        hi_ref[PAIRS + g] = hi
-
-
-def ring_lanes(packed, j, lane):
-    moved = roll(packed, -(GZ + 2 * GZ * j), 1)
+            out[p] = f_ref[c, x, rows] if c < 6 else inv_ref[x, rows]
+        for g in range(ZGROUPS):
+            out[PAIRS + g] = zlo_ref[g, rows]
+            out[PAIRS + ZGROUPS + g] = zhi_ref[g, rows]
+
+
+def z_ends(lo, hi, s, lane):
+    first = lane < GZ * (s + 1) if s < 11 else (lane >= GZ * s) & (lane < GZ * (s + 1))
+    moved = roll(jnp.where(first, lo, hi), CZ - GZ - GZ * s, 1)
     return jnp.where((lane < GZ) | (lane >= CZ - GZ), moved, 0.0)
 
 
-def pack_x(f_ref, inv_ref, h_ref, ylo_ref, yhi_ref, lo_ref, hi_ref):
-    lane = lanes((8, CZ))
+def pack_x(f_ref, inv_ref, zlo_ref, zhi_ref, ylo_ref, yhi_ref, lo_ref, hi_ref):
     row = rows_of((8, CZ))
 
-    def tile_of(c, x, t):
-        p = c * CX + x
+    def main_of(c, x, t):
+        if t == 4:
+            return jnp.where(row >= 4, main_of(c, x, 0), main_of(c, x, 3))
         if t in (1, 2):
-            own = pl.ds(8 * (t - 1), 8)
-            main = f_ref[c, x, own] if c < 6 else inv_ref[x, own]
-            return main, h_ref[c, x, own]
+            rows = pl.ds(8 * (t - 1), 8)
+            return f_ref[c, x, rows] if c < 6 else inv_ref[x, rows]
+        return (ylo_ref if t == 0 else yhi_ref)[c * CX + x]
+
+    def end_of(g, t, e):
         if t == 4:
-            a, b = tile_of(c, x, 0), tile_of(c, x, 3)
-            return jnp.where(row >= 4, a[0], b[0]), jnp.where(row >= 4, a[1], b[1])
-        ref = ylo_ref if t == 0 else yhi_ref
-        return ref[p], ring_lanes(ref[PAIRS + p // YPER], p % YPER, lane)
-
-    for ref, side in ((lo_ref, 0), (hi_ref, 1)):
-        for g in range(XGROUPS):
-            total = jnp.zeros((8, CZ), F32)
-            for j in range(min(YPER, XROWS - g * YPER)):
-                n = g * YPER + j
-                k, c, t = XLIST[n]
-                main, ghost = tile_of(c, k - 1 if side == 0 else CX - k, t)
-                ref[n] = main
-                total = total + roll(ghost, GZ + 2 * GZ * j, 1)
-            ref[XROWS + g] = total
+            return jnp.where(row >= 4, end_of(g, 0, e), end_of(g, 3, e))
+        if t in (1, 2):
+            return (zhi_ref if e else zlo_ref)[g, pl.ds(8 * (t - 1), 8)]
+        return (ylo_ref if t == 0 else yhi_ref)[PAIRS + e * ZGROUPS + g]
+
+    for out, side in ((lo_ref, 0), (hi_ref, 1)):
+        for n, (k, c, t) in enumerate(XMAIN):
+            out[n] = main_of(c, CX - k if side else k - 1, t)
+        for (q, t, e), n in XEND.items():
+            g = CX // 2 + side if q == 5 else (CX // 2 - 1 - q if side else q)
+            out[n] = end_of(g, t, e)
 
 
 def along_y(tiles, t, row):
@@ -150,7 +149,7 @@
     return up(1) - down(1), down(2) - up(2)
 
 
-def taylor(source, inv_ref, x, tiles, scale, put):
+def taylor(source, inv_ref, x, tiles, scale, put, comps=(0, 1, 2, 3, 4, 5)):
     row = rows_of((8, CZ))
     lane = lanes((8, CZ))
     for t in tiles:
@@ -166,18 +165,21 @@
             def dz(c):
                 return along_z(source[half, c, x, t], source[1 - half, c, x, t], lane)
 
-            def rate(plus, minus):
-                return (plus[1] - minus[1]) + 8.0 * (plus[0] - minus[0])
-
+            rates = (
+                lambda: (dy(5), dz(4)),
+                lambda: (dz(3), dx(5)),
+                lambda: (dx(4), dy(3)),
+                lambda: (dz(1), dy(2)),
+                lambda: (dx(2), dz(0)),
+                lambda: (dy(0), dx(1)),
+            )
             inv = inv_ref[half, 6, x, t]
             electric = inv * scale
             magnetic = jnp.where(inv > 0.0, scale, 0.0)
-            put(half, 0, t, electric * rate(dy(5), dz(4)))
-            put(half, 1, t, electric * rate(dz(3), dx(5)))
-            put(half, 2, t, electric * rate(dx(4), dy(3)))
-            put(half, 3, t, magnetic * rate(dz(1), dy(2)))
-            put(half, 4, t, magnetic * rate(dx(2), dz(0)))
-            put(half, 5, t, magnetic * rate(dy(0), dx(1)))
+            for c in comps:
+                plus, minus = rates[c]()
+                rate = (plus[1] - minus[1]) + 8.0 * (plus[0] - minus[0])
+                put(half, c, t, (electric if c < 3 else magnetic) * rate)
 
 
 def dot(a, b, da=1, db=0):
@@ -190,7 +192,7 @@
 
 
 def compute(
-    f_ref, own_inv_ref, h_ref, ylo_ref, yhi_ref, xlo_ref, xhi_ref, req_ref,
+    f_ref, own_inv_ref, zlo_ref, zhi_ref, ylo_ref, yhi_ref, xlo_ref, xhi_ref, req_ref,
     new_ref, ans_ref,
     full, t1, t2, t3, acc, words, wz, wxy, spill, parts,
 ):
@@ -199,40 +201,67 @@
     zero = jnp.zeros((8, CZ), F32)
     for p in range(PAIRS):
         c, x = divmod(p, CX)
+        g, s = z_slot(c, x)
         for t in (1, 2):
             own = pl.ds(8 * (t - 1), 8)
             full[0, c, GX + x, t] = f_ref[c, x, own] if c < 6 else own_inv_ref[x, own]
-            full[1, c, GX + x, t] = h_ref[c, x, own]
+            full[1, c, GX + x, t] = z_ends(zlo_ref[g, own], zhi_ref[g, own], s, lane)
         for ref, t in ((ylo_ref, 0), (yhi_ref, 3)):
             full[0, c, GX + x, t] = ref[p]
-            full[1, c, GX + x, t] = ring_lanes(ref[PAIRS + p // YPER], p % YPER, lane)
+            full[1, c, GX + x, t] = z_ends(ref[PAIRS + g], ref[PAIRS + ZGROUPS + g], s, lane)
     for side in (0, 1):
-        ref = xlo_ref if side == 0 else xhi_ref
-        for n, (k, c, t) in enumerate(XLIST):
-            x = GX - k if side == 0 else GX + CX + k - 1
-            pair = (ref[n], ring_lanes(ref[XROWS + n // YPER], n % YPER, lane))
-            for half in (0, 1):
-                if t == 4:
-                    full[half, c, x, 0] = jnp.where(row >= 4, pair[half], 0.0)
-                    full[half, c, x, 3] = jnp.where(row >= 4, 0.0, pair[half])
-                else:
-                    full[half, c, x, t] = pair[half]
-        for k in (9, 10):
-            x = GX - k if side == 0 else GX + CX + k - 1
-            for c in (1, 2, 4, 5):
+        ref = xhi_ref if side == 0 else xlo_ref
+        where_main = {key: n for n, key in enumerate(XMAIN)}
+        for k in range(1, GX + 1):
+            x = GX + CX + k - 1 if side == 0 else GX - k
+            for c in range(NF):
+                if k > 8 and c in (0, 3, 6):
+                    continue
+                g, s = z_slot(c, k - 1 if side == 0 else CX - k)
+                q = 5 if c == 6 else (k - 1) // 2
+                done = set()
+                for t in (0, 1, 2, 3, 4):
+                    pair = [None, None]
+                    if (k, c, t) in where_main:
+                        pair[0] = ref[where_main[k, c, t]]
+                    if (q, t, 0) in XEND:
+                        pair[1] = z_ends(ref[XEND[q, t, 0]], ref[XEND[q, t, 1]], s, lane)
+                    for half in (0, 1):
+                        if pair[half] is None:
+                            continue
+                        if t == 4:
+                            full[half, c, x, 0] = jnp.where(row >= 4, pair[half], 0.0)
+                            full[half, c, x, 3] = jnp.where(row >= 4, 0.0, pair[half])
+                            done |= {(half, 0), (half, 3)}
+                        else:
+                            full[half, c, x, t] = pair[half]
+                            done.add((half, t))
                 for half in (0, 1):
-                    full[half, c, x, 0] = zero
-                    full[half, c, x, 3] = zero
+                    for t in (0, 3):
+                        if (half, t) not in done:
+                            full[half, c, x, t] = zero
 
     for power, source, target in ((1, full, t1), (2, t1, t2), (3, t2, t3)):
-        def body(x, carry, source=source, target=target, power=power):
+        scale = STEP / power / 12.0
+
+        def body(x, carry, source=source, target=target, scale=scale):
             def put(half, c, t, value):
                 target[half, c, x, t] = value
 
-            taylor(source, full, x, (0, 1, 2, 3), STEP / power / 12.0, put)
+            taylor(source, full, x, (0, 1, 2, 3), scale, put)
             return carry
 
-        lax.fori_loop(2 * power, XW - 2 * power, body, 0)
+        def edge(i, carry, source=source, target=target, scale=scale, power=power):
+            x = jnp.where(i < 2, 2 * power + i, XW - 2 * power - 4 + i)
+
+            def put(half, c, t, value):
+                target[half, c, x, t] = value
+
+            taylor(source, full, x, (1, 2), scale, put, (1, 2, 4, 5))
+            return carry
+
+        lax.fori_loop(0, 4, edge, 0, unroll=2)
+        lax.fori_loop(2 * power + 2, XW - 2 * power - 2, body, 0, unroll=2)
 
     def last(x, carry):
         def put(half, c, t, value):
@@ -244,7 +273,7 @@
         taylor(t3, full, x, (1, 2), STEP / 4 / 12.0, put)
         return carry
 
-    lax.fori_loop(8, XW - 8, last, 0)
+    lax.fori_loop(8, XW - 8, last, 0, unroll=2)
     for c in range(6):
         for t in (0, 1):
             new_ref[c, :, pl.ds(8 * t, 8), :] = acc[0, c, 2:18, t]
@@ -376,11 +405,11 @@
     zshape = (ZGROUPS, CY, CZ)
     zlo, zhi, inv = call(pack_z, [zshape, zshape, (CX, CY, CZ)], (fields, permittivity), 16)
     zlo, zhi = shift_both(zlo, zhi, "gz")
-    yshape = (PAIRS + YGROUPS, 8, CZ)
-    ghosts, ylo, yhi = call(pack_y, [(NF, CX, CY, CZ), yshape, yshape], (fields, inv, zlo, zhi), 16)
+    yshape = (YTOTAL, 8, CZ)
+    ylo, yhi = call(pack_y, [yshape, yshape], (fields, inv, zlo, zhi), 8)
     ylo, yhi = shift_both(ylo, yhi, "gy")
-    xshape = (XROWS + XGROUPS, 8, CZ)
-    xlo, xhi = call(pack_x, [xshape, xshape], (fields, inv, ghosts, ylo, yhi), 20)
+    xshape = (XTOTAL, 8, CZ)
+    xlo, xhi = call(pack_x, [xshape, xshape], (fields, inv, zlo, zhi, ylo, yhi), 8)
     send, pick, rank = call(requests, [(64, 256), (3, 64, 128), (8, 128)], (data,), 8)
     send, xlo, xhi = lax.optimization_barrier((send, xlo, xhi))
     xlo, xhi = shift_both(xlo, xhi, "gx")
@@ -389,8 +418,8 @@
     new_fields, answers = call(
         compute,
         [(6, CX, CY, CZ), (64, 128)],
-        (fields, inv, ghosts, ylo, yhi, xlo, xhi, req),
-        48,
+        (fields, inv, zlo, zhi, ylo, yhi, xlo, xhi, req),
+        42,
         scratch=[
             pltpu.VMEM((2, NF, XW, 4, 8, CZ), F32),
             big,

time: 125 us -> 108 us (0.86)
  Pallas kernels: 40 us -> 24 us
  waiting for transfers between devices: 9.33 us -> 11.2 us
    pallas_call x6, Pallas kernels: 40 us -> 24 us  [call(): pl.pallas_call(body, out_shape=[jax.ShapeDtypeStruct(s, F32) for s in out...]
    ppermute x3, waiting for transfers between devices: 1.34 us -> 2.6 us  [shift_both(): lax.ppermute(high_edge, axis, up)]
  transfers between devices with their start and end apart: 6 -> 6, of which waited for: 4 -> 4; matrix products, arithmetic and copies ran while one was open for 2% -> 1% of each run, Pallas kernels for 1% -> 1%
where the time goes in v2:
time: 108 us; the launch traced here: 107 us
  blocking collectives  50.3 us (47%)
  Pallas kernels  24 us (22%)
  starting transfers between devices  18 us (17%)
  waiting for transfers between devices  11.2 us (10%)
  local copies, waits for them, and re-layouts  3.12 us (3%)
    all_to_all x1, blocking collectives, local(): req = lax.all_to_all(send, ('gy', 'gz'), 0, 0, tiled=True)  29.6 us
    pallas_call x6, Pallas kernels, call(): pl.pallas_call(body, out_shape=[jax.ShapeDtypeStruct(s, F32) for s in out...  24 us
    all_to_all x1, blocking collectives, local(): answers = lax.all_to_all(answers, ('gy', 'gz'), 0, 0, tiled=True)  20.6 us
    ppermute x3, starting transfers between devices, shift_both(): lax.ppermute(high_edge, axis, up)  12.8 us
    ppermute x3, waiting for transfers between devices, shift_both(): lax.ppermute(low_edge, axis, down)  8.6 us
    ppermute x3, starting transfers between devices, shift_both(): lax.ppermute(low_edge, axis, down)  5.13 us
    unnamed x14, local copies, waits for them, and re-layouts  2.74 us
    ppermute x3, waiting for transfers between devices, shift_both(): lax.ppermute(high_edge, axis, up)  2.6 us
  transfers between devices with their start and end apart: 6, of which 4 were waited for; matrix products, arithmetic and copies ran while one was open for 1% of the time, Pallas kernels for 1%

profile of v2, /device:TPU:7, one launch (start us, length us, event | category | flops | bytes accessed | tf_op | source)
XLA Modules:
  0.0 107.4 jit_solution(2639065556316501371)
XLA Ops:
  0.6 0.0 copy-start
  0.6 1.1 %copy-done = f32[6,16,16,128]{3,2,1,0:T(8,128)S(1)} copy-done((f32[6,16,16,128]{3,2,1,0:T(8,128)S(1)}, f32[6,16,16,128]{3,2,1,0:T(8,128)}, u32[]{:S(2)}) %copy-start) | copy-done | bytes 786456
  1.8 0.0 copy-start.2
  1.8 0.9 copy-done.2
  2.7 0.5 shard_map.68
  3.2 3.5 %collective-permute-start = (f32[10,16,128]{2,1,0:T(8,128)S(1)}, f32[10,16,128]{2,1,0:T(8,128)S(1)}, u32[]{:S(2)}, u32[]{:S(2)}) collective-permute-start(f32[10,16,128]{2,1,0:T(8,128)S(1)} %get-tuple-element.18), channel_id=1, source_target_pairs={{0,1},{1,2},{2,3},{3,4},{4,5},{5,6},{6,7},{7,8},{8,9},{9,10},{10,1... | collective-permute-start | bytes 245768 | tf_op jit(solution)/shard_map/ppermute | solution.py:392
  6.8 1.3 %collective-permute-start.1 = (f32[10,16,128]{2,1,0:T(8,128)S(1)}, f32[10,16,128]{2,1,0:T(8,128)S(1)}, u32[]{:S(2)}, u32[]{:S(2)}) collective-permute-start(f32[10,16,128]{2,1,0:T(8,128)S(1)} %get-tuple-element.19), channel_id=1, source_target_pairs={{1,0},{2,1},{3,2},{4,3},{5,4},{6,5},{7,6},{8,7},{9,8},{10,9},{11,1... | collective-permute-start | bytes 245768 | tf_op jit(solution)/shard_map/ppermute | solution.py:392
  8.1 0.2 collective-permute-done.zlo_ref
  8.2 3.9 %collective-permute-done.1.zhi_ref = f32[10,16,128]{2,1,0:T(8,128)S(1)} collective-permute-done((f32[10,16,128]{2,1,0:T(8,128)S(1)}, f32[10,16,128]{2,1,0:T(8,128)S(1)}, u32[]{:S(2)}, u32[]{:S(2)}) %collective-permute-start.1) | collective-permute-done | bytes 81952 | tf_op jit(solution)/shard_map/ppermute | solution.py:392
  12.1 0.0 copy-start.1
  12.1 0.1 shard_map.69
  12.2 0.0 copy-start.5
  12.2 0.0 copy-start.4
  12.2 5.1 %collective-permute-start.2 = (f32[132,8,128]{2,1,0:T(8,128)S(1)}, f32[132,8,128]{2,1,0:T(8,128)S(1)}, u32[]{:S(2)}, u32[]{:S(2)}) collective-permute-start(f32[132,8,128]{2,1,0:T(8,128)S(1)} %get-tuple-element.20), channel_id=1, source_target_pairs={{0,16},{16,32},{32,48},{1,17},{17,33},{33,49},{2,18},{18,34},{34,5... | collective-permute-start | bytes 1622024 | tf_op jit(solution)/shard_map/ppermute | solution.py:392
  17.4 1.9 %collective-permute-start.3 = (f32[132,8,128]{2,1,0:T(8,128)S(1)}, f32[132,8,128]{2,1,0:T(8,128)S(1)}, u32[]{:S(2)}, u32[]{:S(2)}) collective-permute-start(f32[132,8,128]{2,1,0:T(8,128)S(1)} %get-tuple-element.21), channel_id=1, source_target_pairs={{16,0},{32,16},{48,32},{17,1},{33,17},{49,33},{18,2},{34,18},{50,3... | collective-permute-start | bytes 1622024 | tf_op jit(solution)/shard_map/ppermute | solution.py:392
  19.3 0.0 copy-done.5
  19.3 0.0 copy-done.4
  19.4 0.1 copy.10
  19.5 0.0 copy-start.3
  19.5 0.1 copy.12
  19.6 0.6 copy-done.3
  20.2 0.1 copy.11
  20.3 0.1 pad.3.clone
  20.4 0.1 maximum_maximum_fusion.data_ref
  20.5 0.8 shard_map.70
  21.2 2.4 %collective-permute-done.2.ylo_ref = f32[132,8,128]{2,1,0:T(8,128)S(1)} collective-permute-done((f32[132,8,128]{2,1,0:T(8,128)S(1)}, f32[132,8,128]{2,1,0:T(8,128)S(1)}, u32[]{:S(2)}, u32[]{:S(2)}) %collective-permute-start.2) | collective-permute-done | bytes 540704 | tf_op jit(solution)/shard_map/ppermute | solution.py:392
  23.7 4.7 %collective-permute-done.3.yhi_ref = f32[132,8,128]{2,1,0:T(8,128)S(1)} collective-permute-done((f32[132,8,128]{2,1,0:T(8,128)S(1)}, f32[132,8,128]{2,1,0:T(8,128)S(1)}, u32[]{:S(2)}, u32[]{:S(2)}) %collective-permute-start.3) | collective-permute-done | bytes 540704 | tf_op jit(solution)/shard_map/ppermute | solution.py:392
  28.4 0.0 copy-done.1
  28.4 0.1 shard_map.71
  28.5 4.1 %collective-permute-start.4 = (f32[242,8,128]{2,1,0:T(8,128)S(1)}, f32[242,8,128]{2,1,0:T(8,128)S(1)}, u32[]{:S(2)}, u32[]{:S(2)}) collective-permute-start(f32[242,8,128]{2,1,0:T(8,128)S(1)} %get-tuple-element.25), channel_id=1, source_target_pairs={{0,64},{64,128},{128,192},{192,256},{256,320},{320,384},{384,448},... | collective-permute-start | bytes 2973704 | tf_op jit(solution)/shard_map/ppermute | solution.py:392
  32.7 1.9 %collective-permute-start.5 = (f32[242,8,128]{2,1,0:T(8,128)S(1)}, f32[242,8,128]{2,1,0:T(8,128)S(1)}, u32[]{:S(2)}, u32[]{:S(2)}) collective-permute-start(f32[242,8,128]{2,1,0:T(8,128)S(1)} %get-tuple-element.26), channel_id=1, source_target_pairs={{64,0},{128,64},{192,128},{256,192},{320,256},{384,320},{448,384},... | collective-permute-start | bytes 2973704 | tf_op jit(solution)/shard_map/ppermute | solution.py:392
  34.6 0.1 copy.13
  34.7 29.6 %all_to_all.22 = f32[64,1,256]{2,1,0:T(1,128)S(1)} all-to-all(f32[64,1,256]{2,1,0:T(1,128)S(1)} %copy.13), channel_id=1, replica_groups=mesh['gx'=8,'gy'=4,'gz'=16] {'gy','gz'}, dimensions={0} | all-to-all | bytes 131072 | tf_op jit(solution)/shard_map/all_to_all | solution.py:416
  64.3 0.0 collective-permute-done.4.xlo_ref
  64.3 0.0 collective-permute-done.5.xhi_ref
  64.3 21.5 %shard_map.72 = (f32[6,16,16,128]{3,2,1,0:T(8,128)}, f32[64,128]{1,0:T(8,128)S(1)}) custom-call(f32[6,16,16,128]{3,2,1,0:T(8,128)S(1)} %copy-done.1, f32[16,16,128]{2,1,0:T(8,128)S(1)} %get-tuple-element.17.inv_ref.own_inv_ref, f32[10,16,128]{2,1,0:T(8,128)S(1)} %collective-permute-done.zlo_ref, f32[10,16,128]{2,1,0:T(8,128)S(1)} %collective-permute-done.1.zhi_ref, ...), custom_call_target="tpu_custom_call" | custom-call | flops 100000000 | bytes 1000000 | tf_op jit(solution)/shard_map/pallas_call | solution.py:69
  85.8 20.6 %all_to_all.23 = f32[64,1,128]{2,1,0:T(1,128)S(1)} all-to-all(f32[64,1,128]{2,1,0:T(1,128)S(1)} %bitcast.11), channel_id=1, replica_groups=mesh['gx'=8,'gy'=4,'gz'=16] {'gy','gz'}, dimensions={0} | all-to-all | bytes 65536 | tf_op jit(solution)/shard_map/all_to_all | solution.py:437
  106.5 1.0 shard_map.73
  (4 shorter events, 0.0 us)
Async XLA Ops:
  0.6 1.1 %copy-start = (f32[6,16,16,128]{3,2,1,0:T(8,128)S(1)}, f32[6,16,16,128]{3,2,1,0:T(8,128)}, u32[]{:S(2)}) copy-start(f32[6,16,16,128]{3,2,1,0:T(8,128)} %f_ref.7) | copy-start | bytes 2359300
  1.8 0.9 copy-start.2
  3.2 5.0 %collective-permute-start = (f32[10,16,128]{2,1,0:T(8,128)S(1)}, f32[10,16,128]{2,1,0:T(8,128)S(1)}, u32[]{:S(2)}, u32[]{:S(2)}) collective-permute-start(f32[10,16,128]{2,1,0:T(8,128)S(1)} %get-tuple-element.18), channel_id=1, source_target_pairs={{0,1},{1,2},{2,3},{3,4},{4,5},{5,6},{6,7},{7,8},{8,9},{9,10},{10,1... | collective-permute-start | bytes 245768 | tf_op jit(solution)/shard_map/ppermute | solution.py:392
  6.8 5.4 %collective-permute-start.1 = (f32[10,16,128]{2,1,0:T(8,128)S(1)}, f32[10,16,128]{2,1,0:T(8,128)S(1)}, u32[]{:S(2)}, u32[]{:S(2)}) collective-permute-start(f32[10,16,128]{2,1,0:T(8,128)S(1)} %get-tuple-element.19), channel_id=1, source_target_pairs={{1,0},{2,1},{3,2},{4,3},{5,4},{6,5},{7,6},{8,7},{9,8},{10,9},{11,1... | collective-permute-start | bytes 245768 | tf_op jit(solution)/shard_map/ppermute | solution.py:392
  12.1 16.2 %copy-start.1 = (f32[6,16,16,128]{3,2,1,0:T(8,128)S(1)}, f32[6,16,16,128]{3,2,1,0:T(8,128)}, u32[]{:S(2)}) copy-start(f32[6,16,16,128]{3,2,1,0:T(8,128)} %f_ref.7) | copy-start | bytes 2359300
  12.2 7.1 %copy-start.5 = (s32[128,1]{0,1:T(1,128)S(1)}, s32[128,1]{0,1:T(1,128)}, u32[]{:S(2)}) copy-start(s32[128,1]{0,1:T(1,128)} %param.7) | copy-start | bytes 1540
  12.2 7.1 %copy-start.4 = (s32[128,3]{0,1:T(4,128)S(1)}, s32[128,3]{0,1:T(4,128)}, u32[]{:S(2)}) copy-start(s32[128,3]{0,1:T(4,128)} %param.8) | copy-start | bytes 4612
  12.2 11.4 %collective-permute-start.2 = (f32[132,8,128]{2,1,0:T(8,128)S(1)}, f32[132,8,128]{2,1,0:T(8,128)S(1)}, u32[]{:S(2)}, u32[]{:S(2)}) collective-permute-start(f32[132,8,128]{2,1,0:T(8,128)S(1)} %get-tuple-element.20), channel_id=1, source_target_pairs={{0,16},{16,32},{32,48},{1,17},{17,33},{33,49},{2,18},{18,34},{34,5... | collective-permute-start | bytes 1622024 | tf_op jit(solution)/shard_map/ppermute | solution.py:392
  17.4 11.0 %collective-permute-start.3 = (f32[132,8,128]{2,1,0:T(8,128)S(1)}, f32[132,8,128]{2,1,0:T(8,128)S(1)}, u32[]{:S(2)}, u32[]{:S(2)}) collective-permute-start(f32[132,8,128]{2,1,0:T(8,128)S(1)} %get-tuple-element.21), channel_id=1, source_target_pairs={{16,0},{32,16},{48,32},{17,1},{33,17},{49,33},{18,2},{34,18},{50,3... | collective-permute-start | bytes 1622024 | tf_op jit(solution)/shard_map/ppermute | solution.py:392
  19.5 0.7 copy-start.3
  28.5 35.8 %collective-permute-start.4 = (f32[242,8,128]{2,1,0:T(8,128)S(1)}, f32[242,8,128]{2,1,0:T(8,128)S(1)}, u32[]{:S(2)}, u32[]{:S(2)}) collective-permute-start(f32[242,8,128]{2,1,0:T(8,128)S(1)} %get-tuple-element.25), channel_id=1, source_target_pairs={{0,64},{64,128},{128,192},{192,256},{256,320},{320,384},{384,448},... | collective-permute-start | bytes 2973704 | tf_op jit(solution)/shard_map/ppermute | solution.py:392
  32.7 31.6 %collective-permute-start.5 = (f32[242,8,128]{2,1,0:T(8,128)S(1)}, f32[242,8,128]{2,1,0:T(8,128)S(1)}, u32[]{:S(2)}, u32[]{:S(2)}) collective-permute-start(f32[242,8,128]{2,1,0:T(8,128)S(1)} %get-tuple-element.26), channel_id=1, source_target_pairs={{64,0},{128,64},{192,128},{256,192},{320,256},{384,320},{448,384},... | collective-permute-start | bytes 2973704 | tf_op jit(solution)/shard_map/ppermute | solution.py:392

commit v3 on v2

--- a/solution.py
+++ b/solution.py
@@ -64,12 +64,12 @@
     return [pl.BlockSpec(memory_space=pltpu.VMEM)] * count
 
 
-def call(body, outs, ins, limit, scratch=(), flops=1000000):
+def call(body, outs, ins, limit, scratch=(), flops=1000000, space=pltpu.VMEM):
     many = isinstance(outs, list)
     return pl.pallas_call(
         body,
         out_shape=[jax.ShapeDtypeStruct(s, F32) for s in outs] if many else jax.ShapeDtypeStruct(outs, F32),
-        in_specs=vmem(len(ins)),
+        in_specs=[pl.BlockSpec(memory_space=space)] * len(ins),
         out_specs=vmem(len(outs)) if many else vmem(1)[0],
         scratch_shapes=list(scratch),
         compiler_params=pltpu.CompilerParams(vmem_limit_bytes=limit * 1048576),
@@ -77,17 +77,31 @@
     )(*ins)
 
 
-def pack_z(f_ref, e_ref, lo_ref, hi_ref, inv_ref):
-    inv_ref[...] = 1.0 / e_ref[...]
+def pack_z(f_hbm, e_hbm, lo_ref, hi_ref, inv_ref, f_ref, e_ref, sems):
+    copies = [pltpu.make_async_copy(e_hbm, e_ref, sems.at[0])]
+    for g in range(4):
+        part = pl.ds(4 * g, 4)
+        copies.append(pltpu.make_async_copy(f_hbm.at[:, part], f_ref.at[:, part], sems.at[g + 1]))
+    for copy in copies:
+        copy.start()
     lane = lanes((CY, CZ))
     sums = {}
+
+    def add(c, x, tile):
+        g, s = z_slot(c, x)
+        for side, keep in ((0, lane < GZ), (1, lane >= CZ - GZ)):
+            part = roll(jnp.where(keep, tile, 0.0), GZ * (s + 1), 1)
+            sums[g, side] = sums[g, side] + part if (g, side) in sums else part
+
+    copies[0].wait()
+    inv_ref[...] = 1.0 / e_ref[...]
     for x in range(CX):
-        for c in range(NF):
-            g, s = z_slot(c, x)
-            tile = f_ref[c, x] if c < 6 else inv_ref[x]
-            for side, keep in ((0, lane < GZ), (1, lane >= CZ - GZ)):
-                part = roll(jnp.where(keep, tile, 0.0), GZ * (s + 1), 1)
-                sums[g, side] = sums[g, side] + part if (g, side) in sums else part
+        add(6, x, inv_ref[x])
+    for g in range(4):
+        copies[g + 1].wait()
+        for x in range(4 * g, 4 * g + 4):
+            for c in range(6):
+                add(c, x, f_ref[c, x])
     for g in range(ZGROUPS):
         lo_ref[g] = sums[g, 0]
         hi_ref[g] = sums[g, 1]
@@ -136,50 +150,72 @@
             out[n] = end_of(g, t, e)
 
 
-def along_y(tiles, t, row):
-    before, here, after = tiles[(t - 1) % 4], tiles[t], tiles[(t + 1) % 4]
-    down = lambda d: roll(jnp.where(row >= 8 - d, before, here), d, 0)
-    up = lambda d: roll(jnp.where(row < d, after, here), -d, 0)
-    return up(1) - down(1), down(2) - up(2)
-
-
-def along_z(here, other, lane):
-    down = lambda d: roll(jnp.where(lane >= CZ - d, other, here), d, 1)
-    up = lambda d: roll(jnp.where(lane < d, other, here), -d, 1)
-    return up(1) - down(1), down(2) - up(2)
-
-
-def taylor(source, inv_ref, x, tiles, scale, put, comps=(0, 1, 2, 3, 4, 5)):
+def taylor(source, inv_ref, band, x, tiles, scale, put, comps=(0, 1, 2, 3, 4, 5)):
     row = rows_of((8, CZ))
-    lane = lanes((8, CZ))
-    for t in tiles:
+    def load(half, c, t, d=0):
+        return source[half, c, x + d, t % 4]
+
+    def dx(c):
+        return {
+            (half, t): (
+                load(half, c, t, 1) - load(half, c, t, -1),
+                load(half, c, t, 2) - load(half, c, t, -2),
+            )
+            for half in (0, 1)
+            for t in tiles
+        }
+
+    def dy(c):
+        out = {}
         for half in (0, 1):
-            def dx(c):
-                at = lambda d: source[half, c, x + d, t]
-                return at(1) - at(-1), at(-2) - at(2)
-
-            def dy(c):
-                near = {u % 4: source[half, c, x, u % 4] for u in (t - 1, t, t + 1)}
-                return along_y(near, t, row)
-
-            def dz(c):
-                return along_z(source[half, c, x, t], source[1 - half, c, x, t], lane)
-
-            rates = (
-                lambda: (dy(5), dz(4)),
-                lambda: (dz(3), dx(5)),
-                lambda: (dx(4), dy(3)),
-                lambda: (dz(1), dy(2)),
-                lambda: (dx(2), dz(0)),
-                lambda: (dy(0), dx(1)),
-            )
+            u = {}
+            for t in sorted({v % 4 for t in tiles for v in (t, t + 1)}):
+                here = load(half, c, t)
+                u[t] = here - roll(jnp.where(row >= 6, load(half, c, t - 1), here), 2, 0)
+            for t in tiles:
+                low, high = u[t], u[(t + 1) % 4]
+                near = roll(jnp.where(row < 1, high, low), -1, 0)
+                out[half, t] = (near, roll(jnp.where(row < 2, high, low), -2, 0) + low)
+        return out
+
+    def all_dz(fields):
+        block = jnp.concatenate(
+            [jnp.concatenate([load(0, c, t), load(1, c, t)], axis=1) for c in fields for t in tiles], axis=0
+        )
+        high = block.astype(jnp.bfloat16)
+        rest = block - high.astype(F32)
+        middle = rest.astype(jnp.bfloat16)
+        low = (rest - middle.astype(F32)).astype(jnp.bfloat16)
+        total = sum(
+            jnp.dot(part, band[...], preferred_element_type=F32) for part in (low, middle, high)
+        )
+        out = {}
+        for i, c in enumerate(fields):
+            for j, t in enumerate(tiles):
+                start = 8 * (i * len(tiles) + j)
+                for half in (0, 1):
+                    out[c, half, t] = total[start:start + 8, 128 * half:128 * half + 128]
+        return out
+
+    pairs = ((dy, 5, 4, 0), (None, 3, 5, dx), (dx, 4, 3, dy), (None, 1, 2, dy), (dx, 2, 0, 0), (dy, 0, 1, dx))
+    along_z = all_dz([c for c in (4, 3, 1, 0) if {4: 0, 3: 1, 1: 3, 0: 4}[c] in comps])
+    factors = {}
+    for half in (0, 1):
+        for t in tiles:
             inv = inv_ref[half, 6, x, t]
-            electric = inv * scale
-            magnetic = jnp.where(inv > 0.0, scale, 0.0)
-            for c in comps:
-                plus, minus = rates[c]()
-                rate = (plus[1] - minus[1]) + 8.0 * (plus[0] - minus[0])
-                put(half, c, t, (electric if c < 3 else magnetic) * rate)
+            factors[half, t] = (inv * scale, jnp.where(inv > 0.0, scale, 0.0))
+    for c in comps:
+        first, c1, c2, second = pairs[c]
+        plus = first(c1) if first else None
+        minus = second(c2) if second else None
+        for key in factors:
+            if plus and minus:
+                rate = 8.0 * (plus[key][0] - minus[key][0]) - (plus[key][1] - minus[key][1])
+            elif plus:
+                rate = 8.0 * plus[key][0] - plus[key][1] - along_z[(c2,) + key]
+            else:
+                rate = along_z[(c1,) + key] - (8.0 * minus[key][0] - minus[key][1])
+            put(key[0], c, key[1], factors[key][c // 3] * rate)
 
 
 def dot(a, b, da=1, db=0):
@@ -194,7 +230,7 @@
 def compute(
     f_ref, own_inv_ref, zlo_ref, zhi_ref, ylo_ref, yhi_ref, xlo_ref, xhi_ref, req_ref,
     new_ref, ans_ref,
-    full, t1, t2, t3, acc, words, wz, wxy, spill, parts,
+    full, t1, t2, t3, acc, words, wz, wxy, spill, edge_rows, parts, band,
 ):
     lane = lanes((8, CZ))
     row = rows_of((8, CZ))
@@ -241,6 +277,10 @@
                         if (half, t) not in done:
                             full[half, c, x, t] = zero
 
+    ring = (rows_of((256, 256)) - lanes((256, 256)) + 256) % 256
+    one = lambda d: (ring == d % 256).astype(F32)
+    band[...] = (8.0 * (one(1) - one(-1)) + one(-2) - one(2)).astype(jnp.bfloat16)
+
     for power, source, target in ((1, full, t1), (2, t1, t2), (3, t2, t3)):
         scale = STEP / power / 12.0
 
@@ -248,7 +288,7 @@
             def put(half, c, t, value):
                 target[half, c, x, t] = value
 
-            taylor(source, full, x, (0, 1, 2, 3), scale, put)
+            taylor(source, full, band, x, (0, 1, 2, 3), scale, put)
             return carry
 
         def edge(i, carry, source=source, target=target, scale=scale, power=power):
@@ -257,11 +297,11 @@
             def put(half, c, t, value):
                 target[half, c, x, t] = value
 
-            taylor(source, full, x, (1, 2), scale, put, (1, 2, 4, 5))
+            taylor(source, full, band, x, (1, 2), scale, put, (1, 2, 4, 5))
             return carry
 
         lax.fori_loop(0, 4, edge, 0, unroll=2)
-        lax.fori_loop(2 * power + 2, XW - 2 * power - 2, body, 0, unroll=2)
+        lax.fori_loop(2 * power + 2, XW - 2 * power - 2, body, 0, unroll=4)
 
     def last(x, carry):
         def put(half, c, t, value):
@@ -270,10 +310,10 @@
             total = total + t3[half, c, x, t]
             acc[half, c, x - 8, t - 1] = total + value
 
-        taylor(t3, full, x, (1, 2), STEP / 4 / 12.0, put)
+        taylor(t3, full, band, x, (1, 2), STEP / 4 / 12.0, put)
         return carry
 
-    lax.fori_loop(8, XW - 8, last, 0, unroll=2)
+    lax.fori_loop(8, XW - 8, last, 0, unroll=4)
     for c in range(6):
         for t in (0, 1):
             new_ref[c, :, pl.ds(8 * t, 8), :] = acc[0, c, 2:18, t]
@@ -307,25 +347,38 @@
         wz[kind, pl.ds(CZ, CZ), columns] = jnp.zeros((CZ, 128), F32)
         wz[kind, pl.ds(CZ, 8), columns] = weights(low + (CZ + 2.0), bz, wz_rows)
         wz[kind, pl.ds(2 * CZ - 8, 8), columns] = weights(low - 6.0, bz, wz_rows)
-        in_x = [weights(jnp.full((1, 128), float(x), F32), bx, wx) for x in range(CX + 4)]
-        for t in (0, 1):
-            in_y = weights(low + (8.0 * t + 2.0), by, wy)
-            for x in range(CX + 4):
-                if kind == 0:
+        in_x = [weights(jnp.full((1, 128), float(x), F32), bx, wx) for x in range(CX + 4)] if kind == 0 else []
+        if kind == 0:
+            for t in (0, 1):
+                in_y = weights(low + (8.0 * t + 2.0), by, wy)
+                for x in range(CX + 4):
                     wxy[x, t, :, columns] = in_x[x] * in_y
-                elif kind == 2 - t:
-                    spill[kind - 1, x, :, columns] = in_x[x] * in_y
+        else:
+            pair_row = rows_of((8, 128))
+            in_y = weights((pair_row % 2).astype(F32) + (16.0 if kind == 1 else 2.0), by, wy)
+            for g in range(CX // 4 + 1):
+                along = weights((pair_row // 2 + 4 * g).astype(F32), bx, wx)
+                spill[kind - 1, g, :, columns] = along * in_y
+
+    for kind in (0, 1):
+        for half in (0, 1):
+            for c in range(6):
+                for g in range(CX // 4 + 1):
+                    total = None
+                    for i in range(4):
+                        tile = acc[half, c, 4 * g + i, 1 - kind]
+                        moved = roll(tile, 2 * i - (6 if kind == 0 else 0), 0)
+                        total = moved if total is None else jnp.where(row >= 2 * i, moved, total)
+                    edge_rows[kind, half, c, g] = total
 
     parts[...] = jnp.zeros((48, 128), F32)
-    for c in range(6):
-        def both(t):
-            grid = [acc[half, c] if t is None else acc[half, c, :, t] for half in (0, 1)]
-            return jnp.concatenate([g.reshape(-1, CZ) for g in grid], axis=1)
-
-        for kind, t, weight in ((0, None, wxy), (1, 1, spill.at[0]), (2, 0, spill.at[1])):
-            along = dot(both(t), wz[kind])
-            product = along * weight[...].reshape(along.shape)
-            total = jnp.sum(product, axis=0, keepdims=True)
+    for kind in range(3):
+        grid = [acc[half] if kind == 0 else edge_rows[kind - 1, half] for half in (0, 1)]
+        weight = wxy[...].reshape(-1, 256) if kind == 0 else spill[kind - 1].reshape(-1, 256)
+        along = dot(jnp.concatenate([g.reshape(-1, CZ) for g in grid], axis=1), wz[kind])
+        count = weight.shape[0]
+        for c in range(6):
+            total = jnp.sum(along[c * count:c * count + count] * weight, axis=0, keepdims=True)
             for at in (0, 1):
                 parts[pl.ds((2 * kind + at) * 8 + c, 1), :] = total[:, 128 * at:128 * at + 128]
     values = parts[...]
@@ -403,7 +456,18 @@
         axis=1,
     )
     zshape = (ZGROUPS, CY, CZ)
-    zlo, zhi, inv = call(pack_z, [zshape, zshape, (CX, CY, CZ)], (fields, permittivity), 16)
+    zlo, zhi, inv = call(
+        pack_z,
+        [zshape, zshape, (CX, CY, CZ)],
+        (fields, permittivity),
+        8,
+        scratch=[
+            pltpu.VMEM((6, CX, CY, CZ), F32),
+            pltpu.VMEM((CX, CY, CZ), F32),
+            pltpu.SemaphoreType.DMA((5,)),
+        ],
+        space=pltpu.HBM,
+    )
     zlo, zhi = shift_both(zlo, zhi, "gz")
     yshape = (YTOTAL, 8, CZ)
     ylo, yhi = call(pack_y, [yshape, yshape], (fields, inv, zlo, zhi), 8)
@@ -429,8 +493,10 @@
             pltpu.VMEM((2, 256, 128), F32),
             pltpu.VMEM((3, 256, 256), F32),
             pltpu.VMEM((CX + 4, 2, 8, 256), F32),
-            pltpu.VMEM((2, CX + 4, 8, 256), F32),
+            pltpu.VMEM((2, CX // 4 + 1, 8, 256), F32),
+            pltpu.VMEM((2, 2, 6, CX // 4 + 1, 8, CZ), F32),
             pltpu.VMEM((48, 128), F32),
+            pltpu.VMEM((256, 256), jnp.bfloat16),
         ],
         flops=100000000,
     )

time: 108 us -> 105 us (0.972)
  Pallas kernels: 24 us -> 21.6 us
    pallas_call x6, Pallas kernels: 24 us -> 21.6 us  [call(): pl.pallas_call(body, out_shape=[jax.ShapeDtypeStruct(s, F32) for s in out...]
where the time goes in v3:
time: 105 us
  blocking collectives  50.3 us (48%)
  Pallas kernels  21.6 us (21%)
  starting transfers between devices  18 us (17%)
  waiting for transfers between devices  11.2 us (11%)
  local copies, waits for them, and re-layouts  3.12 us (3%)
    all_to_all x1, blocking collectives, local(): req = lax.all_to_all(send, ('gy', 'gz'), 0, 0, tiled=True)  29.6 us
    pallas_call x6, Pallas kernels, call(): pl.pallas_call(body, out_shape=[jax.ShapeDtypeStruct(s, F32) for s in out...  21.6 us
    all_to_all x1, blocking collectives, local(): answers = lax.all_to_all(answers, ('gy', 'gz'), 0, 0, tiled=True)  20.6 us
    ppermute x3, starting transfers between devices, shift_both(): lax.ppermute(high_edge, axis, up)  12.8 us
    ppermute x3, waiting for transfers between devices, shift_both(): lax.ppermute(low_edge, axis, down)  8.6 us
    ppermute x3, starting transfers between devices, shift_both(): lax.ppermute(low_edge, axis, down)  5.13 us
    unnamed x14, local copies, waits for them, and re-layouts  2.74 us
    ppermute x3, waiting for transfers between devices, shift_both(): lax.ppermute(high_edge, axis, up)  2.6 us
  transfers between devices with their start and end apart: 6, of which 4 were waited for; matrix products, arithmetic and copies ran while one was open for 1% of the time, Pallas kernels for 1%

profile of v3, /device:TPU:7, one launch (start us, length us, event | category | flops | bytes accessed | tf_op | source)
XLA Modules:
  0.0 105.1 jit_solution(10045123137569945295)
XLA Ops:
  0.6 0.0 copy-start
  0.6 1.1 %copy-done = f32[6,16,16,128]{3,2,1,0:T(8,128)S(1)} copy-done((f32[6,16,16,128]{3,2,1,0:T(8,128)S(1)}, f32[6,16,16,128]{3,2,1,0:T(8,128)}, u32[]{:S(2)}) %copy-start) | copy-done | bytes 786456
  1.8 0.0 copy-start.2
  1.8 0.9 copy-done.2
  2.7 1.2 %shard_map.68 = (f32[10,16,128]{2,1,0:T(8,128)S(1)}, f32[10,16,128]{2,1,0:T(8,128)S(1)}, f32[16,16,128]{2,1,0:T(8,128)S(1)}) custom-call(f32[6,16,16,128]{3,2,1,0:T(8,128)S(1)} %copy-done, f32[16,16,128]{2,1,0:T(8,128)S(1)} %copy-done.2), custom_call_target="tpu_custom_call" | custom-call | flops 1000000 | bytes 1000000 | tf_op jit(solution)/shard_map/pallas_call | solution.py:69
  3.9 3.5 %collective-permute-start = (f32[10,16,128]{2,1,0:T(8,128)S(1)}, f32[10,16,128]{2,1,0:T(8,128)S(1)}, u32[]{:S(2)}, u32[]{:S(2)}) collective-permute-start(f32[10,16,128]{2,1,0:T(8,128)S(1)} %get-tuple-element.18), channel_id=1, source_target_pairs={{0,1},{1,2},{2,3},{3,4},{4,5},{5,6},{6,7},{7,8},{8,9},{9,10},{10,1... | collective-permute-start | bytes 245768 | tf_op jit(solution)/shard_map/ppermute | solution.py:445
  7.4 1.3 %collective-permute-start.1 = (f32[10,16,128]{2,1,0:T(8,128)S(1)}, f32[10,16,128]{2,1,0:T(8,128)S(1)}, u32[]{:S(2)}, u32[]{:S(2)}) collective-permute-start(f32[10,16,128]{2,1,0:T(8,128)S(1)} %get-tuple-element.19), channel_id=1, source_target_pairs={{1,0},{2,1},{3,2},{4,3},{5,4},{6,5},{7,6},{8,7},{9,8},{10,9},{11,1... | collective-permute-start | bytes 245768 | tf_op jit(solution)/shard_map/ppermute | solution.py:445
  8.7 0.2 collective-permute-done.zlo_ref
  8.9 3.9 %collective-permute-done.1.zhi_ref = f32[10,16,128]{2,1,0:T(8,128)S(1)} collective-permute-done((f32[10,16,128]{2,1,0:T(8,128)S(1)}, f32[10,16,128]{2,1,0:T(8,128)S(1)}, u32[]{:S(2)}, u32[]{:S(2)}) %collective-permute-start.1) | collective-permute-done | bytes 81952 | tf_op jit(solution)/shard_map/ppermute | solution.py:445
  12.8 0.0 copy-start.1
  12.8 0.1 shard_map.69
  12.9 0.0 copy-start.5
  12.9 0.0 copy-start.4
  12.9 5.1 %collective-permute-start.2 = (f32[132,8,128]{2,1,0:T(8,128)S(1)}, f32[132,8,128]{2,1,0:T(8,128)S(1)}, u32[]{:S(2)}, u32[]{:S(2)}) collective-permute-start(f32[132,8,128]{2,1,0:T(8,128)S(1)} %get-tuple-element.20), channel_id=1, source_target_pairs={{0,16},{16,32},{32,48},{1,17},{17,33},{33,49},{2,18},{18,34},{34,5... | collective-permute-start | bytes 1622024 | tf_op jit(solution)/shard_map/ppermute | solution.py:445
  18.0 1.9 %collective-permute-start.3 = (f32[132,8,128]{2,1,0:T(8,128)S(1)}, f32[132,8,128]{2,1,0:T(8,128)S(1)}, u32[]{:S(2)}, u32[]{:S(2)}) collective-permute-start(f32[132,8,128]{2,1,0:T(8,128)S(1)} %get-tuple-element.21), channel_id=1, source_target_pairs={{16,0},{32,16},{48,32},{17,1},{33,17},{49,33},{18,2},{34,18},{50,3... | collective-permute-start | bytes 1622024 | tf_op jit(solution)/shard_map/ppermute | solution.py:445
  20.0 0.0 copy-done.5
  20.0 0.0 copy-done.4
  20.0 0.1 copy.10
  20.1 0.0 copy-start.3
  20.1 0.1 copy.12
  20.2 0.6 copy-done.3
  20.8 0.1 copy.11
  20.9 0.1 pad.3.clone
  21.0 0.1 maximum_maximum_fusion.data_ref
  21.1 0.8 shard_map.70
  21.9 2.4 %collective-permute-done.2.ylo_ref = f32[132,8,128]{2,1,0:T(8,128)S(1)} collective-permute-done((f32[132,8,128]{2,1,0:T(8,128)S(1)}, f32[132,8,128]{2,1,0:T(8,128)S(1)}, u32[]{:S(2)}, u32[]{:S(2)}) %collective-permute-start.2) | collective-permute-done | bytes 540704 | tf_op jit(solution)/shard_map/ppermute | solution.py:445
  24.3 4.7 %collective-permute-done.3.yhi_ref = f32[132,8,128]{2,1,0:T(8,128)S(1)} collective-permute-done((f32[132,8,128]{2,1,0:T(8,128)S(1)}, f32[132,8,128]{2,1,0:T(8,128)S(1)}, u32[]{:S(2)}, u32[]{:S(2)}) %collective-permute-start.3) | collective-permute-done | bytes 540704 | tf_op jit(solution)/shard_map/ppermute | solution.py:445
  29.0 0.0 copy-done.1
  29.0 0.1 shard_map.71
  29.1 4.1 %collective-permute-start.4 = (f32[242,8,128]{2,1,0:T(8,128)S(1)}, f32[242,8,128]{2,1,0:T(8,128)S(1)}, u32[]{:S(2)}, u32[]{:S(2)}) collective-permute-start(f32[242,8,128]{2,1,0:T(8,128)S(1)} %get-tuple-element.25), channel_id=1, source_target_pairs={{0,64},{64,128},{128,192},{192,256},{256,320},{320,384},{384,448},... | collective-permute-start | bytes 2973704 | tf_op jit(solution)/shard_map/ppermute | solution.py:445
  33.3 1.9 %collective-permute-start.5 = (f32[242,8,128]{2,1,0:T(8,128)S(1)}, f32[242,8,128]{2,1,0:T(8,128)S(1)}, u32[]{:S(2)}, u32[]{:S(2)}) collective-permute-start(f32[242,8,128]{2,1,0:T(8,128)S(1)} %get-tuple-element.26), channel_id=1, source_target_pairs={{64,0},{128,64},{192,128},{256,192},{320,256},{384,320},{448,384},... | collective-permute-start | bytes 2973704 | tf_op jit(solution)/shard_map/ppermute | solution.py:445
  35.2 0.1 copy.13
  35.3 29.6 %all_to_all.22 = f32[64,1,256]{2,1,0:T(1,128)S(1)} all-to-all(f32[64,1,256]{2,1,0:T(1,128)S(1)} %copy.13), channel_id=1, replica_groups=mesh['gx'=8,'gy'=4,'gz'=16] {'gy','gz'}, dimensions={0} | all-to-all | bytes 131072 | tf_op jit(solution)/shard_map/all_to_all | solution.py:480
  64.9 0.0 collective-permute-done.4.xlo_ref
  64.9 0.0 collective-permute-done.5.xhi_ref
  64.9 18.5 %shard_map.72 = (f32[6,16,16,128]{3,2,1,0:T(8,128)}, f32[64,128]{1,0:T(8,128)S(1)}) custom-call(f32[6,16,16,128]{3,2,1,0:T(8,128)S(1)} %copy-done.1, f32[16,16,128]{2,1,0:T(8,128)S(1)} %get-tuple-element.17.inv_ref.own_inv_ref, f32[10,16,128]{2,1,0:T(8,128)S(1)} %collective-permute-done.zlo_ref, f32[10,16,128]{2,1,0:T(8,128)S(1)} %collective-permute-done.1.zhi_ref, ...), custom_call_target="tpu_custom_call" | custom-call | flops 100000000 | bytes 1000000 | tf_op jit(solution)/shard_map/pallas_call | solution.py:69
  83.4 20.6 %all_to_all.23 = f32[64,1,128]{2,1,0:T(1,128)S(1)} all-to-all(f32[64,1,128]{2,1,0:T(1,128)S(1)} %bitcast.11), channel_id=1, replica_groups=mesh['gx'=8,'gy'=4,'gz'=16] {'gy','gz'}, dimensions={0} | all-to-all | bytes 65536 | tf_op jit(solution)/shard_map/all_to_all | solution.py:503
  104.1 1.0 shard_map.73
  (4 shorter events, 0.0 us)
Async XLA Ops:
  0.6 1.1 %copy-start = (f32[6,16,16,128]{3,2,1,0:T(8,128)S(1)}, f32[6,16,16,128]{3,2,1,0:T(8,128)}, u32[]{:S(2)}) copy-start(f32[6,16,16,128]{3,2,1,0:T(8,128)} %f_ref.5) | copy-start | bytes 2359300
  1.8 0.9 copy-start.2
  3.9 5.0 %collective-permute-start = (f32[10,16,128]{2,1,0:T(8,128)S(1)}, f32[10,16,128]{2,1,0:T(8,128)S(1)}, u32[]{:S(2)}, u32[]{:S(2)}) collective-permute-start(f32[10,16,128]{2,1,0:T(8,128)S(1)} %get-tuple-element.18), channel_id=1, source_target_pairs={{0,1},{1,2},{2,3},{3,4},{4,5},{5,6},{6,7},{7,8},{8,9},{9,10},{10,1... | collective-permute-start | bytes 245768 | tf_op jit(solution)/shard_map/ppermute | solution.py:445
  7.4 5.4 %collective-permute-start.1 = (f32[10,16,128]{2,1,0:T(8,128)S(1)}, f32[10,16,128]{2,1,0:T(8,128)S(1)}, u32[]{:S(2)}, u32[]{:S(2)}) collective-permute-start(f32[10,16,128]{2,1,0:T(8,128)S(1)} %get-tuple-element.19), channel_id=1, source_target_pairs={{1,0},{2,1},{3,2},{4,3},{5,4},{6,5},{7,6},{8,7},{9,8},{10,9},{11,1... | collective-permute-start | bytes 245768 | tf_op jit(solution)/shard_map/ppermute | solution.py:445
  12.8 16.2 %copy-start.1 = (f32[6,16,16,128]{3,2,1,0:T(8,128)S(1)}, f32[6,16,16,128]{3,2,1,0:T(8,128)}, u32[]{:S(2)}) copy-start(f32[6,16,16,128]{3,2,1,0:T(8,128)} %f_ref.5) | copy-start | bytes 2359300
  12.9 7.1 %copy-start.5 = (s32[128,1]{0,1:T(1,128)S(1)}, s32[128,1]{0,1:T(1,128)}, u32[]{:S(2)}) copy-start(s32[128,1]{0,1:T(1,128)} %param.7) | copy-start | bytes 1540
  12.9 7.1 %copy-start.4 = (s32[128,3]{0,1:T(4,128)S(1)}, s32[128,3]{0,1:T(4,128)}, u32[]{:S(2)}) copy-start(s32[128,3]{0,1:T(4,128)} %param.8) | copy-start | bytes 4612
  12.9 11.4 %collective-permute-start.2 = (f32[132,8,128]{2,1,0:T(8,128)S(1)}, f32[132,8,128]{2,1,0:T(8,128)S(1)}, u32[]{:S(2)}, u32[]{:S(2)}) collective-permute-start(f32[132,8,128]{2,1,0:T(8,128)S(1)} %get-tuple-element.20), channel_id=1, source_target_pairs={{0,16},{16,32},{32,48},{1,17},{17,33},{33,49},{2,18},{18,34},{34,5... | collective-permute-start | bytes 1622024 | tf_op jit(solution)/shard_map/ppermute | solution.py:445
  18.0 11.0 %collective-permute-start.3 = (f32[132,8,128]{2,1,0:T(8,128)S(1)}, f32[132,8,128]{2,1,0:T(8,128)S(1)}, u32[]{:S(2)}, u32[]{:S(2)}) collective-permute-start(f32[132,8,128]{2,1,0:T(8,128)S(1)} %get-tuple-element.21), channel_id=1, source_target_pairs={{16,0},{32,16},{48,32},{17,1},{33,17},{49,33},{18,2},{34,18},{50,3... | collective-permute-start | bytes 1622024 | tf_op jit(solution)/shard_map/ppermute | solution.py:445
  20.1 0.7 copy-start.3
  29.1 35.8 %collective-permute-start.4 = (f32[242,8,128]{2,1,0:T(8,128)S(1)}, f32[242,8,128]{2,1,0:T(8,128)S(1)}, u32[]{:S(2)}, u32[]{:S(2)}) collective-permute-start(f32[242,8,128]{2,1,0:T(8,128)S(1)} %get-tuple-element.25), channel_id=1, source_target_pairs={{0,64},{64,128},{128,192},{192,256},{256,320},{320,384},{384,448},... | collective-permute-start | bytes 2973704 | tf_op jit(solution)/shard_map/ppermute | solution.py:445
  33.3 31.6 %collective-permute-start.5 = (f32[242,8,128]{2,1,0:T(8,128)S(1)}, f32[242,8,128]{2,1,0:T(8,128)S(1)}, u32[]{:S(2)}, u32[]{:S(2)}) collective-permute-start(f32[242,8,128]{2,1,0:T(8,128)S(1)} %get-tuple-element.26), channel_id=1, source_target_pairs={{64,0},{128,64},{192,128},{256,192},{320,256},{384,320},{448,384},... | collective-permute-start | bytes 2973704 | tf_op jit(solution)/shard_map/ppermute | solution.py:445

commit v4 on v3

--- a/solution.py
+++ b/solution.py
@@ -15,6 +15,10 @@
 STRIDE = 20
 EXACT = lax.Precision.HIGHEST
 F32 = jnp.float32
+
+
+def band_of(t, d=0):
+    return pl.ds(8 + 8 * t + d, 8)
 
 
 def z_slot(c, x):
@@ -64,13 +68,13 @@
     return [pl.BlockSpec(memory_space=pltpu.VMEM)] * count
 
 
-def call(body, outs, ins, limit, scratch=(), flops=1000000, space=pltpu.VMEM):
+def call(body, outs, ins, limit, scratch=(), flops=1000000, space=pltpu.VMEM, first=pltpu.VMEM):
     many = isinstance(outs, list)
     return pl.pallas_call(
         body,
         out_shape=[jax.ShapeDtypeStruct(s, F32) for s in outs] if many else jax.ShapeDtypeStruct(outs, F32),
         in_specs=[pl.BlockSpec(memory_space=space)] * len(ins),
-        out_specs=vmem(len(outs)) if many else vmem(1)[0],
+        out_specs=[pl.BlockSpec(memory_space=first)] + vmem(len(outs) - 1) if many else vmem(1)[0],
         scratch_shapes=list(scratch),
         compiler_params=pltpu.CompilerParams(vmem_limit_bytes=limit * 1048576),
         cost_estimate=pl.CostEstimate(flops=flops, bytes_accessed=1000000, transcendentals=0),
@@ -150,10 +154,10 @@
             out[n] = end_of(g, t, e)
 
 
-def taylor(source, inv_ref, band, x, tiles, scale, put, comps=(0, 1, 2, 3, 4, 5)):
+def taylor(source, inv_ref, band, x, tiles, scale, put, comps=(0, 1, 2, 3, 4, 5), skip=0):
     row = rows_of((8, CZ))
-    def load(half, c, t, d=0):
-        return source[half, c, x + d, t % 4]
+    def load(half, c, t, d=0, e=0):
+        return source[half, c, x + d - skip, band_of(t, e)]
 
     def dx(c):
         return {
@@ -166,28 +170,22 @@
         }
 
     def dy(c):
-        out = {}
-        for half in (0, 1):
-            u = {}
-            for t in sorted({v % 4 for t in tiles for v in (t, t + 1)}):
-                here = load(half, c, t)
-                u[t] = here - roll(jnp.where(row >= 6, load(half, c, t - 1), here), 2, 0)
-            for t in tiles:
-                low, high = u[t], u[(t + 1) % 4]
-                near = roll(jnp.where(row < 1, high, low), -1, 0)
-                out[half, t] = (near, roll(jnp.where(row < 2, high, low), -2, 0) + low)
-        return out
+        return {
+            (half, t): (
+                load(half, c, t, 0, 1) - load(half, c, t, 0, -1),
+                load(half, c, t, 0, 2) - load(half, c, t, 0, -2),
+            )
+            for half in (0, 1)
+            for t in tiles
+        }
 
     def all_dz(fields):
         block = jnp.concatenate(
             [jnp.concatenate([load(0, c, t), load(1, c, t)], axis=1) for c in fields for t in tiles], axis=0
         )
-        high = block.astype(jnp.bfloat16)
-        rest = block - high.astype(F32)
-        middle = rest.astype(jnp.bfloat16)
-        low = (rest - middle.astype(F32)).astype(jnp.bfloat16)
-        total = sum(
-            jnp.dot(part, band[...], preferred_element_type=F32) for part in (low, middle, high)
+        high, middle, low = three_parts(block)
+        total = jnp.dot(
+            jnp.concatenate([low, middle, high], axis=1), band[...], preferred_element_type=F32
         )
         out = {}
         for i, c in enumerate(fields):
@@ -202,7 +200,7 @@
     factors = {}
     for half in (0, 1):
         for t in tiles:
-            inv = inv_ref[half, 6, x, t]
+            inv = inv_ref[half, 6, x, band_of(t)]
             factors[half, t] = (inv * scale, jnp.where(inv > 0.0, scale, 0.0))
     for c in comps:
         first, c1, c2, second = pairs[c]
@@ -222,6 +220,23 @@
     return lax.dot_general(a, b, (((da,), (db,)), ((), ())), precision=EXACT, preferred_element_type=F32)
 
 
+def three_parts(value):
+    high = value.astype(jnp.bfloat16)
+    rest = value - high.astype(F32)
+    middle = rest.astype(jnp.bfloat16)
+    return high, middle, (rest - middle.astype(F32)).astype(jnp.bfloat16)
+
+
+def split_dot(a, b):
+    ah, am, al = three_parts(a)
+    bh, bm, bl = three_parts(b)
+    return jnp.dot(
+        jnp.concatenate([al, ah, am, am, ah, ah], axis=1),
+        jnp.concatenate([bh, bl, bm, bh, bm, bh], axis=0),
+        preferred_element_type=F32,
+    )
+
+
 def spread(count, parity):
     shape = (count, 128)
     return (lanes(shape) == rows_of(shape) + parity * 64).astype(F32)
@@ -230,7 +245,7 @@
 def compute(
     f_ref, own_inv_ref, zlo_ref, zhi_ref, ylo_ref, yhi_ref, xlo_ref, xhi_ref, req_ref,
     new_ref, ans_ref,
-    full, t1, t2, t3, acc, words, wz, wxy, spill, edge_rows, parts, band,
+    full, t1, t2, t3, acc, words, wz, wxy, spill, edge_rows, parts, band, sems,
 ):
     lane = lanes((8, CZ))
     row = rows_of((8, CZ))
@@ -240,11 +255,11 @@
         g, s = z_slot(c, x)
         for t in (1, 2):
             own = pl.ds(8 * (t - 1), 8)
-            full[0, c, GX + x, t] = f_ref[c, x, own] if c < 6 else own_inv_ref[x, own]
-            full[1, c, GX + x, t] = z_ends(zlo_ref[g, own], zhi_ref[g, own], s, lane)
+            full[0, c, GX + x, band_of(t)] = f_ref[c, x, own] if c < 6 else own_inv_ref[x, own]
+            full[1, c, GX + x, band_of(t)] = z_ends(zlo_ref[g, own], zhi_ref[g, own], s, lane)
         for ref, t in ((ylo_ref, 0), (yhi_ref, 3)):
-            full[0, c, GX + x, t] = ref[p]
-            full[1, c, GX + x, t] = z_ends(ref[PAIRS + g], ref[PAIRS + ZGROUPS + g], s, lane)
+            full[0, c, GX + x, band_of(t)] = ref[p]
+            full[1, c, GX + x, band_of(t)] = z_ends(ref[PAIRS + g], ref[PAIRS + ZGROUPS + g], s, lane)
     for side in (0, 1):
         ref = xhi_ref if side == 0 else xlo_ref
         where_main = {key: n for n, key in enumerate(XMAIN)}
@@ -266,38 +281,40 @@
                         if pair[half] is None:
                             continue
                         if t == 4:
-                            full[half, c, x, 0] = jnp.where(row >= 4, pair[half], 0.0)
-                            full[half, c, x, 3] = jnp.where(row >= 4, 0.0, pair[half])
+                            full[half, c, x, band_of(0)] = jnp.where(row >= 4, pair[half], 0.0)
+                            full[half, c, x, band_of(3)] = jnp.where(row >= 4, 0.0, pair[half])
                             done |= {(half, 0), (half, 3)}
                         else:
-                            full[half, c, x, t] = pair[half]
+                            full[half, c, x, band_of(t)] = pair[half]
                             done.add((half, t))
                 for half in (0, 1):
                     for t in (0, 3):
                         if (half, t) not in done:
-                            full[half, c, x, t] = zero
+                            full[half, c, x, band_of(t)] = zero
 
     ring = (rows_of((256, 256)) - lanes((256, 256)) + 256) % 256
     one = lambda d: (ring == d % 256).astype(F32)
-    band[...] = (8.0 * (one(1) - one(-1)) + one(-2) - one(2)).astype(jnp.bfloat16)
+    stencil = (8.0 * (one(1) - one(-1)) + one(-2) - one(2)).astype(jnp.bfloat16)
+    for i in range(3):
+        band[pl.ds(256 * i, 256), :] = stencil
 
     for power, source, target in ((1, full, t1), (2, t1, t2), (3, t2, t3)):
         scale = STEP / power / 12.0
 
-        def body(x, carry, source=source, target=target, scale=scale):
+        def body(x, carry, source=source, target=target, scale=scale, power=power):
             def put(half, c, t, value):
-                target[half, c, x, t] = value
-
-            taylor(source, full, band, x, (0, 1, 2, 3), scale, put)
+                target[half, c, x - 2 * power, band_of(t)] = value
+
+            taylor(source, full, band, x, (0, 1, 2, 3), scale, put, skip=2 * power - 2)
             return carry
 
         def edge(i, carry, source=source, target=target, scale=scale, power=power):
             x = jnp.where(i < 2, 2 * power + i, XW - 2 * power - 4 + i)
 
             def put(half, c, t, value):
-                target[half, c, x, t] = value
-
-            taylor(source, full, band, x, (1, 2), scale, put, (1, 2, 4, 5))
+                target[half, c, x - 2 * power, band_of(t)] = value
+
+            taylor(source, full, band, x, (1, 2), scale, put, (1, 2, 4, 5), skip=2 * power - 2)
             return carry
 
         lax.fori_loop(0, 4, edge, 0, unroll=2)
@@ -305,18 +322,21 @@
 
     def last(x, carry):
         def put(half, c, t, value):
-            total = full[half, c, x, t] + t1[half, c, x, t]
-            total = total + t2[half, c, x, t]
-            total = total + t3[half, c, x, t]
+            total = full[half, c, x, band_of(t)] + t1[half, c, x - 2, band_of(t)]
+            total = total + t2[half, c, x - 4, band_of(t)]
+            total = total + t3[half, c, x - 6, band_of(t)]
             acc[half, c, x - 8, t - 1] = total + value
 
-        taylor(t3, full, band, x, (1, 2), STEP / 4 / 12.0, put)
+        taylor(t3, full, band, x, (1, 2), STEP / 4 / 12.0, put, skip=6)
         return carry
 
     lax.fori_loop(8, XW - 8, last, 0, unroll=4)
-    for c in range(6):
-        for t in (0, 1):
-            new_ref[c, :, pl.ds(8 * t, 8), :] = acc[0, c, 2:18, t]
+    writes = [
+        pltpu.make_async_copy(acc.at[0, :, pl.ds(2, CX), t], new_ref.at[:, :, pl.ds(8 * t, 8), :], sems.at[t])
+        for t in (0, 1)
+    ]
+    for write in writes:
+        write.start()
 
     req = req_ref[...]
     words[0] = dot(req, spread(64, 0), 0, 0)
@@ -375,7 +395,7 @@
     for kind in range(3):
         grid = [acc[half] if kind == 0 else edge_rows[kind - 1, half] for half in (0, 1)]
         weight = wxy[...].reshape(-1, 256) if kind == 0 else spill[kind - 1].reshape(-1, 256)
-        along = dot(jnp.concatenate([g.reshape(-1, CZ) for g in grid], axis=1), wz[kind])
+        along = split_dot(jnp.concatenate([g.reshape(-1, CZ) for g in grid], axis=1), wz[kind])
         count = weight.shape[0]
         for c in range(6):
             total = jnp.sum(along[c * count:c * count + count] * weight, axis=0, keepdims=True)
@@ -388,6 +408,8 @@
     ans_ref[...] = dot(spread(64, 0), jnp.concatenate([filled, empty], axis=0), 1, 1) + dot(
         spread(64, 1), jnp.concatenate([empty, filled], axis=0), 1, 1
     )
+    for write in writes:
+        write.wait()
 
 
 def requests(data_ref, send_ref, pick_ref, rank_ref):
@@ -460,7 +482,7 @@
         pack_z,
         [zshape, zshape, (CX, CY, CZ)],
         (fields, permittivity),
-        8,
+        53,
         scratch=[
             pltpu.VMEM((6, CX, CY, CZ), F32),
             pltpu.VMEM((CX, CY, CZ), F32),
@@ -478,17 +500,14 @@
     send, xlo, xhi = lax.optimization_barrier((send, xlo, xhi))
     xlo, xhi = shift_both(xlo, xhi, "gx")
     req = lax.all_to_all(send, ("gy", "gz"), 0, 0, tiled=True)
-    big = pltpu.VMEM((2, 6, XW, 4, 8, CZ), F32)
     new_fields, answers = call(
         compute,
         [(6, CX, CY, CZ), (64, 128)],
         (fields, inv, zlo, zhi, ylo, yhi, xlo, xhi, req),
-        42,
+        46,
         scratch=[
-            pltpu.VMEM((2, NF, XW, 4, 8, CZ), F32),
-            big,
-            big,
-            big,
+            pltpu.VMEM((2, NF, XW, 48, CZ), F32),
+            *[pltpu.VMEM((2, 6, XW - 4 * m, 48, CZ), F32) for m in (1, 2, 3)],
             pltpu.VMEM((2, 6, CX + 4, 2, 8, CZ), F32),
             pltpu.VMEM((2, 256, 128), F32),
             pltpu.VMEM((3, 256, 256), F32),
@@ -496,9 +515,11 @@
             pltpu.VMEM((2, CX // 4 + 1, 8, 256), F32),
             pltpu.VMEM((2, 2, 6, CX // 4 + 1, 8, CZ), F32),
             pltpu.VMEM((48, 128), F32),
-            pltpu.VMEM((256, 256), jnp.bfloat16),
+            pltpu.VMEM((768, 256), jnp.bfloat16),
+            pltpu.SemaphoreType.DMA((2,)),
         ],
         flops=100000000,
+        first=pl.ANY,
     )
     answers = lax.all_to_all(answers, ("gy", "gz"), 0, 0, tiled=True)
     receptor_values = call(collect, (6, 128), (answers, pick, rank), 8)

time: 105 us -> 103 us (0.981)
  Pallas kernels: 21.6 us -> 20.2 us
  local copies, waits for them, and re-layouts: 3.12 us -> 2.05 us
    pallas_call x6, Pallas kernels: 21.6 us -> 20.2 us  [call(): pl.pallas_call(body, out_shape=[jax.ShapeDtypeStruct(s, F32) for s in out...]
    unnamed x14 -> x12, local copies, waits for them, and re-layouts: 2.74 us -> 1.68 us
where the time goes in v4:
time: 103 us; the launch traced here: 102 us
  blocking collectives  50.3 us (49%)
  Pallas kernels  20.2 us (20%)
  starting transfers between devices  17.8 us (17%)
  waiting for transfers between devices  11.2 us (11%)
  local copies, waits for them, and re-layouts  2.05 us (2%)
    all_to_all x1, blocking collectives, local(): req = lax.all_to_all(send, ('gy', 'gz'), 0, 0, tiled=True)  29.6 us
    all_to_all x1, blocking collectives, local(): answers = lax.all_to_all(answers, ('gy', 'gz'), 0, 0, tiled=True)  20.7 us
    pallas_call x6, Pallas kernels, call(): pl.pallas_call(body, out_shape=[jax.ShapeDtypeStruct(s, F32) for s in out...  20.2 us
    ppermute x3, starting transfers between devices, shift_both(): lax.ppermute(high_edge, axis, up)  12.7 us
    ppermute x3, waiting for transfers between devices, shift_both(): lax.ppermute(low_edge, axis, down)  8.6 us
    ppermute x3, starting transfers between devices, shift_both(): lax.ppermute(low_edge, axis, down)  5.13 us
    ppermute x3, waiting for transfers between devices, shift_both(): lax.ppermute(high_edge, axis, up)  2.6 us
  transfers between devices with their start and end apart: 6, of which 4 were waited for; matrix products, arithmetic and copies ran while one was open for 1% of the time, Pallas kernels for 1%

profile of v4, /device:TPU:7, one launch (start us, length us, event | category | flops | bytes accessed | tf_op | source)
XLA Modules:
  0.0 102.4 jit_solution(2243943281116857906)
XLA Ops:
  0.6 0.0 copy-start
  0.6 0.0 copy-start.1
  0.6 1.0 copy-done.1
  1.6 1.8 %shard_map.68 = (f32[10,16,128]{2,1,0:T(8,128)S(1)}, f32[10,16,128]{2,1,0:T(8,128)S(1)}, f32[16,16,128]{2,1,0:T(8,128)S(1)}) custom-call(f32[6,16,16,128]{3,2,1,0:T(8,128)} %f_ref.5, f32[16,16,128]{2,1,0:T(8,128)S(1)} %copy-done.1), custom_call_target="tpu_custom_call" | custom-call | flops 1000000 | bytes 1000000 | tf_op jit(solution)/shard_map/pallas_call | solution.py:73
  3.4 3.5 %collective-permute-start = (f32[10,16,128]{2,1,0:T(8,128)S(1)}, f32[10,16,128]{2,1,0:T(8,128)S(1)}, u32[]{:S(2)}, u32[]{:S(2)}) collective-permute-start(f32[10,16,128]{2,1,0:T(8,128)S(1)} %get-tuple-element.18), channel_id=1, source_target_pairs={{0,1},{1,2},{2,3},{3,4},{4,5},{5,6},{6,7},{7,8},{8,9},{9,10},{10,1... | collective-permute-start | bytes 245768 | tf_op jit(solution)/shard_map/ppermute | solution.py:467
  7.0 1.3 %collective-permute-start.1 = (f32[10,16,128]{2,1,0:T(8,128)S(1)}, f32[10,16,128]{2,1,0:T(8,128)S(1)}, u32[]{:S(2)}, u32[]{:S(2)}) collective-permute-start(f32[10,16,128]{2,1,0:T(8,128)S(1)} %get-tuple-element.19), channel_id=1, source_target_pairs={{1,0},{2,1},{3,2},{4,3},{5,4},{6,5},{7,6},{8,7},{9,8},{10,9},{11,1... | collective-permute-start | bytes 245768 | tf_op jit(solution)/shard_map/ppermute | solution.py:467
  8.3 0.2 collective-permute-done.zlo_ref
  8.4 3.9 %collective-permute-done.1.zhi_ref = f32[10,16,128]{2,1,0:T(8,128)S(1)} collective-permute-done((f32[10,16,128]{2,1,0:T(8,128)S(1)}, f32[10,16,128]{2,1,0:T(8,128)S(1)}, u32[]{:S(2)}, u32[]{:S(2)}) %collective-permute-start.1) | collective-permute-done | bytes 81952 | tf_op jit(solution)/shard_map/ppermute | solution.py:467
  12.3 0.0 copy-done
  12.3 0.1 shard_map.69
  12.4 0.0 copy-start.4
  12.4 0.0 copy-start.3
  12.4 5.0 %collective-permute-start.2 = (f32[132,8,128]{2,1,0:T(8,128)S(1)}, f32[132,8,128]{2,1,0:T(8,128)S(1)}, u32[]{:S(2)}, u32[]{:S(2)}) collective-permute-start(f32[132,8,128]{2,1,0:T(8,128)S(1)} %get-tuple-element.20), channel_id=1, source_target_pairs={{0,16},{16,32},{32,48},{1,17},{17,33},{33,49},{2,18},{18,34},{34,5... | collective-permute-start | bytes 1622024 | tf_op jit(solution)/shard_map/ppermute | solution.py:467
  17.5 1.9 %collective-permute-start.3 = (f32[132,8,128]{2,1,0:T(8,128)S(1)}, f32[132,8,128]{2,1,0:T(8,128)S(1)}, u32[]{:S(2)}, u32[]{:S(2)}) collective-permute-start(f32[132,8,128]{2,1,0:T(8,128)S(1)} %get-tuple-element.21), channel_id=1, source_target_pairs={{16,0},{32,16},{48,32},{17,1},{33,17},{49,33},{18,2},{34,18},{50,3... | collective-permute-start | bytes 1622024 | tf_op jit(solution)/shard_map/ppermute | solution.py:467
  19.4 0.0 copy-done.4
  19.4 0.0 copy-done.3
  19.4 0.1 copy.10
  19.5 0.0 copy-start.2
  19.5 0.1 copy.12
  19.7 0.6 copy-done.2
  20.2 0.1 copy.11
  20.4 0.1 pad.3.clone
  20.4 0.1 maximum_maximum_fusion.data_ref
  20.5 0.8 shard_map.70
  21.3 2.4 %collective-permute-done.2.ylo_ref = f32[132,8,128]{2,1,0:T(8,128)S(1)} collective-permute-done((f32[132,8,128]{2,1,0:T(8,128)S(1)}, f32[132,8,128]{2,1,0:T(8,128)S(1)}, u32[]{:S(2)}, u32[]{:S(2)}) %collective-permute-start.2) | collective-permute-done | bytes 540704 | tf_op jit(solution)/shard_map/ppermute | solution.py:467
  23.7 4.7 %collective-permute-done.3.yhi_ref = f32[132,8,128]{2,1,0:T(8,128)S(1)} collective-permute-done((f32[132,8,128]{2,1,0:T(8,128)S(1)}, f32[132,8,128]{2,1,0:T(8,128)S(1)}, u32[]{:S(2)}, u32[]{:S(2)}) %collective-permute-start.3) | collective-permute-done | bytes 540704 | tf_op jit(solution)/shard_map/ppermute | solution.py:467
  28.4 0.1 shard_map.71
  28.6 4.1 %collective-permute-start.4 = (f32[242,8,128]{2,1,0:T(8,128)S(1)}, f32[242,8,128]{2,1,0:T(8,128)S(1)}, u32[]{:S(2)}, u32[]{:S(2)}) collective-permute-start(f32[242,8,128]{2,1,0:T(8,128)S(1)} %get-tuple-element.25), channel_id=1, source_target_pairs={{0,64},{64,128},{128,192},{192,256},{256,320},{320,384},{384,448},... | collective-permute-start | bytes 2973704 | tf_op jit(solution)/shard_map/ppermute | solution.py:467
  32.7 1.9 %collective-permute-start.5 = (f32[242,8,128]{2,1,0:T(8,128)S(1)}, f32[242,8,128]{2,1,0:T(8,128)S(1)}, u32[]{:S(2)}, u32[]{:S(2)}) collective-permute-start(f32[242,8,128]{2,1,0:T(8,128)S(1)} %get-tuple-element.26), channel_id=1, source_target_pairs={{64,0},{128,64},{192,128},{256,192},{320,256},{384,320},{448,384},... | collective-permute-start | bytes 2973704 | tf_op jit(solution)/shard_map/ppermute | solution.py:467
  34.6 0.1 copy.13
  34.7 29.6 %all_to_all.22 = f32[64,1,256]{2,1,0:T(1,128)S(1)} all-to-all(f32[64,1,256]{2,1,0:T(1,128)S(1)} %copy.13), channel_id=1, replica_groups=mesh['gx'=8,'gy'=4,'gz'=16] {'gy','gz'}, dimensions={0} | all-to-all | bytes 131072 | tf_op jit(solution)/shard_map/all_to_all | solution.py:502
  64.4 0.0 collective-permute-done.4.xlo_ref
  64.4 0.0 collective-permute-done.5.xhi_ref
  64.4 16.5 %shard_map.72 = (f32[6,16,16,128]{3,2,1,0:T(8,128)}, f32[64,128]{1,0:T(8,128)S(1)}) custom-call(f32[6,16,16,128]{3,2,1,0:T(8,128)S(1)} %copy-done, f32[16,16,128]{2,1,0:T(8,128)S(1)} %get-tuple-element.17.inv_ref.own_inv_ref, f32[10,16,128]{2,1,0:T(8,128)S(1)} %collective-permute-done.zlo_ref, f32[10,16,128]{2,1,0:T(8,128)S(1)} %collective-permute-done.1.zhi_ref, ...), custom_call_target="tpu_custom_call" | custom-call | flops 100000000 | bytes 1000000 | tf_op jit(solution)/shard_map/pallas_call | solution.py:73
  80.8 20.7 %all_to_all.23 = f32[64,1,128]{2,1,0:T(1,128)S(1)} all-to-all(f32[64,1,128]{2,1,0:T(1,128)S(1)} %bitcast.11), channel_id=1, replica_groups=mesh['gx'=8,'gy'=4,'gz'=16] {'gy','gz'}, dimensions={0} | all-to-all | bytes 65536 | tf_op jit(solution)/shard_map/all_to_all | solution.py:524
  101.5 1.0 shard_map.73
  (4 shorter events, 0.0 us)
Async XLA Ops:
  0.6 11.7 %copy-start = (f32[6,16,16,128]{3,2,1,0:T(8,128)S(1)}, f32[6,16,16,128]{3,2,1,0:T(8,128)}, u32[]{:S(2)}) copy-start(f32[6,16,16,128]{3,2,1,0:T(8,128)} %f_ref.5) | copy-start | bytes 2359300
  0.6 1.0 copy-start.1
  3.4 5.0 %collective-permute-start = (f32[10,16,128]{2,1,0:T(8,128)S(1)}, f32[10,16,128]{2,1,0:T(8,128)S(1)}, u32[]{:S(2)}, u32[]{:S(2)}) collective-permute-start(f32[10,16,128]{2,1,0:T(8,128)S(1)} %get-tuple-element.18), channel_id=1, source_target_pairs={{0,1},{1,2},{2,3},{3,4},{4,5},{5,6},{6,7},{7,8},{8,9},{9,10},{10,1... | collective-permute-start | bytes 245768 | tf_op jit(solution)/shard_map/ppermute | solution.py:467
  7.0 5.4 %collective-permute-start.1 = (f32[10,16,128]{2,1,0:T(8,128)S(1)}, f32[10,16,128]{2,1,0:T(8,128)S(1)}, u32[]{:S(2)}, u32[]{:S(2)}) collective-permute-start(f32[10,16,128]{2,1,0:T(8,128)S(1)} %get-tuple-element.19), channel_id=1, source_target_pairs={{1,0},{2,1},{3,2},{4,3},{5,4},{6,5},{7,6},{8,7},{9,8},{10,9},{11,1... | collective-permute-start | bytes 245768 | tf_op jit(solution)/shard_map/ppermute | solution.py:467
  12.4 7.0 %copy-start.4 = (s32[128,1]{0,1:T(1,128)S(1)}, s32[128,1]{0,1:T(1,128)}, u32[]{:S(2)}) copy-start(s32[128,1]{0,1:T(1,128)} %param.7) | copy-start | bytes 1540
  12.4 7.0 %copy-start.3 = (s32[128,3]{0,1:T(4,128)S(1)}, s32[128,3]{0,1:T(4,128)}, u32[]{:S(2)}) copy-start(s32[128,3]{0,1:T(4,128)} %param.8) | copy-start | bytes 4612
  12.4 11.3 %collective-permute-start.2 = (f32[132,8,128]{2,1,0:T(8,128)S(1)}, f32[132,8,128]{2,1,0:T(8,128)S(1)}, u32[]{:S(2)}, u32[]{:S(2)}) collective-permute-start(f32[132,8,128]{2,1,0:T(8,128)S(1)} %get-tuple-element.20), channel_id=1, source_target_pairs={{0,16},{16,32},{32,48},{1,17},{17,33},{33,49},{2,18},{18,34},{34,5... | collective-permute-start | bytes 1622024 | tf_op jit(solution)/shard_map/ppermute | solution.py:467
  17.5 11.0 %collective-permute-start.3 = (f32[132,8,128]{2,1,0:T(8,128)S(1)}, f32[132,8,128]{2,1,0:T(8,128)S(1)}, u32[]{:S(2)}, u32[]{:S(2)}) collective-permute-start(f32[132,8,128]{2,1,0:T(8,128)S(1)} %get-tuple-element.21), channel_id=1, source_target_pairs={{16,0},{32,16},{48,32},{17,1},{33,17},{49,33},{18,2},{34,18},{50,3... | collective-permute-start | bytes 1622024 | tf_op jit(solution)/shard_map/ppermute | solution.py:467
  19.5 0.7 copy-start.2
  28.6 35.8 %collective-permute-start.4 = (f32[242,8,128]{2,1,0:T(8,128)S(1)}, f32[242,8,128]{2,1,0:T(8,128)S(1)}, u32[]{:S(2)}, u32[]{:S(2)}) collective-permute-start(f32[242,8,128]{2,1,0:T(8,128)S(1)} %get-tuple-element.25), channel_id=1, source_target_pairs={{0,64},{64,128},{128,192},{192,256},{256,320},{320,384},{384,448},... | collective-permute-start | bytes 2973704 | tf_op jit(solution)/shard_map/ppermute | solution.py:467
  32.7 31.6 %collective-permute-start.5 = (f32[242,8,128]{2,1,0:T(8,128)S(1)}, f32[242,8,128]{2,1,0:T(8,128)S(1)}, u32[]{:S(2)}, u32[]{:S(2)}) collective-permute-start(f32[242,8,128]{2,1,0:T(8,128)S(1)} %get-tuple-element.26), channel_id=1, source_target_pairs={{64,0},{128,64},{192,128},{256,192},{320,256},{384,320},{448,384},... | collective-permute-start | bytes 2973704 | tf_op jit(solution)/shard_map/ppermute | solution.py:467

commit v5 on v4

--- a/solution.py
+++ b/solution.py
@@ -13,6 +13,7 @@
 ZGROUPS = CX // 2 + 2
 XW = CX + 2 * GX
 STRIDE = 20
+ROWS = 4
 EXACT = lax.Precision.HIGHEST
 F32 = jnp.float32
 
@@ -72,7 +73,9 @@
     many = isinstance(outs, list)
     return pl.pallas_call(
         body,
-        out_shape=[jax.ShapeDtypeStruct(s, F32) for s in outs] if many else jax.ShapeDtypeStruct(outs, F32),
+        out_shape=[jax.ShapeDtypeStruct(s, jnp.bfloat16 if s == (4, 256, 256) else F32) for s in outs]
+        if many
+        else jax.ShapeDtypeStruct(outs, F32),
         in_specs=[pl.BlockSpec(memory_space=space)] * len(ins),
         out_specs=[pl.BlockSpec(memory_space=first)] + vmem(len(outs) - 1) if many else vmem(1)[0],
         scratch_shapes=list(scratch),
@@ -122,10 +125,10 @@
             out[PAIRS + ZGROUPS + g] = zhi_ref[g, rows]
 
 
-def z_ends(lo, hi, s, lane):
+def z_ends(lo, hi, s, lane, t, total):
     first = lane < GZ * (s + 1) if s < 11 else (lane >= GZ * s) & (lane < GZ * (s + 1))
-    moved = roll(jnp.where(first, lo, hi), CZ - GZ - GZ * s, 1)
-    return jnp.where((lane < GZ) | (lane >= CZ - GZ), moved, 0.0)
+    moved = roll(jnp.where(first, lo, hi), 32 * t - GZ * s, 1)
+    return jnp.where((lane >= 32 * t) & (lane < 32 * t + 2 * GZ), moved, total)
 
 
 def pack_x(f_ref, inv_ref, zlo_ref, zhi_ref, ylo_ref, yhi_ref, lo_ref, hi_ref):
@@ -154,66 +157,62 @@
             out[n] = end_of(g, t, e)
 
 
-def taylor(source, inv_ref, band, x, tiles, scale, put, comps=(0, 1, 2, 3, 4, 5), skip=0):
-    row = rows_of((8, CZ))
-    def load(half, c, t, d=0, e=0):
-        return source[half, c, x + d - skip, band_of(t, e)]
+def taylor(source, packed, inv_main, inv_packed, band, xs, tiles, scale, put, comps=(0, 1, 2, 3, 4, 5), skip=0):
+    fields = [c for c in (4, 3, 1, 0) if {4: 0, 3: 1, 1: 3, 0: 4}[c] in comps]
+    keys = [(i, c) for i in range(len(xs)) for c in fields]
+    ghosts = three_parts(jnp.concatenate([packed[c, xs[i] - skip, pl.ds(8, 8)] for i, c in keys], axis=0))
+    along_z = {}
+    for t in tiles:
+        mains = three_parts(jnp.concatenate([source[c, xs[i] - skip, band_of(t)] for i, c in keys], axis=0))
+        left = [part for n in (2, 1, 0) for part in (mains[n], ghosts[n])]
+        total = jnp.dot(jnp.concatenate(left, axis=1), jnp.concatenate([band[t]] * 3, axis=0), preferred_element_type=F32)
+        for n, key in enumerate(keys):
+            along_z[key + (t,)] = total[8 * n:8 * n + 8, 0:128]
+            part = total[8 * n:8 * n + 8, 128:256]
+            along_z[key + (4,)] = along_z[key + (4,)] + part if key + (4,) in along_z else part
+    for i, x in enumerate(xs):
+        for t in tuple(tiles) + (4,):
+            one_tile(packed if t == 4 else source, inv_packed if t == 4 else inv_main, along_z, i, x, t, scale, put, comps, skip)
+
+
+def one_tile(source, inv_ref, along_z, i, x, t, scale, put, comps, skip):
+    def load(c, d=0, e=0):
+        return source[c, x + d - skip, pl.ds(8 + e, 8) if t == 4 else band_of(t, e)]
 
     def dx(c):
-        return {
-            (half, t): (
-                load(half, c, t, 1) - load(half, c, t, -1),
-                load(half, c, t, 2) - load(half, c, t, -2),
-            )
-            for half in (0, 1)
-            for t in tiles
-        }
+        return load(c, 1) - load(c, -1), load(c, 2) - load(c, -2)
 
     def dy(c):
-        return {
-            (half, t): (
-                load(half, c, t, 0, 1) - load(half, c, t, 0, -1),
-                load(half, c, t, 0, 2) - load(half, c, t, 0, -2),
-            )
-            for half in (0, 1)
-            for t in tiles
-        }
-
-    def all_dz(fields):
-        block = jnp.concatenate(
-            [jnp.concatenate([load(0, c, t), load(1, c, t)], axis=1) for c in fields for t in tiles], axis=0
-        )
-        high, middle, low = three_parts(block)
-        total = jnp.dot(
-            jnp.concatenate([low, middle, high], axis=1), band[...], preferred_element_type=F32
-        )
-        out = {}
-        for i, c in enumerate(fields):
-            for j, t in enumerate(tiles):
-                start = 8 * (i * len(tiles) + j)
-                for half in (0, 1):
-                    out[c, half, t] = total[start:start + 8, 128 * half:128 * half + 128]
-        return out
+        return load(c, 0, 1) - load(c, 0, -1), load(c, 0, 2) - load(c, 0, -2)
 
     pairs = ((dy, 5, 4, 0), (None, 3, 5, dx), (dx, 4, 3, dy), (None, 1, 2, dy), (dx, 2, 0, 0), (dy, 0, 1, dx))
-    along_z = all_dz([c for c in (4, 3, 1, 0) if {4: 0, 3: 1, 1: 3, 0: 4}[c] in comps])
-    factors = {}
-    for half in (0, 1):
-        for t in tiles:
-            inv = inv_ref[half, 6, x, band_of(t)]
-            factors[half, t] = (inv * scale, jnp.where(inv > 0.0, scale, 0.0))
+    inv = inv_ref[6, x, pl.ds(8, 8) if t == 4 else band_of(t)]
+    factors = (inv * scale, jnp.where(inv > 0.0, scale, 0.0))
     for c in comps:
         first, c1, c2, second = pairs[c]
-        plus = first(c1) if first else None
-        minus = second(c2) if second else None
-        for key in factors:
-            if plus and minus:
-                rate = 8.0 * (plus[key][0] - minus[key][0]) - (plus[key][1] - minus[key][1])
-            elif plus:
-                rate = 8.0 * plus[key][0] - plus[key][1] - along_z[(c2,) + key]
-            else:
-                rate = along_z[(c1,) + key] - (8.0 * minus[key][0] - minus[key][1])
-            put(key[0], c, key[1], factors[key][c // 3] * rate)
+        if first and second:
+            plus, minus = first(c1), second(c2)
+            rate = 8.0 * (plus[0] - minus[0]) - (plus[1] - minus[1])
+        elif first:
+            plus = first(c1)
+            rate = 8.0 * plus[0] - plus[1] - along_z[i, c2, t]
+        else:
+            minus = second(c2)
+            rate = along_z[i, c1, t] - (8.0 * minus[0] - minus[1])
+        put(c, x, t, factors[c // 3] * rate)
+
+
+def store_packed(ref, c, x, value):
+    ref[c, x, pl.ds(8, 8)] = value
+    if c in (0, 2, 3, 5):
+        ref[c, x, pl.ds(0, 8)] = roll(value, 32, 1)
+        ref[c, x, pl.ds(16, 8)] = roll(value, -32, 1)
+
+
+def packed_z(lane, t):
+    place = lane - 32 * t
+    inside = (place >= 0) & (place < 2 * GZ)
+    return jnp.where(inside, jnp.where(place < GZ, place - GZ, place + (CZ - GZ)), -1000)
 
 
 def dot(a, b, da=1, db=0):
@@ -243,9 +242,9 @@
 
 
 def compute(
-    f_ref, own_inv_ref, zlo_ref, zhi_ref, ylo_ref, yhi_ref, xlo_ref, xhi_ref, req_ref,
+    f_ref, own_inv_ref, zlo_ref, zhi_ref, ylo_ref, yhi_ref, xlo_ref, xhi_ref, req_ref, band,
     new_ref, ans_ref,
-    full, t1, t2, t3, acc, words, wz, wxy, spill, edge_rows, parts, band, sems,
+    full, full_p, t1, t2, t3, p1, p2, p3, acc, acc_p, words, wz, wxy, spill, edge_rows, parts, sems,
 ):
     lane = lanes((8, CZ))
     row = rows_of((8, CZ))
@@ -253,13 +252,18 @@
     for p in range(PAIRS):
         c, x = divmod(p, CX)
         g, s = z_slot(c, x)
-        for t in (1, 2):
-            own = pl.ds(8 * (t - 1), 8)
-            full[0, c, GX + x, band_of(t)] = f_ref[c, x, own] if c < 6 else own_inv_ref[x, own]
-            full[1, c, GX + x, band_of(t)] = z_ends(zlo_ref[g, own], zhi_ref[g, own], s, lane)
-        for ref, t in ((ylo_ref, 0), (yhi_ref, 3)):
-            full[0, c, GX + x, band_of(t)] = ref[p]
-            full[1, c, GX + x, band_of(t)] = z_ends(ref[PAIRS + g], ref[PAIRS + ZGROUPS + g], s, lane)
+        total = zero
+        for t in (0, 1, 2, 3):
+            if t in (1, 2):
+                own = pl.ds(8 * (t - 1), 8)
+                full[c, GX + x, band_of(t)] = f_ref[c, x, own] if c < 6 else own_inv_ref[x, own]
+                lo, hi = zlo_ref[g, own], zhi_ref[g, own]
+            else:
+                ref = ylo_ref if t == 0 else yhi_ref
+                full[c, GX + x, band_of(t)] = ref[p]
+                lo, hi = ref[PAIRS + g], ref[PAIRS + ZGROUPS + g]
+            total = z_ends(lo, hi, s, lane, t, total)
+        store_packed(full_p, c, GX + x, total)
     for side in (0, 1):
         ref = xhi_ref if side == 0 else xlo_ref
         where_main = {key: n for n, key in enumerate(XMAIN)}
@@ -270,69 +274,68 @@
                     continue
                 g, s = z_slot(c, k - 1 if side == 0 else CX - k)
                 q = 5 if c == 6 else (k - 1) // 2
-                done = set()
+                mains = [zero, zero, zero, zero]
+                total = zero
                 for t in (0, 1, 2, 3, 4):
-                    pair = [None, None]
                     if (k, c, t) in where_main:
-                        pair[0] = ref[where_main[k, c, t]]
+                        value = ref[where_main[k, c, t]]
+                        if t == 4:
+                            mains[0], mains[3] = jnp.where(row >= 4, value, 0.0), jnp.where(row >= 4, 0.0, value)
+                        else:
+                            mains[t] = value
                     if (q, t, 0) in XEND:
-                        pair[1] = z_ends(ref[XEND[q, t, 0]], ref[XEND[q, t, 1]], s, lane)
-                    for half in (0, 1):
-                        if pair[half] is None:
-                            continue
+                        lo, hi = ref[XEND[q, t, 0]], ref[XEND[q, t, 1]]
                         if t == 4:
-                            full[half, c, x, band_of(0)] = jnp.where(row >= 4, pair[half], 0.0)
-                            full[half, c, x, band_of(3)] = jnp.where(row >= 4, 0.0, pair[half])
-                            done |= {(half, 0), (half, 3)}
+                            top = z_ends(lo, hi, s, lane, 0, zero)
+                            bottom = z_ends(lo, hi, s, lane, 3, zero)
+                            total = total + jnp.where(row >= 4, top, bottom)
                         else:
-                            full[half, c, x, band_of(t)] = pair[half]
-                            done.add((half, t))
-                for half in (0, 1):
-                    for t in (0, 3):
-                        if (half, t) not in done:
-                            full[half, c, x, band_of(t)] = zero
-
-    ring = (rows_of((256, 256)) - lanes((256, 256)) + 256) % 256
-    one = lambda d: (ring == d % 256).astype(F32)
-    stencil = (8.0 * (one(1) - one(-1)) + one(-2) - one(2)).astype(jnp.bfloat16)
-    for i in range(3):
-        band[pl.ds(256 * i, 256), :] = stencil
-
-    for power, source, target in ((1, full, t1), (2, t1, t2), (3, t2, t3)):
-        scale = STEP / power / 12.0
-
-        def body(x, carry, source=source, target=target, scale=scale, power=power):
-            def put(half, c, t, value):
-                target[half, c, x - 2 * power, band_of(t)] = value
-
-            taylor(source, full, band, x, (0, 1, 2, 3), scale, put, skip=2 * power - 2)
+                            total = z_ends(lo, hi, s, lane, t, total)
+                for t in range(4):
+                    full[c, x, band_of(t)] = mains[t]
+                store_packed(full_p, c, x, total)
+
+    for power, source, packed, target, target_p in (
+        (1, full, full_p, t1, p1), (2, t1, p1, t2, p2), (3, t2, p2, t3, p3)
+    ):
+        scale, skip = STEP / power / 12.0, 2 * power - 2
+
+        def put(c, x, t, value, target=target, target_p=target_p, power=power):
+            if t == 4:
+                store_packed(target_p, c, x - 2 * power, value)
+            else:
+                target[c, x - 2 * power, band_of(t)] = value
+
+        def body(i, carry, source=source, packed=packed, scale=scale, skip=skip, put=put, power=power):
+            xs = [2 * power + 2 + ROWS * i + j for j in range(ROWS)]
+            taylor(source, packed, full, full_p, band, xs, (0, 1, 2, 3), scale, put, skip=skip)
             return carry
 
-        def edge(i, carry, source=source, target=target, scale=scale, power=power):
-            x = jnp.where(i < 2, 2 * power + i, XW - 2 * power - 4 + i)
-
-            def put(half, c, t, value):
-                target[half, c, x - 2 * power, band_of(t)] = value
-
-            taylor(source, full, band, x, (1, 2), scale, put, (1, 2, 4, 5), skip=2 * power - 2)
-            return carry
-
-        lax.fori_loop(0, 4, edge, 0, unroll=2)
-        lax.fori_loop(2 * power + 2, XW - 2 * power - 2, body, 0, unroll=4)
-
-    def last(x, carry):
-        def put(half, c, t, value):
-            total = full[half, c, x, band_of(t)] + t1[half, c, x - 2, band_of(t)]
-            total = total + t2[half, c, x - 4, band_of(t)]
-            total = total + t3[half, c, x - 6, band_of(t)]
-            acc[half, c, x - 8, t - 1] = total + value
-
-        taylor(t3, full, band, x, (1, 2), STEP / 4 / 12.0, put, skip=6)
+        ends = [2 * power, 2 * power + 1, XW - 2 * power - 2, XW - 2 * power - 1]
+        taylor(source, packed, full, full_p, band, ends, (1, 2), scale, put, (1, 2, 4, 5), skip)
+        lax.fori_loop(0, (XW - 4 * power - 4) // ROWS, body, 0)
+
+    def finish(c, x, t, value):
+        if t == 4:
+            terms = [ref[c, x - d, pl.ds(8, 8)] for ref, d in ((full_p, 0), (p1, 2), (p2, 4), (p3, 6))]
+        else:
+            terms = [ref[c, x - d, band_of(t)] for ref, d in ((full, 0), (t1, 2), (t2, 4), (t3, 6))]
+        total = terms[0] + terms[1]
+        total = total + terms[2]
+        total = total + terms[3] + value
+        if t == 4:
+            acc_p[c, x - 8] = total
+        else:
+            acc[c, x - 8, t - 1] = total
+
+    def last(i, carry):
+        xs = [8 + ROWS * i + j for j in range(ROWS)]
+        taylor(t3, p3, full, full_p, band, xs, (1, 2), STEP / 4 / 12.0, finish, skip=6)
         return carry
 
-    lax.fori_loop(8, XW - 8, last, 0, unroll=4)
+    lax.fori_loop(0, (XW - 16) // ROWS, last, 0)
     writes = [
-        pltpu.make_async_copy(acc.at[0, :, pl.ds(2, CX), t], new_ref.at[:, :, pl.ds(8 * t, 8), :], sems.at[t])
+        pltpu.make_async_copy(acc.at[:, pl.ds(2, CX), t], new_ref.at[:, :, pl.ds(8 * t, 8), :], sems.at[t])
         for t in (0, 1)
     ]
     for write in writes:
@@ -363,10 +366,11 @@
                 total = jnp.where(away == float(i), values[i], total)
             return total
 
-        wz[kind, pl.ds(0, CZ), columns] = weights(cell + 2.0, bz, wz_rows)
-        wz[kind, pl.ds(CZ, CZ), columns] = jnp.zeros((CZ, 128), F32)
-        wz[kind, pl.ds(CZ, 8), columns] = weights(low + (CZ + 2.0), bz, wz_rows)
-        wz[kind, pl.ds(2 * CZ - 8, 8), columns] = weights(low - 6.0, bz, wz_rows)
+        for t in ((1, 2), (2,), (1,))[kind]:
+            use = (0, 1)[t - 1] if kind == 0 else kind + 1
+            wz[use, pl.ds(0, CZ), columns] = weights(cell + 2.0, bz, wz_rows)
+            ghost_z = packed_z(rows_of((CZ, 128)), t).astype(F32)
+            wz[use, pl.ds(CZ, CZ), columns] = weights(ghost_z + 2.0, bz, wz_rows)
         in_x = [weights(jnp.full((1, 128), float(x), F32), bx, wx) for x in range(CX + 4)] if kind == 0 else []
         if kind == 0:
             for t in (0, 1):
@@ -386,21 +390,27 @@
                 for g in range(CX // 4 + 1):
                     total = None
                     for i in range(4):
-                        tile = acc[half, c, 4 * g + i, 1 - kind]
-                        moved = roll(tile, 2 * i - (6 if kind == 0 else 0), 0)
+                        value = acc_p[c, 4 * g + i] if half else acc[c, 4 * g + i, 1 - kind]
+                        moved = roll(value, 2 * i - (6 if kind == 0 else 0), 0)
                         total = moved if total is None else jnp.where(row >= 2 * i, moved, total)
                     edge_rows[kind, half, c, g] = total
 
     parts[...] = jnp.zeros((48, 128), F32)
-    for kind in range(3):
-        grid = [acc[half] if kind == 0 else edge_rows[kind - 1, half] for half in (0, 1)]
-        weight = wxy[...].reshape(-1, 256) if kind == 0 else spill[kind - 1].reshape(-1, 256)
-        along = split_dot(jnp.concatenate([g.reshape(-1, CZ) for g in grid], axis=1), wz[kind])
+    sums = {}
+    for use in range(4):
+        kind = max(use - 1, 0)
+        if kind == 0:
+            grid, weight = [acc[:, :, use], acc_p[...]], wxy[:, use].reshape(-1, 256)
+        else:
+            grid, weight = [edge_rows[kind - 1, half] for half in (0, 1)], spill[kind - 1].reshape(-1, 256)
+        along = split_dot(jnp.concatenate([g.reshape(-1, CZ) for g in grid], axis=1), wz[use])
         count = weight.shape[0]
         for c in range(6):
             total = jnp.sum(along[c * count:c * count + count] * weight, axis=0, keepdims=True)
-            for at in (0, 1):
-                parts[pl.ds((2 * kind + at) * 8 + c, 1), :] = total[:, 128 * at:128 * at + 128]
+            sums[kind, c] = sums[kind, c] + total if (kind, c) in sums else total
+    for (kind, c), total in sums.items():
+        for at in (0, 1):
+            parts[pl.ds((2 * kind + at) * 8 + c, 1), :] = total[:, 128 * at:128 * at + 128]
     values = parts[...]
     blank = jnp.zeros((16, 128), F32)
     filled = jnp.concatenate([values, blank], axis=0)
@@ -412,7 +422,17 @@
         write.wait()
 
 
-def requests(data_ref, send_ref, pick_ref, rank_ref):
+def requests(data_ref, send_ref, pick_ref, rank_ref, band_ref):
+    for t in range(4):
+        def places(index):
+            return jnp.where(index < CZ, index, packed_z(index - CZ, t))
+
+        apart = places(rows_of((256, 256))) - places(lanes((256, 256)))
+        real = (places(rows_of((256, 256))) > -900) & (places(lanes((256, 256))) > -900)
+        one = lambda d: ((apart == d) & real).astype(F32)
+        stencil = (8.0 * (one(1) - one(-1)) + one(-2) - one(2)).astype(jnp.bfloat16)
+        band_ref[t] = stencil
+
     data = data_ref[...]
     wide = (128, 128)
     owner = jnp.broadcast_to(data[:, 18:19], wide)
@@ -496,26 +516,28 @@
     ylo, yhi = shift_both(ylo, yhi, "gy")
     xshape = (XTOTAL, 8, CZ)
     xlo, xhi = call(pack_x, [xshape, xshape], (fields, inv, zlo, zhi, ylo, yhi), 8)
-    send, pick, rank = call(requests, [(64, 256), (3, 64, 128), (8, 128)], (data,), 8)
+    send, pick, rank, band = call(requests, [(64, 256), (3, 64, 128), (8, 128), (4, 256, 256)], (data,), 8)
     send, xlo, xhi = lax.optimization_barrier((send, xlo, xhi))
     xlo, xhi = shift_both(xlo, xhi, "gx")
     req = lax.all_to_all(send, ("gy", "gz"), 0, 0, tiled=True)
     new_fields, answers = call(
         compute,
         [(6, CX, CY, CZ), (64, 128)],
-        (fields, inv, zlo, zhi, ylo, yhi, xlo, xhi, req),
-        46,
+        (fields, inv, zlo, zhi, ylo, yhi, xlo, xhi, req, band),
+        40,
         scratch=[
-            pltpu.VMEM((2, NF, XW, 48, CZ), F32),
-            *[pltpu.VMEM((2, 6, XW - 4 * m, 48, CZ), F32) for m in (1, 2, 3)],
-            pltpu.VMEM((2, 6, CX + 4, 2, 8, CZ), F32),
+            pltpu.VMEM((NF, XW, 48, CZ), F32),
+            pltpu.VMEM((NF, XW, 24, CZ), F32),
+            *[pltpu.VMEM((6, XW - 4 * m, 48, CZ), F32) for m in (1, 2, 3)],
+            *[pltpu.VMEM((6, XW - 4 * m, 24, CZ), F32) for m in (1, 2, 3)],
+            pltpu.VMEM((6, CX + 4, 2, 8, CZ), F32),
+            pltpu.VMEM((6, CX + 4, 8, CZ), F32),
             pltpu.VMEM((2, 256, 128), F32),
-            pltpu.VMEM((3, 256, 256), F32),
+            pltpu.VMEM((4, 256, 256), F32),
             pltpu.VMEM((CX + 4, 2, 8, 256), F32),
             pltpu.VMEM((2, CX // 4 + 1, 8, 256), F32),
             pltpu.VMEM((2, 2, 6, CX // 4 + 1, 8, CZ), F32),
             pltpu.VMEM((48, 128), F32),
-            pltpu.VMEM((768, 256), jnp.bfloat16),
             pltpu.SemaphoreType.DMA((2,)),
         ],
         flops=100000000,

time: 103 us -> 109 us (1.058)
  Pallas kernels: 20.2 us -> 26.9 us
    pallas_call x6, Pallas kernels: 20.2 us -> 26.9 us  [call(): pl.pallas_call(body, out_shape=[jax.ShapeDtypeStruct(s, jnp.bfloat16 if s...]
where the time goes in v5:
time: 109 us
  blocking collectives  50.3 us (46%)
  Pallas kernels  26.9 us (25%)
  starting transfers between devices  17.8 us (16%)
  waiting for transfers between devices  11 us (10%)
  local copies, waits for them, and re-layouts  2.05 us (2%)
    all_to_all x1, blocking collectives, local(): req = lax.all_to_all(send, ('gy', 'gz'), 0, 0, tiled=True)  29.6 us
    pallas_call x6, Pallas kernels, call(): pl.pallas_call(body, out_shape=[jax.ShapeDtypeStruct(s, jnp.bfloat16 if s...  26.9 us
    all_to_all x1, blocking collectives, local(): answers = lax.all_to_all(answers, ('gy', 'gz'), 0, 0, tiled=True)  20.7 us
    ppermute x3, starting transfers between devices, shift_both(): lax.ppermute(high_edge, axis, up)  12.7 us
    ppermute x3, waiting for transfers between devices, shift_both(): lax.ppermute(low_edge, axis, down)  8.6 us
    ppermute x3, starting transfers between devices, shift_both(): lax.ppermute(low_edge, axis, down)  5.13 us
    ppermute x3, waiting for transfers between devices, shift_both(): lax.ppermute(high_edge, axis, up)  2.43 us
  transfers between devices with their start and end apart: 6, of which 4 were waited for; matrix products, arithmetic and copies ran while one was open for 1% of the time, Pallas kernels for 1%

profile of v5, /device:TPU:7, one launch (start us, length us, event | category | flops | bytes accessed | tf_op | source)
XLA Modules:
  0.0 109.0 jit_solution(12492957017330492930)
XLA Ops:
  0.6 0.0 copy-start
  0.6 0.0 copy-start.1
  0.6 1.0 copy-done.1
  1.6 1.8 %shard_map.68 = (f32[10,16,128]{2,1,0:T(8,128)S(1)}, f32[10,16,128]{2,1,0:T(8,128)S(1)}, f32[16,16,128]{2,1,0:T(8,128)S(1)}) custom-call(f32[6,16,16,128]{3,2,1,0:T(8,128)} %f_ref.5, f32[16,16,128]{2,1,0:T(8,128)S(1)} %copy-done.1), custom_call_target="tpu_custom_call" | custom-call | flops 1000000 | bytes 1000000 | tf_op jit(solution)/shard_map/pallas_call | solution.py:74
  3.4 3.5 %collective-permute-start = (f32[10,16,128]{2,1,0:T(8,128)S(1)}, f32[10,16,128]{2,1,0:T(8,128)S(1)}, u32[]{:S(2)}, u32[]{:S(2)}) collective-permute-start(f32[10,16,128]{2,1,0:T(8,128)S(1)} %get-tuple-element.19), channel_id=1, source_target_pairs={{0,1},{1,2},{2,3},{3,4},{4,5},{5,6},{6,7},{7,8},{8,9},{9,10},{10,1... | collective-permute-start | bytes 245768 | tf_op jit(solution)/shard_map/ppermute | solution.py:487
  7.0 1.3 %collective-permute-start.1 = (f32[10,16,128]{2,1,0:T(8,128)S(1)}, f32[10,16,128]{2,1,0:T(8,128)S(1)}, u32[]{:S(2)}, u32[]{:S(2)}) collective-permute-start(f32[10,16,128]{2,1,0:T(8,128)S(1)} %get-tuple-element.20), channel_id=1, source_target_pairs={{1,0},{2,1},{3,2},{4,3},{5,4},{6,5},{7,6},{8,7},{9,8},{10,9},{11,1... | collective-permute-start | bytes 245768 | tf_op jit(solution)/shard_map/ppermute | solution.py:487
  8.3 0.2 collective-permute-done.zlo_ref
  8.4 3.9 %collective-permute-done.1.zhi_ref = f32[10,16,128]{2,1,0:T(8,128)S(1)} collective-permute-done((f32[10,16,128]{2,1,0:T(8,128)S(1)}, f32[10,16,128]{2,1,0:T(8,128)S(1)}, u32[]{:S(2)}, u32[]{:S(2)}) %collective-permute-start.1) | collective-permute-done | bytes 81952 | tf_op jit(solution)/shard_map/ppermute | solution.py:487
  12.3 0.0 copy-done
  12.3 0.1 shard_map.69
  12.4 0.0 copy-start.4
  12.4 0.0 copy-start.3
  12.4 5.0 %collective-permute-start.2 = (f32[132,8,128]{2,1,0:T(8,128)S(1)}, f32[132,8,128]{2,1,0:T(8,128)S(1)}, u32[]{:S(2)}, u32[]{:S(2)}) collective-permute-start(f32[132,8,128]{2,1,0:T(8,128)S(1)} %get-tuple-element.21), channel_id=1, source_target_pairs={{0,16},{16,32},{32,48},{1,17},{17,33},{33,49},{2,18},{18,34},{34,5... | collective-permute-start | bytes 1622024 | tf_op jit(solution)/shard_map/ppermute | solution.py:487
  17.5 1.9 %collective-permute-start.3 = (f32[132,8,128]{2,1,0:T(8,128)S(1)}, f32[132,8,128]{2,1,0:T(8,128)S(1)}, u32[]{:S(2)}, u32[]{:S(2)}) collective-permute-start(f32[132,8,128]{2,1,0:T(8,128)S(1)} %get-tuple-element.22), channel_id=1, source_target_pairs={{16,0},{32,16},{48,32},{17,1},{33,17},{49,33},{18,2},{34,18},{50,3... | collective-permute-start | bytes 1622024 | tf_op jit(solution)/shard_map/ppermute | solution.py:487
  19.4 0.0 copy-done.4
  19.4 0.0 copy-done.3
  19.4 0.1 copy.10
  19.5 0.0 copy-start.2
  19.5 0.1 copy.12
  19.7 0.6 copy-done.2
  20.2 0.1 copy.11
  20.4 0.1 pad.3.clone
  20.4 0.1 maximum_maximum_fusion.data_ref
  20.5 0.9 shard_map.70
  21.5 2.3 %collective-permute-done.2.ylo_ref = f32[132,8,128]{2,1,0:T(8,128)S(1)} collective-permute-done((f32[132,8,128]{2,1,0:T(8,128)S(1)}, f32[132,8,128]{2,1,0:T(8,128)S(1)}, u32[]{:S(2)}, u32[]{:S(2)}) %collective-permute-start.2) | collective-permute-done | bytes 540704 | tf_op jit(solution)/shard_map/ppermute | solution.py:487
  23.7 4.7 %collective-permute-done.3.yhi_ref = f32[132,8,128]{2,1,0:T(8,128)S(1)} collective-permute-done((f32[132,8,128]{2,1,0:T(8,128)S(1)}, f32[132,8,128]{2,1,0:T(8,128)S(1)}, u32[]{:S(2)}, u32[]{:S(2)}) %collective-permute-start.3) | collective-permute-done | bytes 540704 | tf_op jit(solution)/shard_map/ppermute | solution.py:487
  28.4 0.1 shard_map.71
  28.6 4.1 %collective-permute-start.4 = (f32[242,8,128]{2,1,0:T(8,128)S(1)}, f32[242,8,128]{2,1,0:T(8,128)S(1)}, u32[]{:S(2)}, u32[]{:S(2)}) collective-permute-start(f32[242,8,128]{2,1,0:T(8,128)S(1)} %get-tuple-element.26), channel_id=1, source_target_pairs={{0,64},{64,128},{128,192},{192,256},{256,320},{320,384},{384,448},... | collective-permute-start | bytes 2973704 | tf_op jit(solution)/shard_map/ppermute | solution.py:487
  32.7 1.9 %collective-permute-start.5 = (f32[242,8,128]{2,1,0:T(8,128)S(1)}, f32[242,8,128]{2,1,0:T(8,128)S(1)}, u32[]{:S(2)}, u32[]{:S(2)}) collective-permute-start(f32[242,8,128]{2,1,0:T(8,128)S(1)} %get-tuple-element.27), channel_id=1, source_target_pairs={{64,0},{128,64},{192,128},{256,192},{320,256},{384,320},{448,384},... | collective-permute-start | bytes 2973704 | tf_op jit(solution)/shard_map/ppermute | solution.py:487
  34.6 0.1 copy.13
  34.7 29.6 %all_to_all.22 = f32[64,1,256]{2,1,0:T(1,128)S(1)} all-to-all(f32[64,1,256]{2,1,0:T(1,128)S(1)} %copy.13), channel_id=1, replica_groups=mesh['gx'=8,'gy'=4,'gz'=16] {'gy','gz'}, dimensions={0} | all-to-all | bytes 131072 | tf_op jit(solution)/shard_map/all_to_all | solution.py:522
  64.4 0.0 collective-permute-done.4.xlo_ref
  64.4 0.0 collective-permute-done.5.xhi_ref
  64.4 23.0 %shard_map.72 = (f32[6,16,16,128]{3,2,1,0:T(8,128)}, f32[64,128]{1,0:T(8,128)S(1)}) custom-call(f32[6,16,16,128]{3,2,1,0:T(8,128)S(1)} %copy-done, f32[16,16,128]{2,1,0:T(8,128)S(1)} %get-tuple-element.18.inv_ref.own_inv_ref, f32[10,16,128]{2,1,0:T(8,128)S(1)} %collective-permute-done.zlo_ref, f32[10,16,128]{2,1,0:T(8,128)S(1)} %collective-permute-done.1.zhi_ref, ...), custom_call_target="tpu_custom_call" | custom-call | flops 100000000 | bytes 1000000 | tf_op jit(solution)/shard_map/pallas_call | solution.py:74
  87.4 20.7 %all_to_all.23 = f32[64,1,128]{2,1,0:T(1,128)S(1)} all-to-all(f32[64,1,128]{2,1,0:T(1,128)S(1)} %bitcast.11), channel_id=1, replica_groups=mesh['gx'=8,'gy'=4,'gz'=16] {'gy','gz'}, dimensions={0} | all-to-all | bytes 65536 | tf_op jit(solution)/shard_map/all_to_all | solution.py:546
  108.0 1.0 shard_map.73
  (4 shorter events, 0.0 us)
Async XLA Ops:
  0.6 11.7 %copy-start = (f32[6,16,16,128]{3,2,1,0:T(8,128)S(1)}, f32[6,16,16,128]{3,2,1,0:T(8,128)}, u32[]{:S(2)}) copy-start(f32[6,16,16,128]{3,2,1,0:T(8,128)} %f_ref.5) | copy-start | bytes 2359300
  0.6 1.0 copy-start.1
  3.4 5.0 %collective-permute-start = (f32[10,16,128]{2,1,0:T(8,128)S(1)}, f32[10,16,128]{2,1,0:T(8,128)S(1)}, u32[]{:S(2)}, u32[]{:S(2)}) collective-permute-start(f32[10,16,128]{2,1,0:T(8,128)S(1)} %get-tuple-element.19), channel_id=1, source_target_pairs={{0,1},{1,2},{2,3},{3,4},{4,5},{5,6},{6,7},{7,8},{8,9},{9,10},{10,1... | collective-permute-start | bytes 245768 | tf_op jit(solution)/shard_map/ppermute | solution.py:487
  7.0 5.4 %collective-permute-start.1 = (f32[10,16,128]{2,1,0:T(8,128)S(1)}, f32[10,16,128]{2,1,0:T(8,128)S(1)}, u32[]{:S(2)}, u32[]{:S(2)}) collective-permute-start(f32[10,16,128]{2,1,0:T(8,128)S(1)} %get-tuple-element.20), channel_id=1, source_target_pairs={{1,0},{2,1},{3,2},{4,3},{5,4},{6,5},{7,6},{8,7},{9,8},{10,9},{11,1... | collective-permute-start | bytes 245768 | tf_op jit(solution)/shard_map/ppermute | solution.py:487
  12.4 7.0 %copy-start.4 = (s32[128,1]{0,1:T(1,128)S(1)}, s32[128,1]{0,1:T(1,128)}, u32[]{:S(2)}) copy-start(s32[128,1]{0,1:T(1,128)} %param.7) | copy-start | bytes 1540
  12.4 7.0 %copy-start.3 = (s32[128,3]{0,1:T(4,128)S(1)}, s32[128,3]{0,1:T(4,128)}, u32[]{:S(2)}) copy-start(s32[128,3]{0,1:T(4,128)} %param.8) | copy-start | bytes 4612
  12.4 11.3 %collective-permute-start.2 = (f32[132,8,128]{2,1,0:T(8,128)S(1)}, f32[132,8,128]{2,1,0:T(8,128)S(1)}, u32[]{:S(2)}, u32[]{:S(2)}) collective-permute-start(f32[132,8,128]{2,1,0:T(8,128)S(1)} %get-tuple-element.21), channel_id=1, source_target_pairs={{0,16},{16,32},{32,48},{1,17},{17,33},{33,49},{2,18},{18,34},{34,5... | collective-permute-start | bytes 1622024 | tf_op jit(solution)/shard_map/ppermute | solution.py:487
  17.5 11.0 %collective-permute-start.3 = (f32[132,8,128]{2,1,0:T(8,128)S(1)}, f32[132,8,128]{2,1,0:T(8,128)S(1)}, u32[]{:S(2)}, u32[]{:S(2)}) collective-permute-start(f32[132,8,128]{2,1,0:T(8,128)S(1)} %get-tuple-element.22), channel_id=1, source_target_pairs={{16,0},{32,16},{48,32},{17,1},{33,17},{49,33},{18,2},{34,18},{50,3... | collective-permute-start | bytes 1622024 | tf_op jit(solution)/shard_map/ppermute | solution.py:487
  19.5 0.7 copy-start.2
  28.6 35.8 %collective-permute-start.4 = (f32[242,8,128]{2,1,0:T(8,128)S(1)}, f32[242,8,128]{2,1,0:T(8,128)S(1)}, u32[]{:S(2)}, u32[]{:S(2)}) collective-permute-start(f32[242,8,128]{2,1,0:T(8,128)S(1)} %get-tuple-element.26), channel_id=1, source_target_pairs={{0,64},{64,128},{128,192},{192,256},{256,320},{320,384},{384,448},... | collective-permute-start | bytes 2973704 | tf_op jit(solution)/shard_map/ppermute | solution.py:487
  32.7 31.6 %collective-permute-start.5 = (f32[242,8,128]{2,1,0:T(8,128)S(1)}, f32[242,8,128]{2,1,0:T(8,128)S(1)}, u32[]{:S(2)}, u32[]{:S(2)}) collective-permute-start(f32[242,8,128]{2,1,0:T(8,128)S(1)} %get-tuple-element.27), channel_id=1, source_target_pairs={{64,0},{128,64},{192,128},{256,192},{320,256},{384,320},{448,384},... | collective-permute-start | bytes 2973704 | tf_op jit(solution)/shard_map/ppermute | solution.py:487

commit v6 on v5

--- a/solution.py
+++ b/solution.py
@@ -125,10 +125,10 @@
             out[PAIRS + ZGROUPS + g] = zhi_ref[g, rows]
 
 
-def z_ends(lo, hi, s, lane, t, total):
+def z_ends(lo, hi, s, lane, t):
     first = lane < GZ * (s + 1) if s < 11 else (lane >= GZ * s) & (lane < GZ * (s + 1))
     moved = roll(jnp.where(first, lo, hi), 32 * t - GZ * s, 1)
-    return jnp.where((lane >= 32 * t) & (lane < 32 * t + 2 * GZ), moved, total)
+    return jnp.where((lane >= 32 * t) & (lane < 32 * t + 2 * GZ), moved, 0.0)
 
 
 def pack_x(f_ref, inv_ref, zlo_ref, zhi_ref, ylo_ref, yhi_ref, lo_ref, hi_ref):
@@ -202,11 +202,13 @@
         put(c, x, t, factors[c // 3] * rate)
 
 
-def store_packed(ref, c, x, value):
-    ref[c, x, pl.ds(8, 8)] = value
-    if c in (0, 2, 3, 5):
-        ref[c, x, pl.ds(0, 8)] = roll(value, 32, 1)
-        ref[c, x, pl.ds(16, 8)] = roll(value, -32, 1)
+def store_packed(entries):
+    for ref, c, x, value in entries:
+        ref[c, x, pl.ds(8, 8)] = value
+    for shift, start in ((32, 0), (-32, 16)):
+        for ref, c, x, value in entries:
+            if c in (0, 2, 3, 5):
+                ref[c, x, pl.ds(start, 8)] = roll(value, shift, 1)
 
 
 def packed_z(lane, t):
@@ -227,11 +229,11 @@
 
 
 def split_dot(a, b):
-    ah, am, al = three_parts(a)
-    bh, bm, bl = three_parts(b)
+    ah, am, _ = three_parts(a)
+    bh, bm, _ = three_parts(b)
     return jnp.dot(
-        jnp.concatenate([al, ah, am, am, ah, ah], axis=1),
-        jnp.concatenate([bh, bl, bm, bh, bm, bh], axis=0),
+        jnp.concatenate([am, ah, ah], axis=1),
+        jnp.concatenate([bh, bm, bh], axis=0),
         preferred_element_type=F32,
     )
 
@@ -249,21 +251,20 @@
     lane = lanes((8, CZ))
     row = rows_of((8, CZ))
     zero = jnp.zeros((8, CZ), F32)
+    moves = []
     for p in range(PAIRS):
         c, x = divmod(p, CX)
         g, s = z_slot(c, x)
-        total = zero
         for t in (0, 1, 2, 3):
             if t in (1, 2):
                 own = pl.ds(8 * (t - 1), 8)
                 full[c, GX + x, band_of(t)] = f_ref[c, x, own] if c < 6 else own_inv_ref[x, own]
-                lo, hi = zlo_ref[g, own], zhi_ref[g, own]
+                ends = (zlo_ref, (g, own)), (zhi_ref, (g, own))
             else:
                 ref = ylo_ref if t == 0 else yhi_ref
                 full[c, GX + x, band_of(t)] = ref[p]
-                lo, hi = ref[PAIRS + g], ref[PAIRS + ZGROUPS + g]
-            total = z_ends(lo, hi, s, lane, t, total)
-        store_packed(full_p, c, GX + x, total)
+                ends = (ref, PAIRS + g), (ref, PAIRS + ZGROUPS + g)
+            moves.append((c, GX + x, t, s, ends, 0))
     for side in (0, 1):
         ref = xhi_ref if side == 0 else xlo_ref
         where_main = {key: n for n, key in enumerate(XMAIN)}
@@ -275,7 +276,6 @@
                 g, s = z_slot(c, k - 1 if side == 0 else CX - k)
                 q = 5 if c == 6 else (k - 1) // 2
                 mains = [zero, zero, zero, zero]
-                total = zero
                 for t in (0, 1, 2, 3, 4):
                     if (k, c, t) in where_main:
                         value = ref[where_main[k, c, t]]
@@ -284,35 +284,51 @@
                         else:
                             mains[t] = value
                     if (q, t, 0) in XEND:
-                        lo, hi = ref[XEND[q, t, 0]], ref[XEND[q, t, 1]]
-                        if t == 4:
-                            top = z_ends(lo, hi, s, lane, 0, zero)
-                            bottom = z_ends(lo, hi, s, lane, 3, zero)
-                            total = total + jnp.where(row >= 4, top, bottom)
-                        else:
-                            total = z_ends(lo, hi, s, lane, t, total)
+                        ends = (ref, XEND[q, t, 0]), (ref, XEND[q, t, 1])
+                        for u, part in ((0, 1), (3, 2)) if t == 4 else ((t, 0),):
+                            moves.append((c, x, u, s, ends, part))
                 for t in range(4):
                     full[c, x, band_of(t)] = mains[t]
-                store_packed(full_p, c, x, total)
+    moves.sort(key=lambda m: ((32 * m[2] - GZ * m[3]) % 128, m[0], m[1]))
+    begun = []
+    for c, x, t, s, (low_end, high_end), part in moves:
+        value = z_ends(low_end[0][low_end[1]], high_end[0][high_end[1]], s, lane, t)
+        if part:
+            value = jnp.where((row >= 4) if part == 1 else (row < 4), value, 0.0)
+        if (c, x) in begun:
+            value = value + full_p[c, x, pl.ds(8, 8)]
+        else:
+            begun.append((c, x))
+        full_p[c, x, pl.ds(8, 8)] = value
+    for shift, start in ((32, 0), (-32, 16)):
+        for c, x in begun:
+            if c in (0, 2, 3, 5):
+                full_p[c, x, pl.ds(start, 8)] = roll(full_p[c, x, pl.ds(8, 8)], shift, 1)
 
     for power, source, packed, target, target_p in (
         (1, full, full_p, t1, p1), (2, t1, p1, t2, p2), (3, t2, p2, t3, p3)
     ):
         scale, skip = STEP / power / 12.0, 2 * power - 2
 
-        def put(c, x, t, value, target=target, target_p=target_p, power=power):
+        waiting = []
+
+        def put(c, x, t, value, target=target, target_p=target_p, power=power, waiting=waiting):
             if t == 4:
-                store_packed(target_p, c, x - 2 * power, value)
+                waiting.append((target_p, c, x - 2 * power, value))
             else:
                 target[c, x - 2 * power, band_of(t)] = value
 
-        def body(i, carry, source=source, packed=packed, scale=scale, skip=skip, put=put, power=power):
+        def body(i, carry, source=source, packed=packed, scale=scale, skip=skip, put=put, power=power, waiting=waiting):
             xs = [2 * power + 2 + ROWS * i + j for j in range(ROWS)]
             taylor(source, packed, full, full_p, band, xs, (0, 1, 2, 3), scale, put, skip=skip)
+            store_packed(waiting)
+            waiting.clear()
             return carry
 
         ends = [2 * power, 2 * power + 1, XW - 2 * power - 2, XW - 2 * power - 1]
         taylor(source, packed, full, full_p, band, ends, (1, 2), scale, put, (1, 2, 4, 5), skip)
+        store_packed(waiting)
+        waiting.clear()
         lax.fori_loop(0, (XW - 4 * power - 4) // ROWS, body, 0)
 
     def finish(c, x, t, value):

time: 109 us -> 101 us (0.927)
  Pallas kernels: 26.9 us -> 18.6 us
    pallas_call x6, Pallas kernels: 26.9 us -> 18.6 us  [call(): pl.pallas_call(body, out_shape=[jax.ShapeDtypeStruct(s, jnp.bfloat16 if s...]
where the time goes in v6:
time: 101 us
  blocking collectives  50.3 us (50%)
  Pallas kernels  18.6 us (18%)
  starting transfers between devices  17.8 us (18%)
  waiting for transfers between devices  11 us (11%)
  local copies, waits for them, and re-layouts  2.05 us (2%)
    all_to_all x1, blocking collectives, local(): req = lax.all_to_all(send, ('gy', 'gz'), 0, 0, tiled=True)  29.6 us
    all_to_all x1, blocking collectives, local(): answers = lax.all_to_all(answers, ('gy', 'gz'), 0, 0, tiled=True)  20.7 us
    pallas_call x6, Pallas kernels, call(): pl.pallas_call(body, out_shape=[jax.ShapeDtypeStruct(s, jnp.bfloat16 if s...  18.6 us
    ppermute x3, starting transfers between devices, shift_both(): lax.ppermute(high_edge, axis, up)  12.7 us
    ppermute x3, waiting for transfers between devices, shift_both(): lax.ppermute(low_edge, axis, down)  8.6 us
    ppermute x3, starting transfers between devices, shift_both(): lax.ppermute(low_edge, axis, down)  5.13 us
    ppermute x3, waiting for transfers between devices, shift_both(): lax.ppermute(high_edge, axis, up)  2.43 us
  transfers between devices with their start and end apart: 6, of which 4 were waited for; matrix products, arithmetic and copies ran while one was open for 1% of the time, Pallas kernels for 1%

profile of v6, /device:TPU:7, one launch (start us, length us, event | category | flops | bytes accessed | tf_op | source)
XLA Modules:
  0.0 100.7 jit_solution(13948164176296793732)
XLA Ops:
  0.6 0.0 copy-start
  0.6 0.0 copy-start.1
  0.6 1.0 copy-done.1
  1.6 1.8 %shard_map.68 = (f32[10,16,128]{2,1,0:T(8,128)S(1)}, f32[10,16,128]{2,1,0:T(8,128)S(1)}, f32[16,16,128]{2,1,0:T(8,128)S(1)}) custom-call(f32[6,16,16,128]{3,2,1,0:T(8,128)} %f_ref.5, f32[16,16,128]{2,1,0:T(8,128)S(1)} %copy-done.1), custom_call_target="tpu_custom_call" | custom-call | flops 1000000 | bytes 1000000 | tf_op jit(solution)/shard_map/pallas_call | solution.py:74
  3.4 3.5 %collective-permute-start = (f32[10,16,128]{2,1,0:T(8,128)S(1)}, f32[10,16,128]{2,1,0:T(8,128)S(1)}, u32[]{:S(2)}, u32[]{:S(2)}) collective-permute-start(f32[10,16,128]{2,1,0:T(8,128)S(1)} %get-tuple-element.19), channel_id=1, source_target_pairs={{0,1},{1,2},{2,3},{3,4},{4,5},{5,6},{6,7},{7,8},{8,9},{9,10},{10,1... | collective-permute-start | bytes 245768 | tf_op jit(solution)/shard_map/ppermute | solution.py:503
  7.0 1.3 %collective-permute-start.1 = (f32[10,16,128]{2,1,0:T(8,128)S(1)}, f32[10,16,128]{2,1,0:T(8,128)S(1)}, u32[]{:S(2)}, u32[]{:S(2)}) collective-permute-start(f32[10,16,128]{2,1,0:T(8,128)S(1)} %get-tuple-element.20), channel_id=1, source_target_pairs={{1,0},{2,1},{3,2},{4,3},{5,4},{6,5},{7,6},{8,7},{9,8},{10,9},{11,1... | collective-permute-start | bytes 245768 | tf_op jit(solution)/shard_map/ppermute | solution.py:503
  8.3 0.2 collective-permute-done.zlo_ref
  8.4 3.9 %collective-permute-done.1.zhi_ref = f32[10,16,128]{2,1,0:T(8,128)S(1)} collective-permute-done((f32[10,16,128]{2,1,0:T(8,128)S(1)}, f32[10,16,128]{2,1,0:T(8,128)S(1)}, u32[]{:S(2)}, u32[]{:S(2)}) %collective-permute-start.1) | collective-permute-done | bytes 81952 | tf_op jit(solution)/shard_map/ppermute | solution.py:503
  12.3 0.0 copy-done
  12.3 0.1 shard_map.69
  12.4 0.0 copy-start.4
  12.4 0.0 copy-start.3
  12.4 5.0 %collective-permute-start.2 = (f32[132,8,128]{2,1,0:T(8,128)S(1)}, f32[132,8,128]{2,1,0:T(8,128)S(1)}, u32[]{:S(2)}, u32[]{:S(2)}) collective-permute-start(f32[132,8,128]{2,1,0:T(8,128)S(1)} %get-tuple-element.21), channel_id=1, source_target_pairs={{0,16},{16,32},{32,48},{1,17},{17,33},{33,49},{2,18},{18,34},{34,5... | collective-permute-start | bytes 1622024 | tf_op jit(solution)/shard_map/ppermute | solution.py:503
  17.5 1.9 %collective-permute-start.3 = (f32[132,8,128]{2,1,0:T(8,128)S(1)}, f32[132,8,128]{2,1,0:T(8,128)S(1)}, u32[]{:S(2)}, u32[]{:S(2)}) collective-permute-start(f32[132,8,128]{2,1,0:T(8,128)S(1)} %get-tuple-element.22), channel_id=1, source_target_pairs={{16,0},{32,16},{48,32},{17,1},{33,17},{49,33},{18,2},{34,18},{50,3... | collective-permute-start | bytes 1622024 | tf_op jit(solution)/shard_map/ppermute | solution.py:503
  19.4 0.0 copy-done.4
  19.4 0.0 copy-done.3
  19.4 0.1 copy.10
  19.5 0.0 copy-start.2
  19.5 0.1 copy.12
  19.7 0.6 copy-done.2
  20.2 0.1 copy.11
  20.4 0.1 pad.3.clone
  20.4 0.1 maximum_maximum_fusion.data_ref
  20.5 0.9 shard_map.70
  21.5 2.3 %collective-permute-done.2.ylo_ref = f32[132,8,128]{2,1,0:T(8,128)S(1)} collective-permute-done((f32[132,8,128]{2,1,0:T(8,128)S(1)}, f32[132,8,128]{2,1,0:T(8,128)S(1)}, u32[]{:S(2)}, u32[]{:S(2)}) %collective-permute-start.2) | collective-permute-done | bytes 540704 | tf_op jit(solution)/shard_map/ppermute | solution.py:503
  23.7 4.7 %collective-permute-done.3.yhi_ref = f32[132,8,128]{2,1,0:T(8,128)S(1)} collective-permute-done((f32[132,8,128]{2,1,0:T(8,128)S(1)}, f32[132,8,128]{2,1,0:T(8,128)S(1)}, u32[]{:S(2)}, u32[]{:S(2)}) %collective-permute-start.3) | collective-permute-done | bytes 540704 | tf_op jit(solution)/shard_map/ppermute | solution.py:503
  28.4 0.1 shard_map.71
  28.6 4.1 %collective-permute-start.4 = (f32[242,8,128]{2,1,0:T(8,128)S(1)}, f32[242,8,128]{2,1,0:T(8,128)S(1)}, u32[]{:S(2)}, u32[]{:S(2)}) collective-permute-start(f32[242,8,128]{2,1,0:T(8,128)S(1)} %get-tuple-element.26), channel_id=1, source_target_pairs={{0,64},{64,128},{128,192},{192,256},{256,320},{320,384},{384,448},... | collective-permute-start | bytes 2973704 | tf_op jit(solution)/shard_map/ppermute | solution.py:503
  32.7 1.9 %collective-permute-start.5 = (f32[242,8,128]{2,1,0:T(8,128)S(1)}, f32[242,8,128]{2,1,0:T(8,128)S(1)}, u32[]{:S(2)}, u32[]{:S(2)}) collective-permute-start(f32[242,8,128]{2,1,0:T(8,128)S(1)} %get-tuple-element.27), channel_id=1, source_target_pairs={{64,0},{128,64},{192,128},{256,192},{320,256},{384,320},{448,384},... | collective-permute-start | bytes 2973704 | tf_op jit(solution)/shard_map/ppermute | solution.py:503
  34.6 0.1 copy.13
  34.7 29.6 %all_to_all.22 = f32[64,1,256]{2,1,0:T(1,128)S(1)} all-to-all(f32[64,1,256]{2,1,0:T(1,128)S(1)} %copy.13), channel_id=1, replica_groups=mesh['gx'=8,'gy'=4,'gz'=16] {'gy','gz'}, dimensions={0} | all-to-all | bytes 131072 | tf_op jit(solution)/shard_map/all_to_all | solution.py:538
  64.4 0.0 collective-permute-done.4.xlo_ref
  64.4 0.0 collective-permute-done.5.xhi_ref
  64.4 14.7 %shard_map.72 = (f32[6,16,16,128]{3,2,1,0:T(8,128)}, f32[64,128]{1,0:T(8,128)S(1)}) custom-call(f32[6,16,16,128]{3,2,1,0:T(8,128)S(1)} %copy-done, f32[16,16,128]{2,1,0:T(8,128)S(1)} %get-tuple-element.18.inv_ref.own_inv_ref, f32[10,16,128]{2,1,0:T(8,128)S(1)} %collective-permute-done.zlo_ref, f32[10,16,128]{2,1,0:T(8,128)S(1)} %collective-permute-done.1.zhi_ref, ...), custom_call_target="tpu_custom_call" | custom-call | flops 100000000 | bytes 1000000 | tf_op jit(solution)/shard_map/pallas_call | solution.py:74
  79.1 20.7 %all_to_all.23 = f32[64,1,128]{2,1,0:T(1,128)S(1)} all-to-all(f32[64,1,128]{2,1,0:T(1,128)S(1)} %bitcast.11), channel_id=1, replica_groups=mesh['gx'=8,'gy'=4,'gz'=16] {'gy','gz'}, dimensions={0} | all-to-all | bytes 65536 | tf_op jit(solution)/shard_map/all_to_all | solution.py:562
  99.8 1.0 shard_map.73
  (4 shorter events, 0.0 us)
Async XLA Ops:
  0.6 11.7 %copy-start = (f32[6,16,16,128]{3,2,1,0:T(8,128)S(1)}, f32[6,16,16,128]{3,2,1,0:T(8,128)}, u32[]{:S(2)}) copy-start(f32[6,16,16,128]{3,2,1,0:T(8,128)} %f_ref.5) | copy-start | bytes 2359300
  0.6 1.0 copy-start.1
  3.4 5.0 %collective-permute-start = (f32[10,16,128]{2,1,0:T(8,128)S(1)}, f32[10,16,128]{2,1,0:T(8,128)S(1)}, u32[]{:S(2)}, u32[]{:S(2)}) collective-permute-start(f32[10,16,128]{2,1,0:T(8,128)S(1)} %get-tuple-element.19), channel_id=1, source_target_pairs={{0,1},{1,2},{2,3},{3,4},{4,5},{5,6},{6,7},{7,8},{8,9},{9,10},{10,1... | collective-permute-start | bytes 245768 | tf_op jit(solution)/shard_map/ppermute | solution.py:503
  7.0 5.4 %collective-permute-start.1 = (f32[10,16,128]{2,1,0:T(8,128)S(1)}, f32[10,16,128]{2,1,0:T(8,128)S(1)}, u32[]{:S(2)}, u32[]{:S(2)}) collective-permute-start(f32[10,16,128]{2,1,0:T(8,128)S(1)} %get-tuple-element.20), channel_id=1, source_target_pairs={{1,0},{2,1},{3,2},{4,3},{5,4},{6,5},{7,6},{8,7},{9,8},{10,9},{11,1... | collective-permute-start | bytes 245768 | tf_op jit(solution)/shard_map/ppermute | solution.py:503
  12.4 7.0 %copy-start.4 = (s32[128,1]{0,1:T(1,128)S(1)}, s32[128,1]{0,1:T(1,128)}, u32[]{:S(2)}) copy-start(s32[128,1]{0,1:T(1,128)} %param.7) | copy-start | bytes 1540
  12.4 7.0 %copy-start.3 = (s32[128,3]{0,1:T(4,128)S(1)}, s32[128,3]{0,1:T(4,128)}, u32[]{:S(2)}) copy-start(s32[128,3]{0,1:T(4,128)} %param.8) | copy-start | bytes 4612
  12.4 11.3 %collective-permute-start.2 = (f32[132,8,128]{2,1,0:T(8,128)S(1)}, f32[132,8,128]{2,1,0:T(8,128)S(1)}, u32[]{:S(2)}, u32[]{:S(2)}) collective-permute-start(f32[132,8,128]{2,1,0:T(8,128)S(1)} %get-tuple-element.21), channel_id=1, source_target_pairs={{0,16},{16,32},{32,48},{1,17},{17,33},{33,49},{2,18},{18,34},{34,5... | collective-permute-start | bytes 1622024 | tf_op jit(solution)/shard_map/ppermute | solution.py:503
  17.5 11.0 %collective-permute-start.3 = (f32[132,8,128]{2,1,0:T(8,128)S(1)}, f32[132,8,128]{2,1,0:T(8,128)S(1)}, u32[]{:S(2)}, u32[]{:S(2)}) collective-permute-start(f32[132,8,128]{2,1,0:T(8,128)S(1)} %get-tuple-element.22), channel_id=1, source_target_pairs={{16,0},{32,16},{48,32},{17,1},{33,17},{49,33},{18,2},{34,18},{50,3... | collective-permute-start | bytes 1622024 | tf_op jit(solution)/shard_map/ppermute | solution.py:503
  19.5 0.7 copy-start.2
  28.6 35.8 %collective-permute-start.4 = (f32[242,8,128]{2,1,0:T(8,128)S(1)}, f32[242,8,128]{2,1,0:T(8,128)S(1)}, u32[]{:S(2)}, u32[]{:S(2)}) collective-permute-start(f32[242,8,128]{2,1,0:T(8,128)S(1)} %get-tuple-element.26), channel_id=1, source_target_pairs={{0,64},{64,128},{128,192},{192,256},{256,320},{320,384},{384,448},... | collective-permute-start | bytes 2973704 | tf_op jit(solution)/shard_map/ppermute | solution.py:503
  32.7 31.6 %collective-permute-start.5 = (f32[242,8,128]{2,1,0:T(8,128)S(1)}, f32[242,8,128]{2,1,0:T(8,128)S(1)}, u32[]{:S(2)}, u32[]{:S(2)}) collective-permute-start(f32[242,8,128]{2,1,0:T(8,128)S(1)} %get-tuple-element.27), channel_id=1, source_target_pairs={{64,0},{128,64},{192,128},{256,192},{320,256},{384,320},{448,384},... | collective-permute-start | bytes 2973704 | tf_op jit(solution)/shard_map/ppermute | solution.py:503

commit v7 on v6

--- a/solution.py
+++ b/solution.py
@@ -157,7 +157,7 @@
             out[n] = end_of(g, t, e)
 
 
-def taylor(source, packed, inv_main, inv_packed, band, xs, tiles, scale, put, comps=(0, 1, 2, 3, 4, 5), skip=0):
+def taylor(source, packed, inv_main, inv_packed, band, xs, tiles, scale, put, comps=(0, 1, 2, 3, 4, 5), skip=0, flush=None):
     fields = [c for c in (4, 3, 1, 0) if {4: 0, 3: 1, 1: 3, 0: 4}[c] in comps]
     keys = [(i, c) for i in range(len(xs)) for c in fields]
     ghosts = three_parts(jnp.concatenate([packed[c, xs[i] - skip, pl.ds(8, 8)] for i, c in keys], axis=0))
@@ -171,8 +171,12 @@
             part = total[8 * n:8 * n + 8, 128:256]
             along_z[key + (4,)] = along_z[key + (4,)] + part if key + (4,) in along_z else part
     for i, x in enumerate(xs):
-        for t in tuple(tiles) + (4,):
-            one_tile(packed if t == 4 else source, inv_packed if t == 4 else inv_main, along_z, i, x, t, scale, put, comps, skip)
+        one_tile(packed, inv_packed, along_z, i, x, 4, scale, put, comps, skip)
+    if flush:
+        flush()
+    for i, x in enumerate(xs):
+        for t in tiles:
+            one_tile(source, inv_main, along_z, i, x, t, scale, put, comps, skip)
 
 
 def one_tile(source, inv_ref, along_z, i, x, t, scale, put, comps, skip):
@@ -312,23 +316,23 @@
 
         waiting = []
 
+        def flush(waiting=waiting):
+            store_packed(waiting)
+            waiting.clear()
+
         def put(c, x, t, value, target=target, target_p=target_p, power=power, waiting=waiting):
             if t == 4:
                 waiting.append((target_p, c, x - 2 * power, value))
             else:
                 target[c, x - 2 * power, band_of(t)] = value
 
-        def body(i, carry, source=source, packed=packed, scale=scale, skip=skip, put=put, power=power, waiting=waiting):
+        def body(i, carry, source=source, packed=packed, scale=scale, skip=skip, put=put, power=power, flush=flush):
             xs = [2 * power + 2 + ROWS * i + j for j in range(ROWS)]
-            taylor(source, packed, full, full_p, band, xs, (0, 1, 2, 3), scale, put, skip=skip)
-            store_packed(waiting)
-            waiting.clear()
+            taylor(source, packed, full, full_p, band, xs, (0, 1, 2, 3), scale, put, skip=skip, flush=flush)
             return carry
 
         ends = [2 * power, 2 * power + 1, XW - 2 * power - 2, XW - 2 * power - 1]
-        taylor(source, packed, full, full_p, band, ends, (1, 2), scale, put, (1, 2, 4, 5), skip)
-        store_packed(waiting)
-        waiting.clear()
+        taylor(source, packed, full, full_p, band, ends, (1, 2), scale, put, (1, 2, 4, 5), skip, flush)
         lax.fori_loop(0, (XW - 4 * power - 4) // ROWS, body, 0)
 
     def finish(c, x, t, value):

time: 101 us -> 101 us (level)
  no operation moved by 1% of the time
where the time goes in v7:
time: 101 us
  blocking collectives  50.3 us (50%)
  Pallas kernels  18.6 us (18%)
  starting transfers between devices  17.8 us (18%)
  waiting for transfers between devices  11 us (11%)
  local copies, waits for them, and re-layouts  2.05 us (2%)
    all_to_all x1, blocking collectives, local(): req = lax.all_to_all(send, ('gy', 'gz'), 0, 0, tiled=True)  29.6 us
    all_to_all x1, blocking collectives, local(): answers = lax.all_to_all(answers, ('gy', 'gz'), 0, 0, tiled=True)  20.7 us
    pallas_call x6, Pallas kernels, call(): pl.pallas_call(body, out_shape=[jax.ShapeDtypeStruct(s, jnp.bfloat16 if s...  18.6 us
    ppermute x3, starting transfers between devices, shift_both(): lax.ppermute(high_edge, axis, up)  12.7 us
    ppermute x3, waiting for transfers between devices, shift_both(): lax.ppermute(low_edge, axis, down)  8.6 us
    ppermute x3, starting transfers between devices, shift_both(): lax.ppermute(low_edge, axis, down)  5.13 us
    ppermute x3, waiting for transfers between devices, shift_both(): lax.ppermute(high_edge, axis, up)  2.43 us
  transfers between devices with their start and end apart: 6, of which 4 were waited for; matrix products, arithmetic and copies ran while one was open for 1% of the time, Pallas kernels for 1%

profile of v7, /device:TPU:7, one launch (start us, length us, event | category | flops | bytes accessed | tf_op | source)
XLA Modules:
  0.0 100.7 jit_solution(8402127019902088364)
XLA Ops:
  0.6 0.0 copy-start
  0.6 0.0 copy-start.1
  0.6 1.0 copy-done.1
  1.6 1.8 %shard_map.68 = (f32[10,16,128]{2,1,0:T(8,128)S(1)}, f32[10,16,128]{2,1,0:T(8,128)S(1)}, f32[16,16,128]{2,1,0:T(8,128)S(1)}) custom-call(f32[6,16,16,128]{3,2,1,0:T(8,128)} %f_ref.5, f32[16,16,128]{2,1,0:T(8,128)S(1)} %copy-done.1), custom_call_target="tpu_custom_call" | custom-call | flops 1000000 | bytes 1000000 | tf_op jit(solution)/shard_map/pallas_call | solution.py:74
  3.4 3.5 %collective-permute-start = (f32[10,16,128]{2,1,0:T(8,128)S(1)}, f32[10,16,128]{2,1,0:T(8,128)S(1)}, u32[]{:S(2)}, u32[]{:S(2)}) collective-permute-start(f32[10,16,128]{2,1,0:T(8,128)S(1)} %get-tuple-element.19), channel_id=1, source_target_pairs={{0,1},{1,2},{2,3},{3,4},{4,5},{5,6},{6,7},{7,8},{8,9},{9,10},{10,1... | collective-permute-start | bytes 245768 | tf_op jit(solution)/shard_map/ppermute | solution.py:507
  7.0 1.3 %collective-permute-start.1 = (f32[10,16,128]{2,1,0:T(8,128)S(1)}, f32[10,16,128]{2,1,0:T(8,128)S(1)}, u32[]{:S(2)}, u32[]{:S(2)}) collective-permute-start(f32[10,16,128]{2,1,0:T(8,128)S(1)} %get-tuple-element.20), channel_id=1, source_target_pairs={{1,0},{2,1},{3,2},{4,3},{5,4},{6,5},{7,6},{8,7},{9,8},{10,9},{11,1... | collective-permute-start | bytes 245768 | tf_op jit(solution)/shard_map/ppermute | solution.py:507
  8.3 0.2 collective-permute-done.zlo_ref
  8.4 3.9 %collective-permute-done.1.zhi_ref = f32[10,16,128]{2,1,0:T(8,128)S(1)} collective-permute-done((f32[10,16,128]{2,1,0:T(8,128)S(1)}, f32[10,16,128]{2,1,0:T(8,128)S(1)}, u32[]{:S(2)}, u32[]{:S(2)}) %collective-permute-start.1) | collective-permute-done | bytes 81952 | tf_op jit(solution)/shard_map/ppermute | solution.py:507
  12.3 0.0 copy-done
  12.3 0.1 shard_map.69
  12.4 0.0 copy-start.4
  12.4 0.0 copy-start.3
  12.4 5.0 %collective-permute-start.2 = (f32[132,8,128]{2,1,0:T(8,128)S(1)}, f32[132,8,128]{2,1,0:T(8,128)S(1)}, u32[]{:S(2)}, u32[]{:S(2)}) collective-permute-start(f32[132,8,128]{2,1,0:T(8,128)S(1)} %get-tuple-element.21), channel_id=1, source_target_pairs={{0,16},{16,32},{32,48},{1,17},{17,33},{33,49},{2,18},{18,34},{34,5... | collective-permute-start | bytes 1622024 | tf_op jit(solution)/shard_map/ppermute | solution.py:507
  17.5 1.9 %collective-permute-start.3 = (f32[132,8,128]{2,1,0:T(8,128)S(1)}, f32[132,8,128]{2,1,0:T(8,128)S(1)}, u32[]{:S(2)}, u32[]{:S(2)}) collective-permute-start(f32[132,8,128]{2,1,0:T(8,128)S(1)} %get-tuple-element.22), channel_id=1, source_target_pairs={{16,0},{32,16},{48,32},{17,1},{33,17},{49,33},{18,2},{34,18},{50,3... | collective-permute-start | bytes 1622024 | tf_op jit(solution)/shard_map/ppermute | solution.py:507
  19.4 0.0 copy-done.4
  19.4 0.0 copy-done.3
  19.4 0.1 copy.10
  19.5 0.0 copy-start.2
  19.5 0.1 copy.12
  19.7 0.6 copy-done.2
  20.2 0.1 copy.11
  20.4 0.1 pad.3.clone
  20.4 0.1 maximum_maximum_fusion.data_ref
  20.5 0.9 shard_map.70
  21.5 2.3 %collective-permute-done.2.ylo_ref = f32[132,8,128]{2,1,0:T(8,128)S(1)} collective-permute-done((f32[132,8,128]{2,1,0:T(8,128)S(1)}, f32[132,8,128]{2,1,0:T(8,128)S(1)}, u32[]{:S(2)}, u32[]{:S(2)}) %collective-permute-start.2) | collective-permute-done | bytes 540704 | tf_op jit(solution)/shard_map/ppermute | solution.py:507
  23.7 4.7 %collective-permute-done.3.yhi_ref = f32[132,8,128]{2,1,0:T(8,128)S(1)} collective-permute-done((f32[132,8,128]{2,1,0:T(8,128)S(1)}, f32[132,8,128]{2,1,0:T(8,128)S(1)}, u32[]{:S(2)}, u32[]{:S(2)}) %collective-permute-start.3) | collective-permute-done | bytes 540704 | tf_op jit(solution)/shard_map/ppermute | solution.py:507
  28.4 0.1 shard_map.71
  28.6 4.1 %collective-permute-start.4 = (f32[242,8,128]{2,1,0:T(8,128)S(1)}, f32[242,8,128]{2,1,0:T(8,128)S(1)}, u32[]{:S(2)}, u32[]{:S(2)}) collective-permute-start(f32[242,8,128]{2,1,0:T(8,128)S(1)} %get-tuple-element.26), channel_id=1, source_target_pairs={{0,64},{64,128},{128,192},{192,256},{256,320},{320,384},{384,448},... | collective-permute-start | bytes 2973704 | tf_op jit(solution)/shard_map/ppermute | solution.py:507
  32.7 1.9 %collective-permute-start.5 = (f32[242,8,128]{2,1,0:T(8,128)S(1)}, f32[242,8,128]{2,1,0:T(8,128)S(1)}, u32[]{:S(2)}, u32[]{:S(2)}) collective-permute-start(f32[242,8,128]{2,1,0:T(8,128)S(1)} %get-tuple-element.27), channel_id=1, source_target_pairs={{64,0},{128,64},{192,128},{256,192},{320,256},{384,320},{448,384},... | collective-permute-start | bytes 2973704 | tf_op jit(solution)/shard_map/ppermute | solution.py:507
  34.6 0.1 copy.13
  34.7 29.6 %all_to_all.22 = f32[64,1,256]{2,1,0:T(1,128)S(1)} all-to-all(f32[64,1,256]{2,1,0:T(1,128)S(1)} %copy.13), channel_id=1, replica_groups=mesh['gx'=8,'gy'=4,'gz'=16] {'gy','gz'}, dimensions={0} | all-to-all | bytes 131072 | tf_op jit(solution)/shard_map/all_to_all | solution.py:542
  64.4 0.0 collective-permute-done.4.xlo_ref
  64.4 0.0 collective-permute-done.5.xhi_ref
  64.4 14.7 %shard_map.72 = (f32[6,16,16,128]{3,2,1,0:T(8,128)}, f32[64,128]{1,0:T(8,128)S(1)}) custom-call(f32[6,16,16,128]{3,2,1,0:T(8,128)S(1)} %copy-done, f32[16,16,128]{2,1,0:T(8,128)S(1)} %get-tuple-element.18.inv_ref.own_inv_ref, f32[10,16,128]{2,1,0:T(8,128)S(1)} %collective-permute-done.zlo_ref, f32[10,16,128]{2,1,0:T(8,128)S(1)} %collective-permute-done.1.zhi_ref, ...), custom_call_target="tpu_custom_call" | custom-call | flops 100000000 | bytes 1000000 | tf_op jit(solution)/shard_map/pallas_call | solution.py:74
  79.1 20.7 %all_to_all.23 = f32[64,1,128]{2,1,0:T(1,128)S(1)} all-to-all(f32[64,1,128]{2,1,0:T(1,128)S(1)} %bitcast.11), channel_id=1, replica_groups=mesh['gx'=8,'gy'=4,'gz'=16] {'gy','gz'}, dimensions={0} | all-to-all | bytes 65536 | tf_op jit(solution)/shard_map/all_to_all | solution.py:566
  99.7 1.0 shard_map.73
  (4 shorter events, 0.0 us)
Async XLA Ops:
  0.6 11.7 %copy-start = (f32[6,16,16,128]{3,2,1,0:T(8,128)S(1)}, f32[6,16,16,128]{3,2,1,0:T(8,128)}, u32[]{:S(2)}) copy-start(f32[6,16,16,128]{3,2,1,0:T(8,128)} %f_ref.5) | copy-start | bytes 2359300
  0.6 1.0 copy-start.1
  3.4 5.0 %collective-permute-start = (f32[10,16,128]{2,1,0:T(8,128)S(1)}, f32[10,16,128]{2,1,0:T(8,128)S(1)}, u32[]{:S(2)}, u32[]{:S(2)}) collective-permute-start(f32[10,16,128]{2,1,0:T(8,128)S(1)} %get-tuple-element.19), channel_id=1, source_target_pairs={{0,1},{1,2},{2,3},{3,4},{4,5},{5,6},{6,7},{7,8},{8,9},{9,10},{10,1... | collective-permute-start | bytes 245768 | tf_op jit(solution)/shard_map/ppermute | solution.py:507
  7.0 5.4 %collective-permute-start.1 = (f32[10,16,128]{2,1,0:T(8,128)S(1)}, f32[10,16,128]{2,1,0:T(8,128)S(1)}, u32[]{:S(2)}, u32[]{:S(2)}) collective-permute-start(f32[10,16,128]{2,1,0:T(8,128)S(1)} %get-tuple-element.20), channel_id=1, source_target_pairs={{1,0},{2,1},{3,2},{4,3},{5,4},{6,5},{7,6},{8,7},{9,8},{10,9},{11,1... | collective-permute-start | bytes 245768 | tf_op jit(solution)/shard_map/ppermute | solution.py:507
  12.4 7.0 %copy-start.4 = (s32[128,1]{0,1:T(1,128)S(1)}, s32[128,1]{0,1:T(1,128)}, u32[]{:S(2)}) copy-start(s32[128,1]{0,1:T(1,128)} %param.7) | copy-start | bytes 1540
  12.4 7.0 %copy-start.3 = (s32[128,3]{0,1:T(4,128)S(1)}, s32[128,3]{0,1:T(4,128)}, u32[]{:S(2)}) copy-start(s32[128,3]{0,1:T(4,128)} %param.8) | copy-start | bytes 4612
  12.4 11.3 %collective-permute-start.2 = (f32[132,8,128]{2,1,0:T(8,128)S(1)}, f32[132,8,128]{2,1,0:T(8,128)S(1)}, u32[]{:S(2)}, u32[]{:S(2)}) collective-permute-start(f32[132,8,128]{2,1,0:T(8,128)S(1)} %get-tuple-element.21), channel_id=1, source_target_pairs={{0,16},{16,32},{32,48},{1,17},{17,33},{33,49},{2,18},{18,34},{34,5... | collective-permute-start | bytes 1622024 | tf_op jit(solution)/shard_map/ppermute | solution.py:507
  17.5 11.0 %collective-permute-start.3 = (f32[132,8,128]{2,1,0:T(8,128)S(1)}, f32[132,8,128]{2,1,0:T(8,128)S(1)}, u32[]{:S(2)}, u32[]{:S(2)}) collective-permute-start(f32[132,8,128]{2,1,0:T(8,128)S(1)} %get-tuple-element.22), channel_id=1, source_target_pairs={{16,0},{32,16},{48,32},{17,1},{33,17},{49,33},{18,2},{34,18},{50,3... | collective-permute-start | bytes 1622024 | tf_op jit(solution)/shard_map/ppermute | solution.py:507
  19.5 0.7 copy-start.2
  28.6 35.8 %collective-permute-start.4 = (f32[242,8,128]{2,1,0:T(8,128)S(1)}, f32[242,8,128]{2,1,0:T(8,128)S(1)}, u32[]{:S(2)}, u32[]{:S(2)}) collective-permute-start(f32[242,8,128]{2,1,0:T(8,128)S(1)} %get-tuple-element.26), channel_id=1, source_target_pairs={{0,64},{64,128},{128,192},{192,256},{256,320},{320,384},{384,448},... | collective-permute-start | bytes 2973704 | tf_op jit(solution)/shard_map/ppermute | solution.py:507
  32.7 31.6 %collective-permute-start.5 = (f32[242,8,128]{2,1,0:T(8,128)S(1)}, f32[242,8,128]{2,1,0:T(8,128)S(1)}, u32[]{:S(2)}, u32[]{:S(2)}) collective-permute-start(f32[242,8,128]{2,1,0:T(8,128)S(1)} %get-tuple-element.27), channel_id=1, source_target_pairs={{64,0},{128,64},{192,128},{256,192},{320,256},{384,320},{448,384},... | collective-permute-start | bytes 2973704 | tf_op jit(solution)/shard_map/ppermute | solution.py:507
